TPU v7x, 32 devices: a whole 2x2x4 slice. The times are simulated.
32 devices in a mesh: groups: 2 (over y), seq: 4 (over z), head: 2 (over x), sub: 2 (over core).
Axes of the slice: x: 2, y: 2, z: 4, core: 2. Of those that a mesh axis runs over, the one named last changes fastest.
Arguments:
- queries: bfloat16 [32, 64, 8192], P(('groups', 'seq'), None, 'head'), parts along dimension 0, may hold values from -6 to 6
- new_kv: bfloat16 [32, 64, 2, 1024], P(('groups', 'seq'), None, None, 'head'), parts along dimension 0, may hold values from -6 to 6
- kv_pages: bfloat16 [336, 2, 128, 1024], P(('groups', 'seq', 'sub'), None, None, 'head'), parts along dimension 0, may hold values from -6 to 6
- page_table: int32 [32, 16], P('groups'), parts along dimension 0, may hold values from -1 to 167, as said below
- cached_len: int32 [32], P('groups'), parts along dimension 0, may hold values from 1 to 2048, as said below
- is_prefill: int32 [32], P('groups'), parts along dimension 0, may hold values from 0 to 1, as said below
Outputs:
- attended: bfloat16 [32, 64, 8192], P(('groups', 'seq'), None, 'head'), parts along dimension 0
There are 2 independent parts, one for each index of `groups`. A program takes and returns all parts, laid end to end along the dimension named above; each array names one. Nothing has to cross between parts.
Inputs may be any that keep to these rules, and one draw needn't show every extreme that they name: `page_table`: entry [s, p] is the page number of page p of sequence s for p < ceil(cached_len[s] / 128) and -1 after; page number q lies on owner q // 21 (owner index = seq index * 2 + sub index) in its slot q % 21. Listing the pages of all sequences in order of sequence and page as t = 0, 1, ..., page t has owner (t + c) % 8 and slot (t + c) // 8 for one drawn c. No owner holds more than 8 page of the 4 sequences of one seq shard, and some owner holds exactly 8. `cached_len`: A decode sequence has 1 to 4 cache pages, a prefill sequence 8 to 16; all 4 sequences of one drawn seq shard are prefill sequences with 16 pages. `is_prefill`: exactly 8 sequences are prefill sequences.
All inputs are finite; a program needn't handle non-finite values.
Results may differ from a plain program's by a relative error of at most 0.014.
Values may be sent and summed in bfloat16 or wider, within the bound.
No kernel may reach another device: no remote copies, remote signals or barrier semaphores. Data moves between devices by JAX's collectives and lax.ppermute only.
A program may use at most 64 MiB of HBM per device.

v0:
```python
import jax
import jax.numpy as jnp
from jax import lax
from jax.experimental import pallas as pl
from jax.experimental.pallas import tpu as pltpu
from jax.sharding import PartitionSpec as P

HD = 128
PAGE = 128


NEG_FILL = -1e30


def partial_softmax(
    query_heads, cache_keys, cache_values, cache_valid, fresh_keys, fresh_values, fresh_valid
):
    score_scale = HD ** (-0.5)
    cache_scores = (
        jnp.einsum("rkgd,nkd->kgrn", query_heads, cache_keys, preferred_element_type=jnp.float32)
        * score_scale
    )
    fresh_scores = (
        jnp.einsum("rkgd,jkd->kgrj", query_heads, fresh_keys, preferred_element_type=jnp.float32)
        * score_scale
    )
    cache_mask = cache_valid[None, None, None, :]
    fresh_mask = fresh_valid[None, None, :, :]
    peak = jnp.maximum(
        jnp.max(jnp.where(cache_mask, cache_scores, NEG_FILL), axis=-1),
        jnp.max(jnp.where(fresh_mask, fresh_scores, NEG_FILL), axis=-1),
    )
    cache_weights = jnp.where(cache_mask, jnp.exp(cache_scores - peak[..., None]), 0.0)
    fresh_weights = jnp.where(fresh_mask, jnp.exp(fresh_scores - peak[..., None]), 0.0)
    weight_sum = jnp.sum(cache_weights, axis=-1) + jnp.sum(fresh_weights, axis=-1)
    numerator = jnp.einsum(
        "kgrn,nkd->kgrd",
        cache_weights.astype(jnp.bfloat16),
        cache_values,
        preferred_element_type=jnp.float32,
    )
    numerator = numerator + jnp.einsum(
        "kgrj,jkd->kgrd",
        fresh_weights.astype(jnp.bfloat16),
        fresh_values,
        preferred_element_type=jnp.float32,
    )
    return (peak, weight_sum, numerator)


def attend_all(
    query_block, fresh_block, received, fetch_index, page_here, lengths, live_rows, causal, fresh_on
):
    kv_width = received.shape[-1]
    heads_kv = kv_width // HD
    row_count = query_block.shape[1]
    group_size = query_block.shape[2] // kv_width
    page_count = fetch_index.shape[1]
    positions = jnp.arange(page_count * PAGE, dtype=jnp.int32)

    def one_sequence(inputs):
        query_rows, fresh_rows, index_row, here_row, length, live_row = inputs
        fetched = jnp.take(received, index_row, axis=0)
        cache_keys = fetched[:, 0].reshape(page_count * PAGE, heads_kv, HD)
        cache_values = fetched[:, 1].reshape(page_count * PAGE, heads_kv, HD)
        page_mask = jnp.broadcast_to(here_row[:, None], (page_count, PAGE)).reshape(
            page_count * PAGE
        )
        cache_valid = page_mask & (positions < length)
        query_heads = query_rows.reshape(row_count, heads_kv, group_size, HD)
        fresh_keys = fresh_rows[:, 0].reshape(row_count, heads_kv, HD)
        fresh_values = fresh_rows[:, 1].reshape(row_count, heads_kv, HD)
        fresh_valid = causal & live_row[:, None] & fresh_on
        return partial_softmax(
            query_heads,
            cache_keys,
            cache_values,
            cache_valid,
            fresh_keys,
            fresh_values,
            fresh_valid,
        )

    return lax.map(
        one_sequence, (query_block, fresh_block, fetch_index, page_here, lengths, live_rows)
    )


def finish(weight_sum, numerator, live_rows):
    unused_rows = 1.0 - live_rows.astype(jnp.float32)
    attended = numerator / (weight_sum + unused_rows[:, None, None, :])[..., None]
    attended = jnp.where(live_rows[:, None, None, :, None], attended, 0.0)
    seq_dev, heads_kv, group_size, row_count, head_dim = attended.shape
    return (
        jnp.transpose(attended, (0, 3, 1, 2, 4))
        .reshape(seq_dev, row_count, heads_kv * group_size * head_dim)
        .astype(jnp.bfloat16)
    )


def pages_travel(queries, new_kv, kv_pages, page_table, cached_len, is_prefill):
    seq_shards = lax.axis_size("seq")
    sub_count = lax.axis_size("sub")
    owners = seq_shards * sub_count
    seq_index = lax.axis_index("seq")
    core_index = lax.axis_index("sub")
    owner_self = seq_index * sub_count + core_index
    seq_dev, row_count, query_width = queries.shape
    pages_dev = kv_pages.shape[0]
    kv_width = kv_pages.shape[3]
    page_count = page_table.shape[1]
    entries = seq_dev * page_count
    capacity = (entries + owners - 1) // owners
    table_rows = page_table.reshape(seq_shards, entries)
    holder = jnp.where(table_rows >= 0, table_rows // pages_dev, -1)
    slot_of = jnp.where(table_rows >= 0, table_rows % pages_dev, 0)
    owned_here = holder == owner_self
    rank_among = jnp.cumsum(owned_here.astype(jnp.int32), axis=1) - 1
    picked = owned_here[:, :, None] & (
        rank_among[:, :, None] == jnp.arange(capacity, dtype=jnp.int32)[None, None, :]
    )
    send_slots = jnp.sum(jnp.where(picked, slot_of[:, :, None], 0), axis=1).reshape(
        seq_shards * capacity
    )
    first_seq = seq_index * seq_dev
    my_table = lax.dynamic_slice_in_dim(page_table, first_seq, seq_dev, 0)
    my_lengths = lax.dynamic_slice_in_dim(cached_len, first_seq, seq_dev, 0)
    my_flags = lax.dynamic_slice_in_dim(is_prefill, first_seq, seq_dev, 0)
    flat_table = my_table.reshape(entries)
    my_holder = jnp.where(flat_table >= 0, flat_table // pages_dev, -1)
    entry_order = jnp.arange(entries, dtype=jnp.int32)
    earlier = (my_holder[:, None] == my_holder[None, :]) & (
        entry_order[None, :] < entry_order[:, None]
    )
    my_rank = jnp.sum(earlier.astype(jnp.int32), axis=1)
    row_ids = jnp.arange(row_count, dtype=jnp.int32)
    live_rows = (my_flags[:, None] == 1) | (row_ids[None, :] == 0)
    causal = row_ids[None, :] <= row_ids[:, None]
    part_width = kv_width // sub_count
    split_pages = kv_pages.reshape(pages_dev, 2, PAGE, sub_count, part_width)
    chosen = jnp.take(split_pages, send_slots, axis=0).reshape(
        seq_shards, capacity, 2, PAGE, sub_count, part_width
    )
    outgoing = jnp.moveaxis(chosen, 4, 1).reshape(owners, capacity, 2, PAGE, part_width)
    received = lax.all_to_all(
        outgoing, ("seq", "sub"), split_axis=0, concat_axis=0, tiled=True
    ).reshape(owners * capacity, 2, PAGE, part_width)
    present = flat_table >= 0
    fetch_index = jnp.where(present, my_holder * capacity + my_rank, 0)
    query_part = query_width // sub_count
    my_queries = lax.dynamic_slice_in_dim(queries, core_index * query_part, query_part, 2)
    my_fresh = lax.dynamic_slice_in_dim(new_kv, core_index * part_width, part_width, 3)
    peak, weight_sum, numerator = attend_all(
        my_queries,
        my_fresh,
        received,
        fetch_index.reshape(seq_dev, page_count),
        present.reshape(seq_dev, page_count),
        my_lengths,
        live_rows,
        causal,
        core_index >= 0,
    )
    own_heads = finish(weight_sum, numerator, live_rows)
    return lax.all_gather(own_heads, "sub", axis=2, tiled=True)


LOG2E = 1.4426950408889634
LANES = 128
NO_KEY = -1e30


def page_plan(page_table, cached_len, is_prefill, shard, core, pages_dev, sub_count, picks):
    seqs, page_count = page_table.shape
    present = page_table >= 0
    owner = jnp.where(present, page_table // pages_dev, -1)
    slot = jnp.where(present, page_table % pages_dev, 0)
    page_ids = jnp.arange(page_count, dtype=jnp.int32)
    keys_here = jnp.clip(cached_len[:, None] - page_ids[None, :] * PAGE, 0, PAGE)
    before = page_ids[None, :] < page_ids[:, None]
    same = owner[:, :, None] == owner[:, None, :]
    rank = jnp.sum((same & before[None]).astype(jnp.int32), axis=2)
    cores = (core + jnp.arange(sub_count, dtype=jnp.int32)) % sub_count
    wanted = shard * sub_count + cores
    picked = (owner[:, None, None, :] == wanted[None, :, None, None]) & (
        rank[:, None, None, :] == jnp.arange(picks, dtype=jnp.int32)[None, None, :, None]
    )
    slots = jnp.sum(jnp.where(picked, slot[:, None, None, :], 0), axis=3)
    counts = jnp.sum(jnp.where(picked, keys_here[:, None, None, :], 0), axis=3)
    rows = jnp.concatenate(
        [
            slots.reshape(seqs, sub_count * picks),
            counts.reshape(seqs, sub_count * picks),
            is_prefill[:, None].astype(jnp.int32),
        ],
        axis=1,
    )
    return jnp.concatenate([jnp.stack([shard, core]).astype(jnp.int32), rows.reshape(-1)])


def lse_block(lse_tile, heads):
    lane = lax.broadcasted_iota(jnp.int32, lse_tile.shape, 1)
    high = lse_tile.astype(jnp.bfloat16)
    rest = lse_tile - high.astype(jnp.float32)
    middle = rest.astype(jnp.bfloat16)
    low = rest - middle.astype(jnp.float32)
    mixed = jnp.where(
        lane < heads,
        high.astype(jnp.float32),
        jnp.where(lane < 2 * heads, middle.astype(jnp.float32), low),
    )
    return mixed.astype(jnp.bfloat16)


def read_lse(block, heads):
    tile = block.astype(jnp.float32)
    return (
        tile
        + pltpu.roll(tile, LANES - heads, 1)
        + pltpu.roll(tile, LANES - 2 * heads, 1)
    )


def spread_lse(lse, heads):
    lane = lax.broadcasted_iota(jnp.int32, lse.shape, 1)
    return jnp.where(
        lane < heads,
        lse,
        jnp.where(lane < 2 * heads, pltpu.roll(lse, heads, 1), pltpu.roll(lse, 2 * heads, 1)),
    )


def work_item(chip, item, shards):
    if 2 * chip >= shards:
        return ("right", item, -item) if item <= chip else ("left", item - chip, item - chip)
    far = shards - 1 - chip
    return ("left", item, item) if item <= far else ("right", item - far, far - item)


def by_chip(shard, values):
    picked = values[0]
    for chip in range(1, len(values)):
        if values[chip] != values[chip - 1]:
            picked = jnp.where(shard >= chip, values[chip], picked)
    return picked


def partial_attention(
    plan, sources, choice, homes, pages, twin_pages, fresh, after, *, first, seq_dev, picks, sub_count
):
    count, row_count, width = sources[0].shape
    part_width = twin_pages.shape[3]
    heads_kv = part_width // HD
    heads = width // HD
    group = heads // heads_kv
    refs_per_seq = sub_count * picks
    record = 2 * refs_per_seq + 1
    scale = LOG2E * HD ** (-0.5)
    few = min(row_count, 16)

    def entry(plan_ref, k, column):
        home = by_chip(plan_ref[0], homes)
        return plan_ref[2 + (home * seq_dev + first + k) * record + column]

    def body(plan_ref, *rest):
        query_refs = rest[: len(sources)]
        page_refs = rest[len(sources) : len(sources) + refs_per_seq]
        fresh_ref = rest[len(sources) + refs_per_seq] if fresh is not None else None
        out_ref, query_buf = rest[-2:]
        k = pl.program_id(0)
        shard = plan_ref[0]
        counts = [entry(plan_ref, k, refs_per_seq + n) for n in range(refs_per_seq)]
        flag = entry(plan_ref, k, 2 * refs_per_seq)
        if len(sources) == 1:
            query_ref = query_refs[0]
        else:
            query_ref = query_buf
            for n in range(len(sources)):
                chips = [chip for chip, c in enumerate(choice) if c == n]
                chosen = shard == chips[0]
                for chip in chips[1:]:
                    chosen = chosen | (shard == chip)

                @pl.when(chosen)
                def _(n=n):
                    query_buf[...] = query_refs[n][...]

        def attend(rows, live_rows):
            lane = lax.broadcasted_iota(jnp.int32, (rows, LANES), 1)
            tile = jnp.zeros((rows, LANES), jnp.float32)
            per_block = max(1, min(group, BLOCK_ROWS // rows))
            stacked = per_block * rows
            key_lane = lax.broadcasted_iota(jnp.int32, (stacked, PAGE), 1)
            for h in range(heads_kv):
                cols = slice(h * HD, (h + 1) * HD)
                keys = jnp.concatenate([r[0, 0, :, cols] for r in page_refs], axis=0)
                values = jnp.concatenate([r[0, 1, :, cols] for r in page_refs], axis=0)
                for g0 in range(0, group, per_block):
                    base = h * group + g0
                    q = jnp.concatenate(
                        [
                            query_ref[0, :rows, (base + g) * HD : (base + g + 1) * HD]
                            for g in range(per_block)
                        ],
                        axis=0,
                    )
                    s = lax.dot_general(
                        q, keys, (((1,), (1,)), ((), ())), preferred_element_type=jnp.float32
                    )
                    scores = [
                        jnp.where(
                            key_lane < counts[n], s[:, n * PAGE : (n + 1) * PAGE] * scale, NO_KEY
                        )
                        for n in range(refs_per_seq)
                    ]
                    peak = scores[0]
                    for x in scores[1:]:
                        peak = jnp.maximum(peak, x)
                    peak = jnp.max(peak, axis=1, keepdims=True)
                    if fresh is not None:
                        s = lax.dot_general(
                            q,
                            fresh_ref[0, 0, :, cols],
                            (((1,), (1,)), ((), ())),
                            preferred_element_type=jnp.float32,
                        )
                        row = lax.broadcasted_iota(jnp.int32, (stacked, row_count), 0) % rows
                        col = lax.broadcasted_iota(jnp.int32, (stacked, row_count), 1)
                        new_scores = jnp.where(
                            (col <= row) & (col < live_rows), s * scale, NO_KEY
                        )
                        peak = jnp.maximum(peak, jnp.max(new_scores, axis=1, keepdims=True))
                    weights = [jnp.exp2(x - peak) for x in scores]
                    sums = weights[0]
                    for w in weights[1:]:
                        sums = sums + w
                    weight_sum = jnp.sum(sums, axis=1, keepdims=True)
                    numerator = lax.dot_general(
                        jnp.concatenate([w.astype(jnp.bfloat16) for w in weights], axis=1),
                        values,
                        (((1,), (0,)), ((), ())),
                        preferred_element_type=jnp.float32,
                    )
                    if fresh is not None:
                        w = jnp.exp2(new_scores - peak)
                        weight_sum = weight_sum + jnp.sum(w, axis=1, keepdims=True)
                        numerator = numerator + lax.dot_general(
                            w.astype(jnp.bfloat16),
                            fresh_ref[1, 0, :, cols],
                            (((1,), (0,)), ((), ())),
                            preferred_element_type=jnp.float32,
                        )
                    attended = (numerator / weight_sum).astype(jnp.bfloat16)
                    lse = peak + jnp.log2(weight_sum)
                    for g in range(per_block):
                        head = base + g
                        part = slice(g * rows, (g + 1) * rows)
                        out_ref[0, :rows, head * HD : (head + 1) * HD] = attended[part]
                        mine = (lane == head) | (lane == head + heads) | (lane == head + 2 * heads)
                        tile = jnp.where(mine, lse[part], tile)
            out_ref[0, :rows, width:] = lse_block(tile, heads)

        @pl.when(flag == 1)
        def _():
            attend(row_count, row_count)

        @pl.when(flag != 1)
        def _():
            attend(few, 1)
            if few < row_count:
                out_ref[0, few:, :] = jnp.zeros((row_count - few, width + LANES), jnp.bfloat16)

    page_block = (1, 2, PAGE, part_width)
    in_specs = [pl.BlockSpec((1, row_count, width), lambda k, p: (k, 0, 0)) for _ in sources]
    operands = list(sources)
    for n in range(picks):
        in_specs.append(
            pl.BlockSpec(page_block, lambda k, p, n=n: (entry(p, k, n), 0, 0, p[1]))
        )
        operands.append(pages)
    for n in range(picks, refs_per_seq):
        in_specs.append(pl.BlockSpec(page_block, lambda k, p, n=n: (entry(p, k, n), 0, 0, 0)))
        operands.append(twin_pages)
    if fresh is not None:
        in_specs.append(
            pl.BlockSpec((2, 1, row_count, part_width), lambda k, p: (0, k, 0, 0))
        )
        operands.append(fresh)
    for x in after:
        in_specs.append(pl.BlockSpec(memory_space=pl.ANY))
        operands.append(x)
    return pl.pallas_call(
        body,
        grid_spec=pltpu.PrefetchScalarGridSpec(
            num_scalar_prefetch=1,
            grid=(count,),
            in_specs=in_specs,
            out_specs=pl.BlockSpec((1, row_count, width + LANES), lambda k, p: (k, 0, 0)),
            scratch_shapes=[pltpu.VMEM((1, row_count, width), jnp.bfloat16)],
        ),
        out_shape=jax.ShapeDtypeStruct((count, row_count, width + LANES), jnp.bfloat16),
        name="partial_attention",
        cost_estimate=pl.CostEstimate(
            flops=count * heads * row_count * refs_per_seq * PAGE * HD * 4,
            bytes_accessed=count * row_count * width * 8,
            transcendentals=count * heads * row_count * refs_per_seq * PAGE,
        ),
    )(plan, *operands)


def merge_weights(lses):
    peak = lses[0]
    for lse in lses[1:]:
        peak = jnp.maximum(peak, lse)
    weights = [jnp.exp2(lse - peak) for lse in lses]
    total = weights[0]
    for w in weights[1:]:
        total = total + w
    return [w / total for w in weights], peak + jnp.log2(total)


def merge_pair(plan, mine, incoming, *, chips):
    count, row_count, full = mine.shape
    width = full - LANES
    heads = width // HD

    def body(plan_ref, mine_hbm, incoming_hbm, out_ref, mine_ref, incoming_ref, sems):
        here = plan_ref[0] == chips[0]
        for chip in chips[1:]:
            here = here | (plan_ref[0] == chip)

        @pl.when(here)
        def _():
            copies = [
                pltpu.make_async_copy(mine_hbm, mine_ref, sems.at[0]),
                pltpu.make_async_copy(incoming_hbm, incoming_ref, sems.at[1]),
            ]
            for c in copies:
                c.start()
            for c in copies:
                c.wait()
            parts = [mine_ref, incoming_ref]
            for k in range(count):
                weights, lse = merge_weights([read_lse(r[k, :, width:], heads) for r in parts])
                for h in range(heads):
                    cols = slice(h * HD, (h + 1) * HD)
                    out_ref[k, :, cols] = sum(
                        r[k, :, cols].astype(jnp.float32) * w[:, h : h + 1]
                        for r, w in zip(parts, weights)
                    ).astype(jnp.bfloat16)
                out_ref[k, :, width:] = lse_block(spread_lse(lse, heads), heads)

    any_spec = pl.BlockSpec(memory_space=pl.ANY)
    return pl.pallas_call(
        body,
        grid_spec=pltpu.PrefetchScalarGridSpec(
            num_scalar_prefetch=1,
            grid=(1,),
            in_specs=[any_spec, any_spec],
            out_specs=pl.BlockSpec(mine.shape, lambda g, p: (0, 0, 0)),
            scratch_shapes=[
                pltpu.VMEM(mine.shape, jnp.bfloat16),
                pltpu.VMEM(mine.shape, jnp.bfloat16),
                pltpu.SemaphoreType.DMA((2,)),
            ],
        ),
        out_shape=jax.ShapeDtypeStruct(mine.shape, jnp.bfloat16),
        name="merge_pair",
    )(plan, mine, incoming)


def merge_final(plan, own, arrived, *, first, shards, seq_dev, record):
    count, row_count, full = own.shape
    width = full - LANES
    heads = width // HD
    last = shards - 1

    def body(plan_ref, own_ref, *rest):
        arrived_refs = rest[:last]
        out_ref, right_buf, left_buf, sems = rest[last:]
        shard = plan_ref[0]
        for s, r in enumerate(arrived_refs):
            @pl.when(shard == s)
            def _(r=r):
                pltpu.make_async_copy(r, right_buf, sems.at[0]).start()

            @pl.when(shard == last - s)
            def _(r=r):
                pltpu.make_async_copy(r, left_buf, sems.at[1]).start()

        @pl.when(shard < shards - 1)
        def _():
            pltpu.make_async_copy(arrived_refs[0], right_buf, sems.at[0]).wait()

        @pl.when(shard > 0)
        def _():
            pltpu.make_async_copy(arrived_refs[0], left_buf, sems.at[1]).wait()

        def one(k, carry):
            empty = jnp.full((row_count, LANES), NO_KEY, jnp.float32)
            right_lse = read_lse(right_buf[k, :, width:], heads)
            left_lse = read_lse(left_buf[k, :, width:], heads)
            right_on = shard < shards - 1
            left_on = shard > 0
            lses = [
                read_lse(own_ref[k, :, width:], heads),
                jnp.where(right_on, right_lse, empty),
                jnp.where(left_on, left_lse, empty),
            ]
            weights, _ = merge_weights(lses)
            row = lax.broadcasted_iota(jnp.int32, (row_count, HD), 0)
            flag = plan_ref[2 + (shard * seq_dev + first + k) * record + record - 1]
            live = row < jnp.where(flag == 1, row_count, 1)
            for h in range(heads):
                cols = slice(h * HD, (h + 1) * HD)
                total = own_ref[k, :, cols].astype(jnp.float32) * weights[0][:, h : h + 1]
                total = total + jnp.where(
                    right_on, right_buf[k, :, cols].astype(jnp.float32), 0.0
                ) * weights[1][:, h : h + 1]
                total = total + jnp.where(
                    left_on, left_buf[k, :, cols].astype(jnp.float32), 0.0
                ) * weights[2][:, h : h + 1]
                out_ref[k, :, cols] = jnp.where(live, total, 0.0).astype(jnp.bfloat16)
            return carry

        lax.fori_loop(0, count, one, 0)

    any_spec = pl.BlockSpec(memory_space=pl.ANY)
    return pl.pallas_call(
        body,
        grid_spec=pltpu.PrefetchScalarGridSpec(
            num_scalar_prefetch=1,
            grid=(1,),
            in_specs=[pl.BlockSpec((count, row_count, full), lambda g, p: (0, 0, 0))]
            + [any_spec] * last,
            out_specs=pl.BlockSpec((count, row_count, width), lambda g, p: (0, 0, 0)),
            scratch_shapes=[
                pltpu.VMEM(own.shape, jnp.bfloat16),
                pltpu.VMEM(own.shape, jnp.bfloat16),
                pltpu.SemaphoreType.DMA((2,)),
            ],
        ),
        out_shape=jax.ShapeDtypeStruct((count, row_count, width), jnp.bfloat16),
        name="merge_final",
    )(plan, own, *arrived)


CHUNKS = 2
BLOCK_ROWS = 512


def queries_travel(queries, new_kv, kv_pages, page_table, cached_len, is_prefill):
    shards = lax.axis_size("seq")
    sub_count = lax.axis_size("sub")
    owners = shards * sub_count
    shard = lax.axis_index("seq")
    core = lax.axis_index("sub")
    seq_dev, row_count, query_width = queries.shape
    pages_dev = kv_pages.shape[0]
    part_width = kv_pages.shape[3] // sub_count
    query_part = query_width // sub_count
    picks = -(-page_table.shape[1] // owners)
    record = 2 * sub_count * picks + 1
    chunk = seq_dev // CHUNKS
    firsts = [n * chunk for n in range(CHUNKS)]
    last = shards - 1

    my_queries = lax.dynamic_slice_in_dim(queries, core * query_part, query_part, 2)
    my_queries, later_pages = lax.optimization_barrier((my_queries, kv_pages))
    own_queries = [my_queries[f : f + chunk] for f in firsts]
    plan = page_plan(
        page_table, cached_len, is_prefill, shard, core, pages_dev, sub_count, picks
    )

    twin = lax.dynamic_slice_in_dim(later_pages, (1 - core) * part_width, part_width, 3)
    twin_pages = lax.ppermute(twin, "sub", [(0, 1), (1, 0)])
    fresh = jnp.transpose(
        lax.dynamic_slice_in_dim(new_kv, core * part_width, part_width, 3), (2, 0, 1, 3)
    )

    def partial(n, sources, choice, homes, fresh_part=None, after=()):
        return partial_attention(
            plan,
            sources,
            choice,
            homes,
            kv_pages,
            twin_pages,
            fresh_part,
            after,
            first=firsts[n],
            seq_dev=seq_dev,
            picks=picks,
            sub_count=sub_count,
        )

    own = [
        partial(
            n,
            [own_queries[n]],
            [0] * shards,
            list(range(shards)),
            fresh[:, firsts[n] : firsts[n] + chunk],
        )
        for n in range(CHUNKS)
    ]
    hops = {"right": [own_queries], "left": [own_queries]}
    work = {}
    previous = tuple(own)

    def attend(item, previous):
        items = [work_item(chip, item, shards) for chip in range(shards)]
        kinds = sorted({(way, h) for way, h, _ in items})
        choice = [kinds.index((way, h)) for way, h, _ in items]
        homes = [chip + offset for chip, (_, _, offset) in enumerate(items)]
        for n in range(CHUNKS):
            work[item, n] = partial(
                n, [hops[way][h][n] for way, h in kinds], choice, homes, after=previous
            )
            previous = (work[item, n],)
        return previous

    for h in range(1, shards):
        up = [(a, a + 1) for a in range(h - 1, last)]
        down = [(a, a - 1) for a in range(1, shards - h + 1)]
        moved = {"right": [], "left": []}
        for n in range(CHUNKS):
            for way, pairs in (("right", up), ("left", down)):
                leaving = hops[way][-1][n]
                if h > 1:
                    gate = own[n] if h == 2 else work[h - 2, n]
                    leaving, _ = lax.optimization_barrier((leaving, gate))
                moved[way].append(lax.ppermute(leaving, "seq", pairs))
        for way in hops:
            hops[way].append(moved[way])
        previous = attend(h, previous)

    moved = {}
    waves = sorted(
        ((last - s) + (last - 1 - l), s, l) for s in range(last) for l in range(s, last)
    )
    for _, s, l in waves:
        sender = l + 1
        mirror = last - sender
        way = ("right", sender - s)
        item = next(w for w in range(1, shards) if work_item(sender, w, shards)[:2] == way)
        pairs = [(sender, sender - 1), (mirror, mirror + 1)]
        for n in range(CHUNKS):
            mine = work[item, n]
            if sender < last:
                mine = merge_pair(plan, mine, moved[s, l + 1, n], chips=(sender, mirror))
            moved[s, l, n] = lax.ppermute(mine, "seq", pairs)
    outs = [
        merge_final(
            plan,
            own[n],
            [moved[s, s, n] for s in range(last)],
            first=firsts[n],
            shards=shards,
            seq_dev=seq_dev,
            record=record,
        )
        for n in range(CHUNKS)
    ]
    swapped = [lax.ppermute(o, "sub", [(0, 1), (1, 0)]) for o in outs]
    own_half = jnp.concatenate(outs, axis=0)
    other_half = jnp.concatenate(swapped, axis=0)
    first_core = core == 0
    return jnp.concatenate(
        [jnp.where(first_core, own_half, other_half), jnp.where(first_core, other_half, own_half)],
        axis=2,
    )


def per_device(queries, new_kv, kv_pages, page_table, cached_len, is_prefill):
    shards = lax.axis_size("seq")
    sub_count = lax.axis_size("sub")
    heads = queries.shape[2] // sub_count // HD
    spread = page_table.shape[1] >= shards * sub_count and shards % 2 == 0 and sub_count == 2
    if spread and 3 * heads <= LANES and queries.shape[0] % CHUNKS == 0:
        return queries_travel(queries, new_kv, kv_pages, page_table, cached_len, is_prefill)
    return pages_travel(queries, new_kv, kv_pages, page_table, cached_len, is_prefill)


def solution(mesh):
    placed = (
        P(("groups", "seq"), None, "head"),
        P(("groups", "seq"), None, None, "head"),
        P(("groups", "seq", "sub"), None, None, "head"),
        P("groups", None),
        P("groups"),
        P("groups"),
    )
    return jax.shard_map(
        per_device,
        mesh=mesh,
        in_specs=placed,
        out_specs=P(("groups", "seq"), None, "head"),
        check_vma=False,
    )
```

profile of v0, /device:TPU:0, one launch (start us, length us, event | category | flops | bytes accessed | tf_op | source)
XLA Modules:
  0.0 167.3 jit_solution(10745053577463791109)
XLA Ops:
  0.0 1.6 copy-done
  1.7 3.7 %constant_dynamic-slice_fusion.1 = bf16[21,2,128,256]{3,2,1,0:T(8,128)(2,1)} fusion(bf16[21,2,128,512]{3,2,1,0:T(8,128)(2,1)} %rest_5_.3, s32[]{:T(128)S(6)} %select_n.66), kind=kLoop, calls=%fused_computation.30 | loop fusion | bytes 5505028 | tf_op jit(solution)/shard_map/dynamic_slice | solution.py:575
  5.4 0.5 collective-permute-start
  5.9 1.1 fusion.7
  6.9 1.3 collective-permute-start.1
  8.2 5.9 %collective-permute-start.3 = (bf16[2,64,2048]{2,1,0:T(8,128)(2,1)}, bf16[2,64,2048]{2,1,0:T(8,128)(2,1)}, u32[]{:S(2)}, u32[]{:S(2)}) collective-permute-start(bf16[2,64,2048]{2,1,0:T(8,128)(2,1)} %get-tuple-element.30.rest_0_), channel_id=1, source_target_pairs={{0,4},{4,8},{8,12},{1,5},{5,9},{9,13},{2,6},{6,10},{10,14},{3,7},{... | collective-permute-start | bytes 1572872 | tf_op jit(solution)/shard_map/ppermute | solution.py:633
  14.1 1.3 collective-permute-start.7
  15.4 4.6 %collective-permute-start.9 = (bf16[2,64,2048]{2,1,0:T(8,128)(2,1)}, bf16[2,64,2048]{2,1,0:T(8,128)(2,1)S(1)}, u32[]{:S(2)}, u32[]{:S(2)}) collective-permute-start(bf16[2,64,2048]{2,1,0:T(8,128)(2,1)} %get-tuple-element.29.rest_0_), channel_id=1, source_target_pairs={{0,4},{4,8},{8,12},{1,5},{5,9},{9,13},{2,6},{6,10},{10,14},{3,7},{... | collective-permute-start | bytes 1572872 | tf_op jit(solution)/shard_map/ppermute | solution.py:633
  20.1 0.1 fusion.2
  20.2 0.4 convert_reduce_fusion
  20.7 0.2 fusion
  20.9 0.1 copy.10
  21.0 0.1 reshape.86
  21.1 1.1 constant_dynamic-slice_fusion
  22.2 0.7 pad_add_fusion.1.plan_ref
  22.9 0.7 fusion.8
  23.7 5.6 %partial_attention.8.rest_6_.own_ref = bf16[2,64,2176]{2,1,0:T(8,128)(2,1)} custom-call(s32[146]{0:T(256)} %pad_add_fusion.1.plan_ref, bf16[2,64,2048]{2,1,0:T(8,128)(2,1)} %get-tuple-element.30.rest_0_, bf16[21,2,128,512]{3,2,1,0:T(8,128)(2,1)} %rest_5_.3, bf16[21,2,128,512]{3,2,1,0:T(8,128)(2,1)} %rest_5_.3, ...), custom_call_target="tpu_custom_call" | custom-call | flops 536870912 | bytes 2097152 | tf_op jit(solution)/shard_map/partial_attention/pallas_call | solution.py:392
  29.3 1.3 collective-permute-start.2
  30.6 1.5 collective-permute-start.5
  32.0 5.6 %partial_attention.9.rest_7_.own_ref = bf16[2,64,2176]{2,1,0:T(8,128)(2,1)} custom-call(s32[146]{0:T(256)} %pad_add_fusion.1.plan_ref, bf16[2,64,2048]{2,1,0:T(8,128)(2,1)} %get-tuple-element.29.rest_0_, bf16[21,2,128,512]{3,2,1,0:T(8,128)(2,1)} %rest_5_.3, bf16[21,2,128,512]{3,2,1,0:T(8,128)(2,1)} %rest_5_.3, ...), custom_call_target="tpu_custom_call" | custom-call | flops 536870912 | bytes 2097152 | tf_op jit(solution)/shard_map/partial_attention/pallas_call | solution.py:392
  37.6 1.3 collective-permute-start.8
  38.9 1.5 collective-permute-start.10
  40.4 4.2 %partial_attention.10.rest_6_.mine_hbm = bf16[2,64,2176]{2,1,0:T(8,128)(2,1)} custom-call(s32[146]{0:T(256)} %pad_add_fusion.1.plan_ref, bf16[2,64,2048]{2,1,0:T(8,128)(2,1)} %collective-permute-done.1.rest_0_, bf16[2,64,2048]{2,1,0:T(8,128)(2,1)} %collective-permute-done.3.rest_1_.rest_2_, bf16[21,2,128,512]{3,2,1,0:T(8,128)(2,1)} %rest_5_.3, ...), custom_call_target="tpu_custom_call" | custom-call | flops 536870912 | bytes 2097152 | tf_op jit(solution)/shard_map/partial_attention/pallas_call | solution.py:392
  44.7 2.3 %collective-permute-done.2.rest_0_ = bf16[2,64,2048]{2,1,0:T(8,128)(2,1)} collective-permute-done((bf16[2,64,2048]{2,1,0:T(8,128)(2,1)}, bf16[2,64,2048]{2,1,0:T(8,128)(2,1)}, u32[]{:S(2)}, u32[]{:S(2)}) %collective-permute-start.2) | collective-permute-done | bytes 524320 | tf_op jit(solution)/shard_map/ppermute | solution.py:633
  47.0 1.3 collective-permute-start.4
  48.3 1.5 collective-permute-start.6
  49.7 4.5 %partial_attention.11.rest_6_.mine_hbm = bf16[2,64,2176]{2,1,0:T(8,128)(2,1)} custom-call(s32[146]{0:T(256)} %pad_add_fusion.1.plan_ref, bf16[2,64,2048]{2,1,0:T(8,128)(2,1)} %copy-done.3, bf16[2,64,2048]{2,1,0:T(8,128)(2,1)} %copy-done.4, bf16[21,2,128,512]{3,2,1,0:T(8,128)(2,1)} %rest_5_.3, bf16[21,2,128,512]{3,2,1,0:T(8,128)(2,1)} %rest_5_.3, ...), custom_call_target="tpu_custom_call" | custom-call | flops 536870912 | bytes 2097152 | tf_op jit(solution)/shard_map/partial_attention/pallas_call | solution.py:392
  54.3 3.9 %collective-permute-done.8.rest_0_ = bf16[2,64,2048]{2,1,0:T(8,128)(2,1)} collective-permute-done((bf16[2,64,2048]{2,1,0:T(8,128)(2,1)S(1)}, bf16[2,64,2048]{2,1,0:T(8,128)(2,1)}, u32[]{:S(2)}, u32[]{:S(2)}) %collective-permute-start.8) | collective-permute-done | bytes 524320 | tf_op jit(solution)/shard_map/ppermute | solution.py:633
  58.2 1.3 collective-permute-start.17
  59.5 0.9 collective-permute-start.18
  60.4 4.6 %partial_attention.12.rest_6_.mine_hbm = bf16[2,64,2176]{2,1,0:T(8,128)(2,1)} custom-call(s32[146]{0:T(256)} %pad_add_fusion.1.plan_ref, bf16[2,64,2048]{2,1,0:T(8,128)(2,1)} %collective-permute-done.2.rest_0_, bf16[2,64,2048]{2,1,0:T(8,128)(2,1)} %collective-permute-done.5.rest_1_, bf16[21,2,128,512]{3,2,1,0:T(8,128)(2,1)} %rest_5_.3, ...), custom_call_target="tpu_custom_call" | custom-call | flops 536870912 | bytes 2097152 | tf_op jit(solution)/shard_map/partial_attention/pallas_call | solution.py:392
  65.0 4.7 %partial_attention.13.rest_8_.mine_hbm = bf16[2,64,2176]{2,1,0:T(8,128)(2,1)} custom-call(s32[146]{0:T(256)} %pad_add_fusion.1.plan_ref, bf16[2,64,2048]{2,1,0:T(8,128)(2,1)} %collective-permute-done.8.rest_0_, bf16[2,64,2048]{2,1,0:T(8,128)(2,1)} %collective-permute-done.10.rest_1_, bf16[21,2,128,512]{3,2,1,0:T(8,128)(2,1)} %rest_5_.3, ...), custom_call_target="tpu_custom_call" | custom-call | flops 536870912 | bytes 2097152 | tf_op jit(solution)/shard_map/partial_attention/pallas_call | solution.py:392
  69.7 5.1 %partial_attention.14.mine_hbm.rest_8_ = bf16[2,64,2176]{2,1,0:T(8,128)(2,1)} custom-call(s32[146]{0:T(256)} %pad_add_fusion.1.plan_ref, bf16[2,64,2048]{2,1,0:T(8,128)(2,1)} %collective-permute-done.1.rest_0_, bf16[2,64,2048]{2,1,0:T(8,128)(2,1)} %collective-permute-done.4.rest_1_, bf16[2,64,2048]{2,1,0:T(8,128)(2,1)} %collective-permute-done.3.rest_1_.rest_2_, ...), custom_call_target="tpu_custom_call" | custom-call | flops 536870912 | bytes 2097152 | tf_op jit(solution)/shard_map/partial_attention/pallas_call | solution.py:392
  74.9 6.3 %collective-permute-start.11 = (bf16[2,64,2176]{2,1,0:T(8,128)(2,1)}, bf16[2,64,2176]{2,1,0:T(8,128)(2,1)S(1)}, u32[]{:S(2)}, u32[]{:S(2)}) collective-permute-start(bf16[2,64,2176]{2,1,0:T(8,128)(2,1)} %partial_attention.14.mine_hbm.rest_8_), channel_id=1, source_target_pairs={{12,8},{0,4},{13,9},{1,5},{14,10},{2,6},{15,11},{3,7},{28,24},{16,... | collective-permute-start | bytes 1671176 | tf_op jit(solution)/shard_map/ppermute | solution.py:652
  81.2 0.8 copy-done.7
  82.0 4.5 %partial_attention.15.mine_hbm = bf16[2,64,2176]{2,1,0:T(8,128)(2,1)} custom-call(s32[146]{0:T(256)} %pad_add_fusion.1.plan_ref, bf16[2,64,2048]{2,1,0:T(8,128)(2,1)} %copy-done.3, bf16[2,64,2048]{2,1,0:T(8,128)(2,1)} %collective-permute-done.17.rest_1_, bf16[2,64,2048]{2,1,0:T(8,128)(2,1)} %copy-done.4, bf16[2,64,2048]{2,1,0:T(8,128)(2,1)} %copy-done.7, ...), custom_call_target="tpu_custom_call" | custom-call | flops 536870912 | bytes 2097152 | tf_op jit(solution)/shard_map/partial_attention/pallas_call | solution.py:392
  86.5 2.8 %collective-permute-start.19 = (bf16[2,64,2176]{2,1,0:T(8,128)(2,1)}, bf16[2,64,2176]{2,1,0:T(8,128)(2,1)}, u32[]{:S(2)}, u32[]{:S(2)}) collective-permute-start(bf16[2,64,2176]{2,1,0:T(8,128)(2,1)} %partial_attention.15.mine_hbm), channel_id=1, source_target_pairs={{12,8},{0,4},{13,9},{1,5},{14,10},{2,6},{15,11},{3,7},{28,24},{16,... | collective-permute-start | bytes 1671176 | tf_op jit(solution)/shard_map/ppermute | solution.py:652
  89.4 2.2 %collective-permute-start.14 = (bf16[2,64,2176]{2,1,0:T(8,128)(2,1)}, bf16[2,64,2176]{2,1,0:T(8,128)(2,1)}, u32[]{:S(2)}, u32[]{:S(2)}) collective-permute-start(bf16[2,64,2176]{2,1,0:T(8,128)(2,1)} %partial_attention.12.rest_6_.mine_hbm), channel_id=1, source_target_pairs={{12,8},{0,4},{13,9},{1,5},{14,10},{2,6},{15,11},{3,7},{28,24},{16,... | collective-permute-start | bytes 1671176 | tf_op jit(solution)/shard_map/ppermute | solution.py:652
  91.5 2.9 %collective-permute-done.11.incoming_hbm = bf16[2,64,2176]{2,1,0:T(8,128)(2,1)S(1)} collective-permute-done((bf16[2,64,2176]{2,1,0:T(8,128)(2,1)}, bf16[2,64,2176]{2,1,0:T(8,128)(2,1)S(1)}, u32[]{:S(2)}, u32[]{:S(2)}) %collective-permute-start.11) | collective-permute-done | bytes 557088 | tf_op jit(solution)/shard_map/ppermute | solution.py:652
  94.5 0.8 copy-done.6
  95.3 1.6 merge_pair.6
  96.8 1.6 collective-permute-start.12
  98.5 12.4 %collective-permute-start.22 = (bf16[2,64,2176]{2,1,0:T(8,128)(2,1)}, bf16[2,64,2176]{2,1,0:T(8,128)(2,1)}, u32[]{:S(2)}, u32[]{:S(2)}) collective-permute-start(bf16[2,64,2176]{2,1,0:T(8,128)(2,1)} %partial_attention.13.rest_8_.mine_hbm), channel_id=1, source_target_pairs={{12,8},{0,4},{13,9},{1,5},{14,10},{2,6},{15,11},{3,7},{28,24},{16,... | collective-permute-start | bytes 1671176 | tf_op jit(solution)/shard_map/ppermute | solution.py:652
  110.9 1.5 merge_pair.9
  112.4 1.5 collective-permute-start.20
  113.9 8.1 %collective-permute-start.16 = (bf16[2,64,2176]{2,1,0:T(8,128)(2,1)S(1)}, bf16[2,64,2176]{2,1,0:T(8,128)(2,1)}, u32[]{:S(2)}, u32[]{:S(2)}) collective-permute-start(bf16[2,64,2176]{2,1,0:T(8,128)(2,1)S(1)} %copy-done.2), channel_id=1, source_target_pairs={{12,8},{0,4},{13,9},{1,5},{14,10},{2,6},{15,11},{3,7},{28,24},{16,... | collective-permute-start | bytes 1671176 | tf_op jit(solution)/shard_map/ppermute | solution.py:652
  121.9 1.5 merge_pair.8
  123.5 1.5 collective-permute-start.15
  124.9 1.5 merge_pair.7
  126.5 1.3 collective-permute-start.13
  127.8 2.5 %collective-permute-done.22.incoming_hbm = bf16[2,64,2176]{2,1,0:T(8,128)(2,1)} collective-permute-done((bf16[2,64,2176]{2,1,0:T(8,128)(2,1)}, bf16[2,64,2176]{2,1,0:T(8,128)(2,1)}, u32[]{:S(2)}, u32[]{:S(2)}) %collective-permute-start.22) | collective-permute-done | bytes 557088 | tf_op jit(solution)/shard_map/ppermute | solution.py:652
  130.3 9.6 %collective-permute-start.24 = (bf16[2,64,2176]{2,1,0:T(8,128)(2,1)S(1)}, bf16[2,64,2176]{2,1,0:T(8,128)(2,1)}, u32[]{:S(2)}, u32[]{:S(2)}) collective-permute-start(bf16[2,64,2176]{2,1,0:T(8,128)(2,1)S(1)} %copy-done.1), channel_id=1, source_target_pairs={{12,8},{0,4},{13,9},{1,5},{14,10},{2,6},{15,11},{3,7},{28,24},{16,... | collective-permute-start | bytes 1671176 | tf_op jit(solution)/shard_map/ppermute | solution.py:652
  139.8 1.5 merge_pair.11
  141.4 1.5 collective-permute-start.23
  142.8 1.7 %merge_pair.10 = bf16[2,64,2176]{2,1,0:T(8,128)(2,1)} custom-call(s32[146]{0:T(256)} %pad_add_fusion.1.plan_ref, bf16[2,64,2176]{2,1,0:T(8,128)(2,1)} %partial_attention.15.mine_hbm, bf16[2,64,2176]{2,1,0:T(8,128)(2,1)} %collective-permute-done.20.incoming_hbm), custom_call_target="tpu_custom_call" | custom-call | tf_op jit(solution)/shard_map/merge_pair/pallas_call | solution.py:454
  144.6 1.3 collective-permute-start.21
  145.9 4.9 %merge_final.2 = bf16[2,64,2048]{2,1,0:T(8,128)(2,1)} custom-call(s32[146]{0:T(256)} %pad_add_fusion.1.plan_ref, bf16[2,64,2176]{2,1,0:T(8,128)(2,1)} %partial_attention.8.rest_6_.own_ref, bf16[2,64,2176]{2,1,0:T(8,128)(2,1)} %collective-permute-done.13.rest_0_, bf16[2,64,2176]{2,1,0:T(8,128)(2,1)} %collective-permute-done.15.rest_1_, ...), custom_call_target="tpu_custom_call" | custom-call | tf_op jit(solution)/shard_map/merge_final/pallas_call | solution.py:529
  150.9 0.8 collective-permute-done.24.rest_2_
  151.7 5.8 %collective-permute-done.21.rest_0_ = bf16[2,64,2176]{2,1,0:T(8,128)(2,1)} collective-permute-done((bf16[2,64,2176]{2,1,0:T(8,128)(2,1)}, bf16[2,64,2176]{2,1,0:T(8,128)(2,1)}, u32[]{:S(2)}, u32[]{:S(2)}) %collective-permute-start.21) | collective-permute-done | bytes 557088 | tf_op jit(solution)/shard_map/ppermute | solution.py:652
  157.5 4.8 %merge_final.3 = bf16[2,64,2048]{2,1,0:T(8,128)(2,1)} custom-call(s32[146]{0:T(256)} %pad_add_fusion.1.plan_ref, bf16[2,64,2176]{2,1,0:T(8,128)(2,1)} %partial_attention.9.rest_7_.own_ref, bf16[2,64,2176]{2,1,0:T(8,128)(2,1)} %collective-permute-done.21.rest_0_, bf16[2,64,2176]{2,1,0:T(8,128)(2,1)} %collective-permute-done.23.rest_1_, ...), custom_call_target="tpu_custom_call" | custom-call | tf_op jit(solution)/shard_map/merge_final/pallas_call | solution.py:529
  162.5 1.1 constant_dynamic-update-slice_fusion.1
  163.6 1.0 collective-permute-done.26
  164.6 1.2 broadcast_select_fusion.1
  165.8 1.5 pad_maximum_fusion
  (50 shorter events, 0.5 us)
Async XLA Ops:
  0.0 1.6 copy-start
  1.7 18.4 %copy-start.8 = (s32[16,16]{1,0:T(8,128)S(1)}, s32[16,16]{1,0:T(8,128)}, u32[]{:S(2)}) copy-start(s32[16,16]{1,0:T(8,128)} %param.9) | copy-start | bytes 3076
  1.7 18.4 %copy-start.9 = (s32[16]{0:T(128)S(1)}, s32[16]{0:T(128)}, u32[]{:S(2)}) copy-start(s32[16]{0:T(128)} %param.10) | copy-start | bytes 196
  1.7 19.2 %copy-start.10 = (s32[16]{0:T(128)S(1)}, s32[16]{0:T(128)}, u32[]{:S(2)}) copy-start(s32[16]{0:T(128)} %param.11) | copy-start | bytes 196
  5.4 18.3 %collective-permute-start = (bf16[21,2,128,256]{3,2,1,0:T(8,128)(2,1)}, bf16[21,2,128,256]{3,2,1,0:T(8,128)(2,1)}, u32[]{:S(2)}, u32[]{:S(2)}) collective-permute-start(bf16[21,2,128,256]{3,2,1,0:T(8,128)(2,1)} %constant_dynamic-slice_fusion.1), channel_id=1, source_target_pairs={{0,1},{1,0},{2,3},{3,2},{4,5},{5,4},{6,7},{7,6},{8,9},{9,8},{10,11... | collective-permute-start | bytes 8257544 | tf_op jit(solution)/shard_map/ppermute | solution.py:576
  6.9 22.3 %collective-permute-start.1 = (bf16[2,64,2048]{2,1,0:T(8,128)(2,1)}, bf16[2,64,2048]{2,1,0:T(8,128)(2,1)}, u32[]{:S(2)}, u32[]{:S(2)}) collective-permute-start(bf16[2,64,2048]{2,1,0:T(8,128)(2,1)} %get-tuple-element.30.rest_0_), channel_id=1, source_target_pairs={{4,0},{8,4},{12,8},{5,1},{9,5},{13,9},{6,2},{10,6},{14,10},{7,3},{... | collective-permute-start | bytes 1572872 | tf_op jit(solution)/shard_map/ppermute | solution.py:633
  8.2 22.3 %collective-permute-start.3 = (bf16[2,64,2048]{2,1,0:T(8,128)(2,1)}, bf16[2,64,2048]{2,1,0:T(8,128)(2,1)}, u32[]{:S(2)}, u32[]{:S(2)}) collective-permute-start(bf16[2,64,2048]{2,1,0:T(8,128)(2,1)} %get-tuple-element.30.rest_0_), channel_id=1, source_target_pairs={{0,4},{4,8},{8,12},{1,5},{5,9},{9,13},{2,6},{6,10},{10,14},{3,7},{... | collective-permute-start | bytes 1572872 | tf_op jit(solution)/shard_map/ppermute | solution.py:633
  14.1 23.5 %collective-permute-start.7 = (bf16[2,64,2048]{2,1,0:T(8,128)(2,1)}, bf16[2,64,2048]{2,1,0:T(8,128)(2,1)S(1)}, u32[]{:S(2)}, u32[]{:S(2)}) collective-permute-start(bf16[2,64,2048]{2,1,0:T(8,128)(2,1)} %get-tuple-element.29.rest_0_), channel_id=1, source_target_pairs={{4,0},{8,4},{12,8},{5,1},{9,5},{13,9},{6,2},{10,6},{14,10},{7,3},{... | collective-permute-start | bytes 1572872 | tf_op jit(solution)/shard_map/ppermute | solution.py:633
  15.4 23.5 %collective-permute-start.9 = (bf16[2,64,2048]{2,1,0:T(8,128)(2,1)}, bf16[2,64,2048]{2,1,0:T(8,128)(2,1)S(1)}, u32[]{:S(2)}, u32[]{:S(2)}) collective-permute-start(bf16[2,64,2048]{2,1,0:T(8,128)(2,1)} %get-tuple-element.29.rest_0_), channel_id=1, source_target_pairs={{0,4},{4,8},{8,12},{1,5},{5,9},{9,13},{2,6},{6,10},{10,14},{3,7},{... | collective-permute-start | bytes 1572872 | tf_op jit(solution)/shard_map/ppermute | solution.py:633
  29.3 17.7 %collective-permute-start.2 = (bf16[2,64,2048]{2,1,0:T(8,128)(2,1)}, bf16[2,64,2048]{2,1,0:T(8,128)(2,1)}, u32[]{:S(2)}, u32[]{:S(2)}) collective-permute-start(bf16[2,64,2048]{2,1,0:T(8,128)(2,1)} %collective-permute-done.1.rest_0_), channel_id=1, source_target_pairs={{4,0},{8,4},{5,1},{9,5},{6,2},{10,6},{7,3},{11,7},{20,16},{24,20},... | collective-permute-start | bytes 1572872 | tf_op jit(solution)/shard_map/ppermute | solution.py:633
  30.6 17.7 %collective-permute-start.5 = (bf16[2,64,2048]{2,1,0:T(8,128)(2,1)}, bf16[2,64,2048]{2,1,0:T(8,128)(2,1)}, u32[]{:S(2)}, u32[]{:S(2)}) collective-permute-start(bf16[2,64,2048]{2,1,0:T(8,128)(2,1)} %collective-permute-done.3.rest_1_.rest_2_), channel_id=1, source_target_pairs={{4,8},{8,12},{5,9},{9,13},{6,10},{10,14},{7,11},{11,15},{20,24},{2... | collective-permute-start | bytes 1572872 | tf_op jit(solution)/shard_map/ppermute | solution.py:633
  37.6 7.0 %copy-start.3 = (bf16[2,64,2048]{2,1,0:T(8,128)(2,1)}, bf16[2,64,2048]{2,1,0:T(8,128)(2,1)S(1)}, u32[]{:S(2)}) copy-start(bf16[2,64,2048]{2,1,0:T(8,128)(2,1)S(1)} %collective-permute-done.7.rest_0_) | copy-start | bytes 1572868
  37.6 20.6 %collective-permute-start.8 = (bf16[2,64,2048]{2,1,0:T(8,128)(2,1)S(1)}, bf16[2,64,2048]{2,1,0:T(8,128)(2,1)}, u32[]{:S(2)}, u32[]{:S(2)}) collective-permute-start(bf16[2,64,2048]{2,1,0:T(8,128)(2,1)S(1)} %collective-permute-done.7.rest_0_), channel_id=1, source_target_pairs={{4,0},{8,4},{5,1},{9,5},{6,2},{10,6},{7,3},{11,7},{20,16},{24,20},... | collective-permute-start | bytes 1572872 | tf_op jit(solution)/shard_map/ppermute | solution.py:633
  38.9 5.7 %copy-start.4 = (bf16[2,64,2048]{2,1,0:T(8,128)(2,1)}, bf16[2,64,2048]{2,1,0:T(8,128)(2,1)S(1)}, u32[]{:S(2)}) copy-start(bf16[2,64,2048]{2,1,0:T(8,128)(2,1)S(1)} %collective-permute-done.9.rest_1_.rest_2_) | copy-start | bytes 1572868
  38.9 20.5 %collective-permute-start.10 = (bf16[2,64,2048]{2,1,0:T(8,128)(2,1)S(1)}, bf16[2,64,2048]{2,1,0:T(8,128)(2,1)}, u32[]{:S(2)}, u32[]{:S(2)}) collective-permute-start(bf16[2,64,2048]{2,1,0:T(8,128)(2,1)S(1)} %collective-permute-done.9.rest_1_.rest_2_), channel_id=1, source_target_pairs={{4,8},{8,12},{5,9},{9,13},{6,10},{10,14},{7,11},{11,15},{20,24},{2... | collective-permute-start | bytes 1572872 | tf_op jit(solution)/shard_map/ppermute | solution.py:633
  47.0 22.7 %collective-permute-start.4 = (bf16[2,64,2048]{2,1,0:T(8,128)(2,1)}, bf16[2,64,2048]{2,1,0:T(8,128)(2,1)}, u32[]{:S(2)}, u32[]{:S(2)}) collective-permute-start(bf16[2,64,2048]{2,1,0:T(8,128)(2,1)} %collective-permute-done.2.rest_0_), channel_id=1, source_target_pairs={{4,0},{5,1},{6,2},{7,3},{20,16},{21,17},{22,18},{23,19}} | collective-permute-start | bytes 1572872 | tf_op jit(solution)/shard_map/ppermute | solution.py:633
  48.3 21.4 %collective-permute-start.6 = (bf16[2,64,2048]{2,1,0:T(8,128)(2,1)}, bf16[2,64,2048]{2,1,0:T(8,128)(2,1)}, u32[]{:S(2)}, u32[]{:S(2)}) collective-permute-start(bf16[2,64,2048]{2,1,0:T(8,128)(2,1)} %collective-permute-done.5.rest_1_), channel_id=1, source_target_pairs={{8,12},{9,13},{10,14},{11,15},{24,28},{25,29},{26,30},{27,31}} | collective-permute-start | bytes 1572872 | tf_op jit(solution)/shard_map/ppermute | solution.py:633
  58.2 23.0 %collective-permute-start.17 = (bf16[2,64,2048]{2,1,0:T(8,128)(2,1)}, bf16[2,64,2048]{2,1,0:T(8,128)(2,1)}, u32[]{:S(2)}, u32[]{:S(2)}) collective-permute-start(bf16[2,64,2048]{2,1,0:T(8,128)(2,1)} %collective-permute-done.8.rest_0_), channel_id=1, source_target_pairs={{4,0},{5,1},{6,2},{7,3},{20,16},{21,17},{22,18},{23,19}} | collective-permute-start | bytes 1572872 | tf_op jit(solution)/shard_map/ppermute | solution.py:633
  59.5 21.7 %collective-permute-start.18 = (bf16[2,64,2048]{2,1,0:T(8,128)(2,1)}, bf16[2,64,2048]{2,1,0:T(8,128)(2,1)S(1)}, u32[]{:S(2)}, u32[]{:S(2)}) collective-permute-start(bf16[2,64,2048]{2,1,0:T(8,128)(2,1)} %collective-permute-done.10.rest_1_), channel_id=1, source_target_pairs={{8,12},{9,13},{10,14},{11,15},{24,28},{25,29},{26,30},{27,31}} | collective-permute-start | bytes 1572872 | tf_op jit(solution)/shard_map/ppermute | solution.py:633
  74.9 19.6 %collective-permute-start.11 = (bf16[2,64,2176]{2,1,0:T(8,128)(2,1)}, bf16[2,64,2176]{2,1,0:T(8,128)(2,1)S(1)}, u32[]{:S(2)}, u32[]{:S(2)}) collective-permute-start(bf16[2,64,2176]{2,1,0:T(8,128)(2,1)} %partial_attention.14.mine_hbm.rest_8_), channel_id=1, source_target_pairs={{12,8},{0,4},{13,9},{1,5},{14,10},{2,6},{15,11},{3,7},{28,24},{16,... | collective-permute-start | bytes 1671176 | tf_op jit(solution)/shard_map/ppermute | solution.py:652
  81.2 0.8 copy-start.7
  86.5 27.4 %copy-start.2 = (bf16[2,64,2176]{2,1,0:T(8,128)(2,1)S(1)}, bf16[2,64,2176]{2,1,0:T(8,128)(2,1)}, u32[]{:S(2)}) copy-start(bf16[2,64,2176]{2,1,0:T(8,128)(2,1)} %partial_attention.10.rest_6_.mine_hbm) | copy-start | bytes 1671172
  86.5 24.3 %collective-permute-start.19 = (bf16[2,64,2176]{2,1,0:T(8,128)(2,1)}, bf16[2,64,2176]{2,1,0:T(8,128)(2,1)}, u32[]{:S(2)}, u32[]{:S(2)}) collective-permute-start(bf16[2,64,2176]{2,1,0:T(8,128)(2,1)} %partial_attention.15.mine_hbm), channel_id=1, source_target_pairs={{12,8},{0,4},{13,9},{1,5},{14,10},{2,6},{15,11},{3,7},{28,24},{16,... | collective-permute-start | bytes 1671176 | tf_op jit(solution)/shard_map/ppermute | solution.py:652
  89.4 32.6 %collective-permute-start.14 = (bf16[2,64,2176]{2,1,0:T(8,128)(2,1)}, bf16[2,64,2176]{2,1,0:T(8,128)(2,1)}, u32[]{:S(2)}, u32[]{:S(2)}) collective-permute-start(bf16[2,64,2176]{2,1,0:T(8,128)(2,1)} %partial_attention.12.rest_6_.mine_hbm), channel_id=1, source_target_pairs={{12,8},{0,4},{13,9},{1,5},{14,10},{2,6},{15,11},{3,7},{28,24},{16,... | collective-permute-start | bytes 1671176 | tf_op jit(solution)/shard_map/ppermute | solution.py:652
  94.4 0.8 copy-start.6
  96.8 33.4 %copy-start.1 = (bf16[2,64,2176]{2,1,0:T(8,128)(2,1)S(1)}, bf16[2,64,2176]{2,1,0:T(8,128)(2,1)}, u32[]{:S(2)}) copy-start(bf16[2,64,2176]{2,1,0:T(8,128)(2,1)} %partial_attention.11.rest_6_.mine_hbm) | copy-start | bytes 1671172
  96.8 28.1 %collective-permute-start.12 = (bf16[2,64,2176]{2,1,0:T(8,128)(2,1)}, bf16[2,64,2176]{2,1,0:T(8,128)(2,1)}, u32[]{:S(2)}, u32[]{:S(2)}) collective-permute-start(bf16[2,64,2176]{2,1,0:T(8,128)(2,1)} %merge_pair.6), channel_id=1, source_target_pairs={{8,4},{4,8},{9,5},{5,9},{10,6},{6,10},{11,7},{7,11},{24,20},{20,24... | collective-permute-start | bytes 1671176 | tf_op jit(solution)/shard_map/ppermute | solution.py:652
  98.5 31.8 %collective-permute-start.22 = (bf16[2,64,2176]{2,1,0:T(8,128)(2,1)}, bf16[2,64,2176]{2,1,0:T(8,128)(2,1)}, u32[]{:S(2)}, u32[]{:S(2)}) collective-permute-start(bf16[2,64,2176]{2,1,0:T(8,128)(2,1)} %partial_attention.13.rest_8_.mine_hbm), channel_id=1, source_target_pairs={{12,8},{0,4},{13,9},{1,5},{14,10},{2,6},{15,11},{3,7},{28,24},{16,... | collective-permute-start | bytes 1671176 | tf_op jit(solution)/shard_map/ppermute | solution.py:652
  112.4 29.0 %collective-permute-start.20 = (bf16[2,64,2176]{2,1,0:T(8,128)(2,1)}, bf16[2,64,2176]{2,1,0:T(8,128)(2,1)}, u32[]{:S(2)}, u32[]{:S(2)}) collective-permute-start(bf16[2,64,2176]{2,1,0:T(8,128)(2,1)} %merge_pair.9), channel_id=1, source_target_pairs={{8,4},{4,8},{9,5},{5,9},{10,6},{6,10},{11,7},{7,11},{24,20},{20,24... | collective-permute-start | bytes 1671176 | tf_op jit(solution)/shard_map/ppermute | solution.py:652
  113.9 30.7 %collective-permute-start.16 = (bf16[2,64,2176]{2,1,0:T(8,128)(2,1)S(1)}, bf16[2,64,2176]{2,1,0:T(8,128)(2,1)}, u32[]{:S(2)}, u32[]{:S(2)}) collective-permute-start(bf16[2,64,2176]{2,1,0:T(8,128)(2,1)S(1)} %copy-done.2), channel_id=1, source_target_pairs={{12,8},{0,4},{13,9},{1,5},{14,10},{2,6},{15,11},{3,7},{28,24},{16,... | collective-permute-start | bytes 1671176 | tf_op jit(solution)/shard_map/ppermute | solution.py:652
  123.5 22.4 %collective-permute-start.15 = (bf16[2,64,2176]{2,1,0:T(8,128)(2,1)}, bf16[2,64,2176]{2,1,0:T(8,128)(2,1)}, u32[]{:S(2)}, u32[]{:S(2)}) collective-permute-start(bf16[2,64,2176]{2,1,0:T(8,128)(2,1)} %merge_pair.8), channel_id=1, source_target_pairs={{8,4},{4,8},{9,5},{5,9},{10,6},{6,10},{11,7},{7,11},{24,20},{20,24... | collective-permute-start | bytes 1671176 | tf_op jit(solution)/shard_map/ppermute | solution.py:652
  126.5 19.4 %collective-permute-start.13 = (bf16[2,64,2176]{2,1,0:T(8,128)(2,1)}, bf16[2,64,2176]{2,1,0:T(8,128)(2,1)}, u32[]{:S(2)}, u32[]{:S(2)}) collective-permute-start(bf16[2,64,2176]{2,1,0:T(8,128)(2,1)} %merge_pair.7), channel_id=1, source_target_pairs={{4,0},{8,12},{5,1},{9,13},{6,2},{10,14},{7,3},{11,15},{20,16},{24,... | collective-permute-start | bytes 1671176 | tf_op jit(solution)/shard_map/ppermute | solution.py:652
  130.3 21.4 %collective-permute-start.24 = (bf16[2,64,2176]{2,1,0:T(8,128)(2,1)S(1)}, bf16[2,64,2176]{2,1,0:T(8,128)(2,1)}, u32[]{:S(2)}, u32[]{:S(2)}) collective-permute-start(bf16[2,64,2176]{2,1,0:T(8,128)(2,1)S(1)} %copy-done.1), channel_id=1, source_target_pairs={{12,8},{0,4},{13,9},{1,5},{14,10},{2,6},{15,11},{3,7},{28,24},{16,... | collective-permute-start | bytes 1671176 | tf_op jit(solution)/shard_map/ppermute | solution.py:652
  141.4 10.3 %collective-permute-start.23 = (bf16[2,64,2176]{2,1,0:T(8,128)(2,1)}, bf16[2,64,2176]{2,1,0:T(8,128)(2,1)}, u32[]{:S(2)}, u32[]{:S(2)}) collective-permute-start(bf16[2,64,2176]{2,1,0:T(8,128)(2,1)} %merge_pair.11), channel_id=1, source_target_pairs={{8,4},{4,8},{9,5},{5,9},{10,6},{6,10},{11,7},{7,11},{24,20},{20,24... | collective-permute-start | bytes 1671176 | tf_op jit(solution)/shard_map/ppermute | solution.py:652
  144.6 13.0 %collective-permute-start.21 = (bf16[2,64,2176]{2,1,0:T(8,128)(2,1)}, bf16[2,64,2176]{2,1,0:T(8,128)(2,1)}, u32[]{:S(2)}, u32[]{:S(2)}) collective-permute-start(bf16[2,64,2176]{2,1,0:T(8,128)(2,1)} %merge_pair.10), channel_id=1, source_target_pairs={{4,0},{8,12},{5,1},{9,13},{6,2},{10,14},{7,3},{11,15},{20,16},{24,... | collective-permute-start | bytes 1671176 | tf_op jit(solution)/shard_map/ppermute | solution.py:652
  150.8 13.8 %copy-start.5 = (bf16[2,64,2048]{2,1,0:T(8,128)(2,1)S(1)}, bf16[2,64,2048]{2,1,0:T(8,128)(2,1)}, u32[]{:S(2)}) copy-start(bf16[2,64,2048]{2,1,0:T(8,128)(2,1)} %merge_final.2) | copy-start | bytes 1572868
  150.8 11.7 %collective-permute-start.25 = (bf16[2,64,2048]{2,1,0:T(8,128)(2,1)}, bf16[2,64,2048]{2,1,0:T(8,128)(2,1)}, u32[]{:S(2)}, u32[]{:S(2)}) collective-permute-start(bf16[2,64,2048]{2,1,0:T(8,128)(2,1)} %merge_final.2), channel_id=1, source_target_pairs={{0,1},{1,0},{2,3},{3,2},{4,5},{5,4},{6,7},{7,6},{8,9},{9,8},{10,11... | collective-permute-start | bytes 1572872 | tf_op jit(solution)/shard_map/ppermute | solution.py:665
  162.4 2.2 %collective-permute-start.26 = (bf16[2,64,2048]{2,1,0:T(8,128)(2,1)}, bf16[2,64,2048]{2,1,0:T(8,128)(2,1)S(1)}, u32[]{:S(2)}, u32[]{:S(2)}) collective-permute-start(bf16[2,64,2048]{2,1,0:T(8,128)(2,1)} %merge_final.3), channel_id=1, source_target_pairs={{0,1},{1,0},{2,3},{3,2},{4,5},{5,4},{6,7},{7,6},{8,9},{9,8},{10,11... | collective-permute-start | bytes 1572872 | tf_op jit(solution)/shard_map/ppermute | solution.py:665
where the time goes:
time: 169 us; the launch traced here: 167 us
  starting transfers between devices  74.1 us (44%)
  Pallas kernels  58 us (34%)
  waiting for transfers between devices  19.4 us (11%)
  local copies, waits for them, and re-layouts  11.2 us (7%)
  other arithmetic  4.24 us (3%)
    ppermute x12, starting transfers between devices, queries_travel(): moved[s, l, n] = lax.ppermute(mine, 'seq', pairs)  50 us
    pallas_call x8, Pallas kernels, partial_attention(): pl.pallas_call(body, grid_spec=pltpu.PrefetchScalarGridSpec(num_scalar_pr...  38.9 us
    ppermute x12, starting transfers between devices, queries_travel(): moved[way].append(lax.ppermute(leaving, 'seq', pairs))  23.5 us
    ppermute x12, waiting for transfers between devices, queries_travel(): moved[s, l, n] = lax.ppermute(mine, 'seq', pairs)  12.1 us
    pallas_call x2, Pallas kernels, merge_final(): pl.pallas_call(body, grid_spec=pltpu.PrefetchScalarGridSpec(num_scalar_pr...  9.71 us
    pallas_call x6, Pallas kernels, merge_pair(): pl.pallas_call(body, grid_spec=pltpu.PrefetchScalarGridSpec(num_scalar_pr...  9.4 us
    ppermute x12, waiting for transfers between devices, queries_travel(): moved[way].append(lax.ppermute(leaving, 'seq', pairs))  6.26 us
    unnamed x24, local copies, waits for them, and re-layouts  4.32 us
  transfers between devices with their start and end apart: 27, of which 7 were waited for; matrix products, arithmetic and copies ran while one was open for 3% of the time, Pallas kernels for 35%

commit v1 on v0

--- a/solution.py
+++ b/solution.py
@@ -4,6 +4,7 @@
 from jax.experimental import pallas as pl
 from jax.experimental.pallas import tpu as pltpu
 from jax.sharding import PartitionSpec as P
+
 
 HD = 128
 PAGE = 128
@@ -150,7 +151,7 @@
     query_part = query_width // sub_count
     my_queries = lax.dynamic_slice_in_dim(queries, core_index * query_part, query_part, 2)
     my_fresh = lax.dynamic_slice_in_dim(new_kv, core_index * part_width, part_width, 3)
-    peak, weight_sum, numerator = attend_all(
+    _, weight_sum, numerator = attend_all(
         my_queries,
         my_fresh,
         received,
@@ -230,11 +231,13 @@
     )
 
 
-def work_item(chip, item, shards):
-    if 2 * chip >= shards:
-        return ("right", item, -item) if item <= chip else ("left", item - chip, item - chip)
-    far = shards - 1 - chip
-    return ("left", item, item) if item <= far else ("right", item - far, far - item)
+def one_of(shard, table, value):
+    found = None
+    for chip, entry in enumerate(table):
+        if entry == value:
+            here = shard == chip
+            found = here if found is None else found | here
+    return found
 
 
 def by_chip(shard, values):
@@ -246,9 +249,10 @@
 
 
 def partial_attention(
-    plan, sources, choice, homes, pages, twin_pages, fresh, after, *, first, seq_dev, picks, sub_count
+    plan, sources, choice, homes, pages, twin_pages, fresh, relays, *, count, width, first, seq_dev,
+    picks, sub_count
 ):
-    count, row_count, width = sources[0].shape
+    row_count = sources[0].shape[1]
     part_width = twin_pages.shape[3]
     heads_kv = part_width // HD
     heads = width // HD
@@ -266,7 +270,9 @@
         query_refs = rest[: len(sources)]
         page_refs = rest[len(sources) : len(sources) + refs_per_seq]
         fresh_ref = rest[len(sources) + refs_per_seq] if fresh is not None else None
-        out_ref, query_buf = rest[-2:]
+        query_buf = rest[-1]
+        out_ref = rest[-2 - len(relays)]
+        relay_refs = rest[-1 - len(relays) : -1]
         k = pl.program_id(0)
         shard = plan_ref[0]
         counts = [entry(plan_ref, k, refs_per_seq + n) for n in range(refs_per_seq)]
@@ -276,14 +282,16 @@
         else:
             query_ref = query_buf
             for n in range(len(sources)):
-                chips = [chip for chip, c in enumerate(choice) if c == n]
-                chosen = shard == chips[0]
-                for chip in chips[1:]:
-                    chosen = chosen | (shard == chip)
-
-                @pl.when(chosen)
+                @pl.when(one_of(shard, choice, n))
                 def _(n=n):
                     query_buf[...] = query_refs[n][...]
+
+        for relay, relay_ref in zip(relays, relay_refs):
+            for n in range(len(sources)):
+                if n in relay:
+                    @pl.when(one_of(shard, relay, n))
+                    def _(n=n, relay_ref=relay_ref):
+                        relay_ref[0, :, :width] = query_refs[n][0]
 
         def attend(rows, live_rows):
             lane = lax.broadcasted_iota(jnp.int32, (rows, LANES), 1)
@@ -370,8 +378,16 @@
             if few < row_count:
                 out_ref[0, few:, :] = jnp.zeros((row_count - few, width + LANES), jnp.bfloat16)
 
+        for relay, relay_ref in zip(relays, relay_refs):
+            @pl.when(one_of(shard, relay, -1))
+            def _(relay_ref=relay_ref):
+                relay_ref[...] = out_ref[...]
+
     page_block = (1, 2, PAGE, part_width)
-    in_specs = [pl.BlockSpec((1, row_count, width), lambda k, p: (k, 0, 0)) for _ in sources]
+    if fresh is None:
+        in_specs = [pl.BlockSpec((1, row_count, width), lambda k, p: (k, 0, 0)) for _ in sources]
+    else:
+        in_specs = [pl.BlockSpec((1, row_count, width), lambda k, p: (k, 0, p[1]))]
     operands = list(sources)
     for n in range(picks):
         in_specs.append(
@@ -386,19 +402,18 @@
             pl.BlockSpec((2, 1, row_count, part_width), lambda k, p: (0, k, 0, 0))
         )
         operands.append(fresh)
-    for x in after:
-        in_specs.append(pl.BlockSpec(memory_space=pl.ANY))
-        operands.append(x)
+    message = jax.ShapeDtypeStruct((count, row_count, width + LANES), jnp.bfloat16)
+    outs = 1 + len(relays)
     return pl.pallas_call(
         body,
         grid_spec=pltpu.PrefetchScalarGridSpec(
             num_scalar_prefetch=1,
             grid=(count,),
             in_specs=in_specs,
-            out_specs=pl.BlockSpec((1, row_count, width + LANES), lambda k, p: (k, 0, 0)),
+            out_specs=[pl.BlockSpec((1, row_count, width + LANES), lambda k, p: (k, 0, 0))] * outs,
             scratch_shapes=[pltpu.VMEM((1, row_count, width), jnp.bfloat16)],
         ),
-        out_shape=jax.ShapeDtypeStruct((count, row_count, width + LANES), jnp.bfloat16),
+        out_shape=[message] * outs,
         name="partial_attention",
         cost_estimate=pl.CostEstimate(
             flops=count * heads * row_count * refs_per_seq * PAGE * HD * 4,
@@ -419,28 +434,30 @@
     return [w / total for w in weights], peak + jnp.log2(total)
 
 
-def merge_pair(plan, mine, incoming, *, chips):
-    count, row_count, full = mine.shape
+def merge_pair(plan, mine, incoming, other, *, chips):
+    count, _, full = mine.shape
     width = full - LANES
     heads = width // HD
-
-    def body(plan_ref, mine_hbm, incoming_hbm, out_ref, mine_ref, incoming_ref, sems):
-        here = plan_ref[0] == chips[0]
-        for chip in chips[1:]:
-            here = here | (plan_ref[0] == chip)
+    inputs = [mine, incoming] + ([other] if other is not None else [])
+
+    def body(plan_ref, *rest):
+        hbm = rest[: len(inputs)]
+        out_ref, mine_ref, incoming_ref, sems = rest[len(inputs) :]
+        here = one_of(plan_ref[0], chips, 1)
 
         @pl.when(here)
         def _():
+            parts = [mine_ref, incoming_ref]
             copies = [
-                pltpu.make_async_copy(mine_hbm, mine_ref, sems.at[0]),
-                pltpu.make_async_copy(incoming_hbm, incoming_ref, sems.at[1]),
+                [pltpu.make_async_copy(h.at[k], r.at[k], sems.at[k, n]) for n, (h, r) in enumerate(zip(hbm, parts))]
+                for k in range(count)
             ]
-            for c in copies:
-                c.start()
-            for c in copies:
-                c.wait()
-            parts = [mine_ref, incoming_ref]
+            for pair in copies:
+                for c in pair:
+                    c.start()
             for k in range(count):
+                for c in copies[k]:
+                    c.wait()
                 weights, lse = merge_weights([read_lse(r[k, :, width:], heads) for r in parts])
                 for h in range(heads):
                     cols = slice(h * HD, (h + 1) * HD)
@@ -450,80 +467,67 @@
                     ).astype(jnp.bfloat16)
                 out_ref[k, :, width:] = lse_block(spread_lse(lse, heads), heads)
 
+        if other is not None:
+            @pl.when(jnp.logical_not(here))
+            def _():
+                copy = pltpu.make_async_copy(hbm[2], out_ref, sems.at[0, 0])
+                copy.start()
+                copy.wait()
+
     any_spec = pl.BlockSpec(memory_space=pl.ANY)
     return pl.pallas_call(
         body,
         grid_spec=pltpu.PrefetchScalarGridSpec(
             num_scalar_prefetch=1,
             grid=(1,),
-            in_specs=[any_spec, any_spec],
+            in_specs=[any_spec] * len(inputs),
             out_specs=pl.BlockSpec(mine.shape, lambda g, p: (0, 0, 0)),
             scratch_shapes=[
                 pltpu.VMEM(mine.shape, jnp.bfloat16),
                 pltpu.VMEM(mine.shape, jnp.bfloat16),
-                pltpu.SemaphoreType.DMA((2,)),
+                pltpu.SemaphoreType.DMA((count, 2)),
             ],
         ),
         out_shape=jax.ShapeDtypeStruct(mine.shape, jnp.bfloat16),
         name="merge_pair",
-    )(plan, mine, incoming)
-
-
-def merge_final(plan, own, arrived, *, first, shards, seq_dev, record):
-    count, row_count, full = own.shape
+    )(plan, *inputs)
+
+
+def merge_final(plan, own, last_in, first_in, choice, *, first, seq_dev, record):
+    count, row_count, full = last_in.shape
     width = full - LANES
     heads = width // HD
-    last = shards - 1
-
-    def body(plan_ref, own_ref, *rest):
-        arrived_refs = rest[:last]
-        out_ref, right_buf, left_buf, sems = rest[last:]
+
+    def body(plan_ref, own_hbm, last_hbm, *rest):
+        first_hbm = rest[: len(first_in)]
+        out_ref, own_ref, last_ref, first_ref, sems = rest[len(first_in) :]
         shard = plan_ref[0]
-        for s, r in enumerate(arrived_refs):
-            @pl.when(shard == s)
-            def _(r=r):
-                pltpu.make_async_copy(r, right_buf, sems.at[0]).start()
-
-            @pl.when(shard == last - s)
-            def _(r=r):
-                pltpu.make_async_copy(r, left_buf, sems.at[1]).start()
-
-        @pl.when(shard < shards - 1)
-        def _():
-            pltpu.make_async_copy(arrived_refs[0], right_buf, sems.at[0]).wait()
-
-        @pl.when(shard > 0)
-        def _():
-            pltpu.make_async_copy(arrived_refs[0], left_buf, sems.at[1]).wait()
-
-        def one(k, carry):
-            empty = jnp.full((row_count, LANES), NO_KEY, jnp.float32)
-            right_lse = read_lse(right_buf[k, :, width:], heads)
-            left_lse = read_lse(left_buf[k, :, width:], heads)
-            right_on = shard < shards - 1
-            left_on = shard > 0
-            lses = [
-                read_lse(own_ref[k, :, width:], heads),
-                jnp.where(right_on, right_lse, empty),
-                jnp.where(left_on, left_lse, empty),
-            ]
-            weights, _ = merge_weights(lses)
+        parts = [own_ref, last_ref, first_ref]
+
+        def copy(source, n, k):
+            return pltpu.make_async_copy(source, parts[n].at[k], sems.at[n, k])
+
+        for k in range(count):
+            copy(own_hbm.at[first + k], 0, k).start()
+            copy(last_hbm.at[k], 1, k).start()
+            for n, r in enumerate(first_hbm):
+                @pl.when(one_of(shard, choice, n))
+                def _(r=r, k=k):
+                    copy(r.at[k], 2, k).start()
+        for k in range(count):
+            for n, r in enumerate((own_hbm, last_hbm, first_hbm[0])):
+                copy(r.at[k], n, k).wait()
+            weights, _ = merge_weights([read_lse(r[k, :, width:], heads) for r in parts])
             row = lax.broadcasted_iota(jnp.int32, (row_count, HD), 0)
             flag = plan_ref[2 + (shard * seq_dev + first + k) * record + record - 1]
             live = row < jnp.where(flag == 1, row_count, 1)
             for h in range(heads):
                 cols = slice(h * HD, (h + 1) * HD)
-                total = own_ref[k, :, cols].astype(jnp.float32) * weights[0][:, h : h + 1]
-                total = total + jnp.where(
-                    right_on, right_buf[k, :, cols].astype(jnp.float32), 0.0
-                ) * weights[1][:, h : h + 1]
-                total = total + jnp.where(
-                    left_on, left_buf[k, :, cols].astype(jnp.float32), 0.0
-                ) * weights[2][:, h : h + 1]
+                total = sum(
+                    r[k, :, cols].astype(jnp.float32) * w[:, h : h + 1]
+                    for r, w in zip(parts, weights)
+                )
                 out_ref[k, :, cols] = jnp.where(live, total, 0.0).astype(jnp.bfloat16)
-            return carry
-
-        lax.fori_loop(0, count, one, 0)
 
     any_spec = pl.BlockSpec(memory_space=pl.ANY)
     return pl.pallas_call(
@@ -531,22 +535,86 @@
         grid_spec=pltpu.PrefetchScalarGridSpec(
             num_scalar_prefetch=1,
             grid=(1,),
-            in_specs=[pl.BlockSpec((count, row_count, full), lambda g, p: (0, 0, 0))]
-            + [any_spec] * last,
+            in_specs=[any_spec] * (2 + len(first_in)),
             out_specs=pl.BlockSpec((count, row_count, width), lambda g, p: (0, 0, 0)),
-            scratch_shapes=[
-                pltpu.VMEM(own.shape, jnp.bfloat16),
-                pltpu.VMEM(own.shape, jnp.bfloat16),
-                pltpu.SemaphoreType.DMA((2,)),
-            ],
+            scratch_shapes=[pltpu.VMEM(last_in.shape, jnp.bfloat16)] * 3
+            + [pltpu.SemaphoreType.DMA((3, count))],
         ),
         out_shape=jax.ShapeDtypeStruct((count, row_count, width), jnp.bfloat16),
         name="merge_final",
-    )(plan, own, *arrived)
+    )(plan, own, last_in, *first_in)
 
 
 CHUNKS = 2
 BLOCK_ROWS = 512
+
+
+def own_columns(core_of, queries, parts, chunk):
+    seqs, row_count, full = queries.shape
+    width = full // parts
+
+    def body(core_ref, *refs):
+        count = len(refs) // 2
+        for k in range(count):
+            refs[count + k][...] = refs[k][...]
+
+    pieces = seqs // chunk
+    return pl.pallas_call(
+        body,
+        grid_spec=pltpu.PrefetchScalarGridSpec(
+            num_scalar_prefetch=1,
+            grid=(chunk,),
+            in_specs=[
+                pl.BlockSpec((1, row_count, width), lambda k, c, n=n: (n * chunk + k, 0, c[0]))
+                for n in range(pieces)
+            ],
+            out_specs=[
+                pl.BlockSpec((1, row_count, width), lambda k, c: (k, 0, 0)) for _ in range(pieces)
+            ],
+        ),
+        out_shape=[
+            jax.ShapeDtypeStruct((chunk, row_count, width), queries.dtype) for _ in range(pieces)
+        ],
+        name="own_columns",
+    )(core_of, *([queries] * pieces))
+
+
+def place_columns(core_of, own, other, whole, *, first, seqs):
+    count, row_count, width = own.shape
+
+    def body(core_ref, own_ref, other_ref, *rest):
+        out_ref = rest[-1]
+
+        @pl.when(core_ref[0] == 0)
+        def _():
+            out_ref[:, :, :width] = own_ref[...]
+            out_ref[:, :, width:] = other_ref[...]
+
+        @pl.when(core_ref[0] != 0)
+        def _():
+            out_ref[:, :, :width] = other_ref[...]
+            out_ref[:, :, width:] = own_ref[...]
+
+    block = pl.BlockSpec((1, row_count, width), lambda k, c: (k, 0, 0))
+    operands = [own, other]
+    specs = [block, block]
+    aliases = {}
+    if whole is not None:
+        operands.append(whole)
+        specs.append(pl.BlockSpec(memory_space=pl.ANY))
+        aliases = {3: 0}
+    return pl.pallas_call(
+        body,
+        grid_spec=pltpu.PrefetchScalarGridSpec(
+            num_scalar_prefetch=1,
+            grid=(count,),
+            in_specs=specs,
+            out_specs=pl.BlockSpec((1, row_count, 2 * width), lambda k, c: (first + k, 0, 0)),
+        ),
+        out_shape=jax.ShapeDtypeStruct((seqs, row_count, 2 * width), own.dtype),
+        input_output_aliases=aliases,
+        name="place_columns",
+    )(core_of, *operands)
 
 
 def queries_travel(queries, new_kv, kv_pages, page_table, cached_len, is_prefill):
@@ -555,19 +623,17 @@
     owners = shards * sub_count
     shard = lax.axis_index("seq")
     core = lax.axis_index("sub")
-    seq_dev, row_count, query_width = queries.shape
+    seq_dev = queries.shape[0]
     pages_dev = kv_pages.shape[0]
     part_width = kv_pages.shape[3] // sub_count
-    query_part = query_width // sub_count
     picks = -(-page_table.shape[1] // owners)
     record = 2 * sub_count * picks + 1
     chunk = seq_dev // CHUNKS
     firsts = [n * chunk for n in range(CHUNKS)]
-    last = shards - 1
-
-    my_queries = lax.dynamic_slice_in_dim(queries, core * query_part, query_part, 2)
-    my_queries, later_pages = lax.optimization_barrier((my_queries, kv_pages))
-    own_queries = [my_queries[f : f + chunk] for f in firsts]
+
+    core_of = core.astype(jnp.int32)[None]
+    own_queries = own_columns(core_of, queries, sub_count, chunk)
+    *own_queries, later_pages = lax.optimization_barrier((*own_queries, kv_pages))
     plan = page_plan(
         page_table, cached_len, is_prefill, shard, core, pages_dev, sub_count, picks
     )
@@ -578,108 +644,67 @@
         lax.dynamic_slice_in_dim(new_kv, core * part_width, part_width, 3), (2, 0, 1, 3)
     )
 
-    def partial(n, sources, choice, homes, fresh_part=None, after=()):
+    whole_width = queries.shape[2] // sub_count
+    common = dict(width=whole_width, seq_dev=seq_dev, picks=picks, sub_count=sub_count)
+
+    def attend(n, sources, choice, homes, relays):
         return partial_attention(
-            plan,
-            sources,
-            choice,
-            homes,
-            kv_pages,
-            twin_pages,
-            fresh_part,
-            after,
-            first=firsts[n],
-            seq_dev=seq_dev,
-            picks=picks,
-            sub_count=sub_count,
+            plan, sources, choice, homes, kv_pages, twin_pages, None, relays,
+            count=chunk, first=firsts[n], **common
         )
 
-    own = [
-        partial(
-            n,
-            [own_queries[n]],
-            [0] * shards,
-            list(range(shards)),
-            fresh[:, firsts[n] : firsts[n] + chunk],
+    def move(array, pairs):
+        return lax.ppermute(array, "seq", pairs)
+
+    up = [(0, 1), (1, 2), (2, 3)]
+    down = [(3, 2), (2, 1), (1, 0)]
+    outward = [(2, 3), (1, 0)]
+    inward = [(3, 2), (0, 1)]
+    across = [(1, 2), (2, 1)]
+    ends = [(3, 0), (0, 3)]
+    inner = (0, 1, 1, 0)
+    arrived = {}
+    for n in range(CHUNKS):
+        right1 = move(own_queries[n], up)
+        left1 = move(own_queries[n], down)
+        one, pay_right, pay_left = attend(
+            n, [right1, left1], (1, 1, 0, 0), (1, 2, 1, 2), ((-1, 0, 0, 0), (1, 1, 1, -1))
         )
-        for n in range(CHUNKS)
-    ]
-    hops = {"right": [own_queries], "left": [own_queries]}
-    work = {}
-    previous = tuple(own)
-
-    def attend(item, previous):
-        items = [work_item(chip, item, shards) for chip in range(shards)]
-        kinds = sorted({(way, h) for way, h, _ in items})
-        choice = [kinds.index((way, h)) for way, h, _ in items]
-        homes = [chip + offset for chip, (_, _, offset) in enumerate(items)]
-        for n in range(CHUNKS):
-            work[item, n] = partial(
-                n, [hops[way][h][n] for way, h in kinds], choice, homes, after=previous
+        right2 = move(pay_right, up)
+        left2 = move(pay_left, down)
+        two, pay = attend(n, [right2, left2], (1, 1, 0, 0), (2, 3, 0, 1), ((-1, 1, 0, -1),))
+        third = move(pay, outward + inward)
+        crossed = move(two, across)
+        (three,) = attend(n, [third, left1, right1], (0, 2, 1, 0), (3, 0, 3, 0), ())
+        joined = merge_pair(plan, one, third, three, chips=inner)
+        final = move(joined, across + ends)
+        paired = merge_pair(plan, three, crossed, None, chips=inner)
+        home = move(paired, outward)
+        arrived[n] = (final, [home, right2, left2])
+    (own,) = partial_attention(
+        plan, [queries], (0,) * shards, tuple(range(shards)), kv_pages, twin_pages, fresh, (),
+        count=seq_dev, first=0, **common
+    )
+    outs = []
+    for n in range(CHUNKS):
+        final, firsts_in = arrived[n]
+        outs.append(
+            merge_final(
+                plan, own, final, firsts_in, (0, 1, 2, 0),
+                first=firsts[n], seq_dev=seq_dev, record=record,
             )
-            previous = (work[item, n],)
-        return previous
-
-    for h in range(1, shards):
-        up = [(a, a + 1) for a in range(h - 1, last)]
-        down = [(a, a - 1) for a in range(1, shards - h + 1)]
-        moved = {"right": [], "left": []}
-        for n in range(CHUNKS):
-            for way, pairs in (("right", up), ("left", down)):
-                leaving = hops[way][-1][n]
-                if h > 1:
-                    gate = own[n] if h == 2 else work[h - 2, n]
-                    leaving, _ = lax.optimization_barrier((leaving, gate))
-                moved[way].append(lax.ppermute(leaving, "seq", pairs))
-        for way in hops:
-            hops[way].append(moved[way])
-        previous = attend(h, previous)
-
-    moved = {}
-    waves = sorted(
-        ((last - s) + (last - 1 - l), s, l) for s in range(last) for l in range(s, last)
-    )
-    for _, s, l in waves:
-        sender = l + 1
-        mirror = last - sender
-        way = ("right", sender - s)
-        item = next(w for w in range(1, shards) if work_item(sender, w, shards)[:2] == way)
-        pairs = [(sender, sender - 1), (mirror, mirror + 1)]
-        for n in range(CHUNKS):
-            mine = work[item, n]
-            if sender < last:
-                mine = merge_pair(plan, mine, moved[s, l + 1, n], chips=(sender, mirror))
-            moved[s, l, n] = lax.ppermute(mine, "seq", pairs)
-    outs = [
-        merge_final(
-            plan,
-            own[n],
-            [moved[s, s, n] for s in range(last)],
-            first=firsts[n],
-            shards=shards,
-            seq_dev=seq_dev,
-            record=record,
         )
-        for n in range(CHUNKS)
-    ]
-    swapped = [lax.ppermute(o, "sub", [(0, 1), (1, 0)]) for o in outs]
-    own_half = jnp.concatenate(outs, axis=0)
-    other_half = jnp.concatenate(swapped, axis=0)
-    first_core = core == 0
-    return jnp.concatenate(
-        [jnp.where(first_core, own_half, other_half), jnp.where(first_core, other_half, own_half)],
-        axis=2,
-    )
-
-
-def per_device(queries, new_kv, kv_pages, page_table, cached_len, is_prefill):
-    shards = lax.axis_size("seq")
-    sub_count = lax.axis_size("sub")
-    heads = queries.shape[2] // sub_count // HD
-    spread = page_table.shape[1] >= shards * sub_count and shards % 2 == 0 and sub_count == 2
-    if spread and 3 * heads <= LANES and queries.shape[0] % CHUNKS == 0:
-        return queries_travel(queries, new_kv, kv_pages, page_table, cached_len, is_prefill)
-    return pages_travel(queries, new_kv, kv_pages, page_table, cached_len, is_prefill)
+    whole = None
+    for n in range(CHUNKS):
+        other = lax.ppermute(outs[n], "sub", [(0, 1), (1, 0)])
+        whole = place_columns(core_of, outs[n], other, whole, first=firsts[n], seqs=seq_dev)
+    return whole
+
+
+def can_travel(shards, sub_count, seq_dev, query_width, page_count):
+    heads = query_width // sub_count // HD
+    spread = page_count >= shards * sub_count and shards == 4 and sub_count == 2
+    return spread and 3 * heads <= LANES and seq_dev % CHUNKS == 0
 
 
 def solution(mesh):
@@ -691,10 +716,24 @@
         P("groups"),
         P("groups"),
     )
-    return jax.shard_map(
-        per_device,
-        mesh=mesh,
-        in_specs=placed,
-        out_specs=P(("groups", "seq"), None, "head"),
-        check_vma=False,
-    )
+    shards = mesh.shape["seq"]
+
+    def placed_map(body):
+        return jax.shard_map(
+            body,
+            mesh=mesh,
+            in_specs=placed,
+            out_specs=P(("groups", "seq"), None, "head"),
+            check_vma=False,
+        )
+
+    def run(queries, new_kv, kv_pages, page_table, cached_len, is_prefill):
+        args = (queries, new_kv, kv_pages, page_table, cached_len, is_prefill)
+        seq_dev = queries.shape[0] // (mesh.shape["groups"] * shards)
+        width = queries.shape[2] // mesh.shape["head"]
+        if not can_travel(shards, mesh.shape["sub"], seq_dev, width, page_table.shape[1]):
+            return placed_map(pages_travel)(*args)
+
+        return placed_map(queries_travel)(*args)
+
+    return run

time: 169 us -> 160 us (0.947)
  starting transfers between devices: 74.1 us -> 33.8 us
  waiting for transfers between devices: 19.4 us -> 50.2 us
  local copies, waits for them, and re-layouts: 11.2 us -> 14.4 us
  other arithmetic: 4.24 us -> 1.5 us
    ppermute x26 -> x18, starting transfers between devices: 73.6 us -> 33.3 us  [the longest x16 33.1 us: move(): return lax.ppermute(array, 'seq', pairs)]
    ppermute x26 -> x18, waiting for transfers between devices: 19.4 us -> 50.2 us  [the longest x16 50.2 us: move(): return lax.ppermute(array, 'seq', pairs)]
    pallas_call x0 -> x3, Pallas kernels: none -> 6.15 us  [the longest x2 4.07 us: place_columns(): pl.pallas_call(body, grid_spec=pltpu.PrefetchScalarGridSpec(num_scalar_pr...]
    unnamed x24 -> x39, local copies, waits for them, and re-layouts: 4.32 us -> 10.4 us
    pallas_call x8 -> x7, Pallas kernels: 38.9 us -> 36.6 us  [partial_attention(): pl.pallas_call(body, grid_spec=pltpu.PrefetchScalarGridSpec(num_scalar_pr...]
    pallas_call x2, Pallas kernels: 9.71 us -> 7.79 us  [merge_final(): pl.pallas_call(body, grid_spec=pltpu.PrefetchScalarGridSpec(num_scalar_pr...]
    slice x2 -> x0, local copies, waits for them, and re-layouts: 1.83 us -> none  [the longest x1 1.09 us: queries_travel(): own_queries = [my_queries[f:f + chunk] for f in firsts]]
    pallas_call x6 -> x4, Pallas kernels: 9.4 us -> 8.44 us  [merge_pair(): pl.pallas_call(body, grid_spec=pltpu.PrefetchScalarGridSpec(num_scalar_pr...]
  transfers between devices with their start and end apart: 27 -> 19, of which waited for: 7 -> 9; matrix products, arithmetic and copies ran while one was open for 3% -> 2% of each run, Pallas kernels for 35% -> 34%
where the time goes in v1:
time: 160 us; the launch traced here: 159 us
  Pallas kernels  59 us (37%)
  waiting for transfers between devices  50.2 us (31%)
  starting transfers between devices  33.8 us (21%)
  local copies, waits for them, and re-layouts  14.4 us (9%)
    ppermute x16, waiting for transfers between devices, move(): return lax.ppermute(array, 'seq', pairs)  50.2 us
    pallas_call x7, Pallas kernels, partial_attention(): pl.pallas_call(body, grid_spec=pltpu.PrefetchScalarGridSpec(num_scalar_pr...  36.6 us
    ppermute x16, starting transfers between devices, move(): return lax.ppermute(array, 'seq', pairs)  33.1 us
    unnamed x39, local copies, waits for them, and re-layouts  10.4 us
    pallas_call x4, Pallas kernels, merge_pair(): pl.pallas_call(body, grid_spec=pltpu.PrefetchScalarGridSpec(num_scalar_pr...  8.44 us
    pallas_call x2, Pallas kernels, merge_final(): pl.pallas_call(body, grid_spec=pltpu.PrefetchScalarGridSpec(num_scalar_pr...  7.79 us
    pallas_call x2, Pallas kernels, place_columns(): pl.pallas_call(body, grid_spec=pltpu.PrefetchScalarGridSpec(num_scalar_pr...  4.07 us
    dynamic_slice x1, local copies, waits for them, and re-layouts, queries_travel(): lax.dynamic_slice_in_dim(later_pages, (1 - core) * part_width, part_width...  3.63 us
  transfers between devices with their start and end apart: 19, of which 9 were waited for; matrix products, arithmetic and copies ran while one was open for 2% of the time, Pallas kernels for 34%

profile of v1, /device:TPU:0, one launch (start us, length us, event | category | flops | bytes accessed | tf_op | source)
XLA Modules:
  0.0 159.2 jit_solution(7449284568380212649)
XLA Ops:
  0.0 2.1 %own_columns.1 = (bf16[2,64,2048]{2,1,0:T(8,128)(2,1)}, bf16[2,64,2048]{2,1,0:T(8,128)(2,1)}) custom-call(s32[1]{0:T(128)} %bitcast.core_ref, bf16[4,64,4096]{2,1,0:T(8,128)(2,1)} %rest_0_.1, bf16[4,64,4096]{2,1,0:T(8,128)(2,1)} %rest_0_.1), custom_call_target="tpu_custom_call" | custom-call | tf_op jit(solution)/shard_map/own_columns/pallas_call | solution.py:562
  2.1 3.6 %constant_dynamic-slice_fusion.1 = bf16[21,2,128,256]{3,2,1,0:T(8,128)(2,1)} fusion(bf16[21,2,128,512]{3,2,1,0:T(8,128)(2,1)} %rest_4_.3, s32[]{:T(128)S(6)} %select_n.49), kind=kLoop, calls=%fused_computation.27 | loop fusion | bytes 5505028 | tf_op jit(solution)/shard_map/dynamic_slice | solution.py:641
  5.7 0.5 collective-permute-start
  6.2 5.3 %collective-permute-start.1 = (bf16[2,64,2048]{2,1,0:T(8,128)(2,1)}, bf16[2,64,2048]{2,1,0:T(8,128)(2,1)}, u32[]{:S(2)}, u32[]{:S(2)}) collective-permute-start(bf16[2,64,2048]{2,1,0:T(8,128)(2,1)} %get-tuple-element.23), channel_id=1, source_target_pairs={{0,4},{4,8},{8,12},{1,5},{5,9},{9,13},{2,6},{6,10},{10,14},{3,7},{... | collective-permute-start | bytes 1572872 | tf_op jit(solution)/shard_map/ppermute | solution.py:657
  11.5 1.3 collective-permute-start.2
  12.8 5.4 %collective-permute-start.10 = (bf16[2,64,2048]{2,1,0:T(8,128)(2,1)}, bf16[2,64,2048]{2,1,0:T(8,128)(2,1)}, u32[]{:S(2)}, u32[]{:S(2)}) collective-permute-start(bf16[2,64,2048]{2,1,0:T(8,128)(2,1)} %get-tuple-element.29), channel_id=1, source_target_pairs={{0,4},{4,8},{8,12},{1,5},{5,9},{9,13},{2,6},{6,10},{10,14},{3,7},{... | collective-permute-start | bytes 1572872 | tf_op jit(solution)/shard_map/ppermute | solution.py:657
  18.1 1.3 collective-permute-start.11
  19.5 0.1 fusion.2
  19.6 0.4 convert_reduce_fusion
  20.0 0.1 broadcast_compare_fusion
  20.1 0.2 fusion
  20.3 0.1 copy.11
  20.4 0.1 reshape.86
  20.5 0.7 pad_add_fusion.1.plan_ref
  21.2 12.9 %collective-permute-done.10.rest_0_.rest_2_ = bf16[2,64,2048]{2,1,0:T(8,128)(2,1)} collective-permute-done((bf16[2,64,2048]{2,1,0:T(8,128)(2,1)}, bf16[2,64,2048]{2,1,0:T(8,128)(2,1)}, u32[]{:S(2)}, u32[]{:S(2)}) %collective-permute-start.10) | collective-permute-done | bytes 524320 | tf_op jit(solution)/shard_map/ppermute | solution.py:657
  34.1 4.9 %collective-permute-done.11.rest_1_ = bf16[2,64,2048]{2,1,0:T(8,128)(2,1)} collective-permute-done((bf16[2,64,2048]{2,1,0:T(8,128)(2,1)}, bf16[2,64,2048]{2,1,0:T(8,128)(2,1)}, u32[]{:S(2)}, u32[]{:S(2)}) %collective-permute-start.11) | collective-permute-done | bytes 524320 | tf_op jit(solution)/shard_map/ppermute | solution.py:657
  39.0 1.5 copy-done.1
  40.5 5.3 %partial_attention.11 = (bf16[2,64,2176]{2,1,0:T(8,128)(2,1)}, bf16[2,64,2176]{2,1,0:T(8,128)(2,1)}, bf16[2,64,2176]{2,1,0:T(8,128)(2,1)}) custom-call(s32[146]{0:T(256)} %pad_add_fusion.1.plan_ref, bf16[2,64,2048]{2,1,0:T(8,128)(2,1)} %collective-permute-done.10.rest_0_.rest_2_, bf16[2,64,2048]{2,1,0:T(8,128)(2,1)} %collective-permute-done.11.rest_1_, ...), custom_call_target="tpu_custom_call" | custom-call | flops 536870912 | bytes 2097152 | tf_op jit(solution)/shard_map/partial_attention/pallas_call | solution.py:407
  45.8 2.7 %collective-permute-start.12 = (bf16[2,64,2176]{2,1,0:T(8,128)(2,1)}, bf16[2,64,2176]{2,1,0:T(8,128)(2,1)S(1)}, u32[]{:S(2)}, u32[]{:S(2)}) collective-permute-start(bf16[2,64,2176]{2,1,0:T(8,128)(2,1)} %get-tuple-element.31), channel_id=1, source_target_pairs={{0,4},{4,8},{8,12},{1,5},{5,9},{9,13},{2,6},{6,10},{10,14},{3,7},{... | collective-permute-start | bytes 1671176 | tf_op jit(solution)/shard_map/ppermute | solution.py:657
  48.6 1.3 collective-permute-start.13
  49.9 5.3 %partial_attention.8 = (bf16[2,64,2176]{2,1,0:T(8,128)(2,1)}, bf16[2,64,2176]{2,1,0:T(8,128)(2,1)}, bf16[2,64,2176]{2,1,0:T(8,128)(2,1)}) custom-call(s32[146]{0:T(256)} %pad_add_fusion.1.plan_ref, bf16[2,64,2048]{2,1,0:T(8,128)(2,1)} %collective-permute-done.1.rest_0_.rest_2_, bf16[2,64,2048]{2,1,0:T(8,128)(2,1)} %collective-permute-done.2.rest_1_, ...), custom_call_target="tpu_custom_call" | custom-call | flops 536870912 | bytes 2097152 | tf_op jit(solution)/shard_map/partial_attention/pallas_call | solution.py:407
  55.2 3.8 %collective-permute-start.3 = (bf16[2,64,2176]{2,1,0:T(8,128)(2,1)}, bf16[2,64,2176]{2,1,0:T(8,128)(2,1)S(1)}, u32[]{:S(2)}, u32[]{:S(2)}) collective-permute-start(bf16[2,64,2176]{2,1,0:T(8,128)(2,1)} %get-tuple-element.25), channel_id=1, source_target_pairs={{0,4},{4,8},{8,12},{1,5},{5,9},{9,13},{2,6},{6,10},{10,14},{3,7},{... | collective-permute-start | bytes 1671176 | tf_op jit(solution)/shard_map/ppermute | solution.py:657
  59.0 1.3 collective-permute-start.4
  60.3 1.5 collective-permute-done.12.rest_0_.rest_1_
  61.8 3.9 %collective-permute-done.13.rest_1_.rest_2_ = bf16[2,64,2176]{2,1,0:T(8,128)(2,1)S(1)} collective-permute-done((bf16[2,64,2176]{2,1,0:T(8,128)(2,1)}, bf16[2,64,2176]{2,1,0:T(8,128)(2,1)S(1)}, u32[]{:S(2)}, u32[]{:S(2)}) %collective-permute-start.13) | collective-permute-done | bytes 557088 | tf_op jit(solution)/shard_map/ppermute | solution.py:657
  65.8 0.8 copy-done.4
  66.6 5.2 %partial_attention.12 = (bf16[2,64,2176]{2,1,0:T(8,128)(2,1)}, bf16[2,64,2176]{2,1,0:T(8,128)(2,1)}) custom-call(s32[146]{0:T(256)} %pad_add_fusion.1.plan_ref, bf16[2,64,2176]{2,1,0:T(8,128)(2,1)} %copy-done.2, bf16[2,64,2176]{2,1,0:T(8,128)(2,1)} %copy-done.4, bf16[21,2,128,512]{3,2,1,0:T(8,128)(2,1)} %rest_4_.3, bf16[21,2,128,512]{3,2,1,0:T(8,128)(2,1)} %rest_4_.3, ...), custom_call_target="tpu_custom_call" | custom-call | flops 536870912 | bytes 2097152 | tf_op jit(solution)/shard_map/partial_attention/pallas_call | solution.py:407
  71.8 0.6 collective-permute-start.14
  72.4 0.7 collective-permute-start.16
  73.1 0.7 collective-permute-done.3.rest_0_.rest_1_
  73.8 3.9 %collective-permute-done.4.rest_1_.rest_2_ = bf16[2,64,2176]{2,1,0:T(8,128)(2,1)S(1)} collective-permute-done((bf16[2,64,2176]{2,1,0:T(8,128)(2,1)}, bf16[2,64,2176]{2,1,0:T(8,128)(2,1)S(1)}, u32[]{:S(2)}, u32[]{:S(2)}) %collective-permute-start.4) | collective-permute-done | bytes 557088 | tf_op jit(solution)/shard_map/ppermute | solution.py:657
  77.7 0.8 copy-done.5
  78.6 4.5 %partial_attention.9 = (bf16[2,64,2176]{2,1,0:T(8,128)(2,1)}, bf16[2,64,2176]{2,1,0:T(8,128)(2,1)}) custom-call(s32[146]{0:T(256)} %pad_add_fusion.1.plan_ref, bf16[2,64,2176]{2,1,0:T(8,128)(2,1)} %copy-done.3, bf16[2,64,2176]{2,1,0:T(8,128)(2,1)} %copy-done.5, bf16[21,2,128,512]{3,2,1,0:T(8,128)(2,1)} %rest_4_.3, bf16[21,2,128,512]{3,2,1,0:T(8,128)(2,1)} %rest_4_.3, ...), custom_call_target="tpu_custom_call" | custom-call | flops 536870912 | bytes 2097152 | tf_op jit(solution)/shard_map/partial_attention/pallas_call | solution.py:407
  83.1 1.4 collective-permute-start.5
  84.5 0.7 collective-permute-start.7
  85.2 4.5 %collective-permute-done.14.rest_0_.rest_1_ = bf16[2,64,2176]{2,1,0:T(8,128)(2,1)S(1)} collective-permute-done((bf16[2,64,2176]{2,1,0:T(8,128)(2,1)}, bf16[2,64,2176]{2,1,0:T(8,128)(2,1)S(1)}, u32[]{:S(2)}, u32[]{:S(2)}) %collective-permute-start.14) | collective-permute-done | bytes 557088 | tf_op jit(solution)/shard_map/ppermute | solution.py:657
  89.7 0.8 copy-done.7
  90.5 4.4 %partial_attention.13.rest_2_.rest_0_ = bf16[2,64,2176]{2,1,0:T(8,128)(2,1)} custom-call(s32[146]{0:T(256)} %pad_add_fusion.1.plan_ref, bf16[2,64,2176]{2,1,0:T(8,128)(2,1)} %copy-done.7, bf16[2,64,2048]{2,1,0:T(8,128)(2,1)} %collective-permute-done.11.rest_1_, bf16[2,64,2048]{2,1,0:T(8,128)(2,1)} %collective-permute-done.10.rest_0_.rest_2_, ...), custom_call_target="tpu_custom_call" | custom-call | flops 536870912 | bytes 2097152 | tf_op jit(solution)/shard_map/partial_attention/pallas_call | solution.py:407
  94.9 2.6 %merge_pair.6 = bf16[2,64,2176]{2,1,0:T(8,128)(2,1)} custom-call(s32[146]{0:T(256)} %pad_add_fusion.1.plan_ref, bf16[2,64,2176]{2,1,0:T(8,128)(2,1)} %get-tuple-element.30.rest_0_, bf16[2,64,2176]{2,1,0:T(8,128)(2,1)} %copy-done.7, bf16[2,64,2176]{2,1,0:T(8,128)(2,1)} %partial_attention.13.rest_2_.rest_0_), custom_call_target="tpu_custom_call" | custom-call | tf_op jit(solution)/shard_map/merge_pair/pallas_call | solution.py:478
  97.5 0.3 collective-permute-start.15
  97.8 0.8 copy-done.13
  98.6 1.7 %merge_pair.7 = bf16[2,64,2176]{2,1,0:T(8,128)(2,1)} custom-call(s32[146]{0:T(256)} %pad_add_fusion.1.plan_ref, bf16[2,64,2176]{2,1,0:T(8,128)(2,1)} %partial_attention.13.rest_2_.rest_0_, bf16[2,64,2176]{2,1,0:T(8,128)(2,1)} %copy-done.13), custom_call_target="tpu_custom_call" | custom-call | tf_op jit(solution)/shard_map/merge_pair/pallas_call | solution.py:478
  100.3 1.3 collective-permute-start.17
  101.6 0.8 copy-done.6
  102.4 4.2 %partial_attention.10.rest_2_.rest_0_ = bf16[2,64,2176]{2,1,0:T(8,128)(2,1)} custom-call(s32[146]{0:T(256)} %pad_add_fusion.1.plan_ref, bf16[2,64,2176]{2,1,0:T(8,128)(2,1)} %copy-done.6, bf16[2,64,2048]{2,1,0:T(8,128)(2,1)} %collective-permute-done.2.rest_1_, bf16[2,64,2048]{2,1,0:T(8,128)(2,1)} %collective-permute-done.1.rest_0_.rest_2_, ...), custom_call_target="tpu_custom_call" | custom-call | flops 536870912 | bytes 2097152 | tf_op jit(solution)/shard_map/partial_attention/pallas_call | solution.py:407
  106.6 2.6 %merge_pair.4 = bf16[2,64,2176]{2,1,0:T(8,128)(2,1)} custom-call(s32[146]{0:T(256)} %pad_add_fusion.1.plan_ref, bf16[2,64,2176]{2,1,0:T(8,128)(2,1)} %get-tuple-element.24.rest_0_, bf16[2,64,2176]{2,1,0:T(8,128)(2,1)} %copy-done.6, bf16[2,64,2176]{2,1,0:T(8,128)(2,1)} %partial_attention.10.rest_2_.rest_0_), custom_call_target="tpu_custom_call" | custom-call | tf_op jit(solution)/shard_map/merge_pair/pallas_call | solution.py:478
  109.2 4.6 %collective-permute-start.6 = (bf16[2,64,2176]{2,1,0:T(8,128)(2,1)}, bf16[2,64,2176]{2,1,0:T(8,128)(2,1)S(1)}, u32[]{:S(2)}, u32[]{:S(2)}) collective-permute-start(bf16[2,64,2176]{2,1,0:T(8,128)(2,1)} %merge_pair.4), channel_id=1, source_target_pairs={{4,8},{8,4},{12,0},{0,12},{5,9},{9,5},{13,1},{1,13},{6,10},{10,6},... | collective-permute-start | bytes 1671176 | tf_op jit(solution)/shard_map/ppermute | solution.py:657
  113.8 0.8 copy-done.12
  114.6 1.5 merge_pair.5
  116.2 1.3 collective-permute-start.8
  117.5 0.2 constant_dynamic-slice_fusion
  117.7 0.8 copy.15
  118.4 7.7 %partial_attention.7.own_hbm = bf16[4,64,2176]{2,1,0:T(8,128)(2,1)} custom-call(s32[146]{0:T(256)} %pad_add_fusion.1.plan_ref, bf16[4,64,4096]{2,1,0:T(8,128)(2,1)} %rest_0_.1, bf16[21,2,128,512]{3,2,1,0:T(8,128)(2,1)} %rest_4_.3, bf16[21,2,128,512]{3,2,1,0:T(8,128)(2,1)} %rest_4_.3, bf16[21,2,128,256]{3,2,1,0:T(8,128)(2,1)} %copy-done.1, ...), custom_call_target="tpu_custom_call" | custom-call | flops 1073741824 | bytes 4194304 | tf_op jit(solution)/shard_map/partial_attention/pallas_call | solution.py:407
  126.1 10.7 %collective-permute-done.17.rest_0_ = bf16[2,64,2176]{2,1,0:T(8,128)(2,1)S(1)} collective-permute-done((bf16[2,64,2176]{2,1,0:T(8,128)(2,1)}, bf16[2,64,2176]{2,1,0:T(8,128)(2,1)S(1)}, u32[]{:S(2)}, u32[]{:S(2)}) %collective-permute-start.17) | collective-permute-done | bytes 557088 | tf_op jit(solution)/shard_map/ppermute | solution.py:657
  136.8 0.8 copy-done.10
  137.6 3.9 %merge_final.3.own_ref = bf16[2,64,2048]{2,1,0:T(8,128)(2,1)} custom-call(s32[146]{0:T(256)} %pad_add_fusion.1.plan_ref, bf16[4,64,2176]{2,1,0:T(8,128)(2,1)} %partial_attention.7.own_hbm, bf16[2,64,2176]{2,1,0:T(8,128)(2,1)} %copy-done.8, bf16[2,64,2176]{2,1,0:T(8,128)(2,1)} %copy-done.10, bf16[2,64,2176]{2,1,0:T(8,128)(2,1)} %copy-done.2, ...), custom_call_target="tpu_custom_call" | custom-call | tf_op jit(solution)/shard_map/merge_final/pallas_call | solution.py:533
  141.6 7.0 %collective-permute-done.8.rest_0_ = bf16[2,64,2176]{2,1,0:T(8,128)(2,1)S(1)} collective-permute-done((bf16[2,64,2176]{2,1,0:T(8,128)(2,1)}, bf16[2,64,2176]{2,1,0:T(8,128)(2,1)S(1)}, u32[]{:S(2)}, u32[]{:S(2)}) %collective-permute-start.8) | collective-permute-done | bytes 557088 | tf_op jit(solution)/shard_map/ppermute | solution.py:657
  148.7 0.8 copy-done.11
  149.5 3.9 %merge_final.2.own_ref = bf16[2,64,2048]{2,1,0:T(8,128)(2,1)} custom-call(s32[146]{0:T(256)} %pad_add_fusion.1.plan_ref, bf16[4,64,2176]{2,1,0:T(8,128)(2,1)} %partial_attention.7.own_hbm, bf16[2,64,2176]{2,1,0:T(8,128)(2,1)} %copy-done.9, bf16[2,64,2176]{2,1,0:T(8,128)(2,1)} %copy-done.11, bf16[2,64,2176]{2,1,0:T(8,128)(2,1)} %copy-done.3, ...), custom_call_target="tpu_custom_call" | custom-call | tf_op jit(solution)/shard_map/merge_final/pallas_call | solution.py:533
  153.4 0.1 collective-permute-start.9
  153.5 0.8 copy-done.14
  154.3 2.0 %place_columns.2.rest_0_ = bf16[4,64,4096]{2,1,0:T(8,128)(2,1)} custom-call(s32[1]{0:T(128)} %bitcast.core_ref, bf16[2,64,2048]{2,1,0:T(8,128)(2,1)} %merge_final.3.own_ref, bf16[2,64,2048]{2,1,0:T(8,128)(2,1)} %copy-done.14), custom_call_target="tpu_custom_call" | custom-call | tf_op jit(solution)/shard_map/place_columns/pallas_call | solution.py:606
  156.3 0.8 copy-done.15
  157.1 2.0 %place_columns.3 = bf16[4,64,4096]{2,1,0:T(8,128)(2,1)} custom-call(s32[1]{0:T(128)} %bitcast.core_ref, bf16[2,64,2048]{2,1,0:T(8,128)(2,1)} %merge_final.2.own_ref, bf16[2,64,2048]{2,1,0:T(8,128)(2,1)} %copy-done.15, bf16[4,64,4096]{2,1,0:T(8,128)(2,1)} %place_columns.2.rest_0_), custom_call_target="tpu_custom_call", output_to_operand_aliasing={{}: (3, {})} | custom-call | tf_op jit(solution)/shard_map/place_columns/pallas_call | solution.py:606
  (43 shorter events, 0.2 us)
Async XLA Ops:
  0.0 117.5 %copy-start = (bf16[4,64,2,512]{3,2,1,0:T(2,128)(2,1)S(1)}, bf16[4,64,2,512]{3,2,1,0:T(2,128)(2,1)}, u32[]{:S(2)}) copy-start(bf16[4,64,2,512]{3,2,1,0:T(2,128)(2,1)} %param.7) | copy-start | bytes 1572868
  2.1 17.4 %copy-start.16 = (s32[16,16]{1,0:T(8,128)S(1)}, s32[16,16]{1,0:T(8,128)}, u32[]{:S(2)}) copy-start(s32[16,16]{1,0:T(8,128)} %param.9) | copy-start | bytes 3076
  2.1 17.4 %copy-start.17 = (s32[16]{0:T(128)S(1)}, s32[16]{0:T(128)}, u32[]{:S(2)}) copy-start(s32[16]{0:T(128)} %param.10) | copy-start | bytes 196
  2.1 18.2 %copy-start.18 = (s32[16]{0:T(128)S(1)}, s32[16]{0:T(128)}, u32[]{:S(2)}) copy-start(s32[16]{0:T(128)} %param.11) | copy-start | bytes 196
  5.7 33.3 %collective-permute-start = (bf16[21,2,128,256]{3,2,1,0:T(8,128)(2,1)}, bf16[21,2,128,256]{3,2,1,0:T(8,128)(2,1)S(1)}, u32[]{:S(2)}, u32[]{:S(2)}) collective-permute-start(bf16[21,2,128,256]{3,2,1,0:T(8,128)(2,1)} %constant_dynamic-slice_fusion.1), channel_id=1, source_target_pairs={{0,1},{1,0},{2,3},{3,2},{4,5},{5,4},{6,7},{7,6},{8,9},{9,8},{10,11... | collective-permute-start | bytes 8257544 | tf_op jit(solution)/shard_map/ppermute | solution.py:642
  6.2 43.6 %collective-permute-start.1 = (bf16[2,64,2048]{2,1,0:T(8,128)(2,1)}, bf16[2,64,2048]{2,1,0:T(8,128)(2,1)}, u32[]{:S(2)}, u32[]{:S(2)}) collective-permute-start(bf16[2,64,2048]{2,1,0:T(8,128)(2,1)} %get-tuple-element.23), channel_id=1, source_target_pairs={{0,4},{4,8},{8,12},{1,5},{5,9},{9,13},{2,6},{6,10},{10,14},{3,7},{... | collective-permute-start | bytes 1572872 | tf_op jit(solution)/shard_map/ppermute | solution.py:657
  11.5 38.4 %collective-permute-start.2 = (bf16[2,64,2048]{2,1,0:T(8,128)(2,1)}, bf16[2,64,2048]{2,1,0:T(8,128)(2,1)}, u32[]{:S(2)}, u32[]{:S(2)}) collective-permute-start(bf16[2,64,2048]{2,1,0:T(8,128)(2,1)} %get-tuple-element.23), channel_id=1, source_target_pairs={{12,8},{8,4},{4,0},{13,9},{9,5},{5,1},{14,10},{10,6},{6,2},{15,11}... | collective-permute-start | bytes 1572872 | tf_op jit(solution)/shard_map/ppermute | solution.py:657
  12.8 21.3 %collective-permute-start.10 = (bf16[2,64,2048]{2,1,0:T(8,128)(2,1)}, bf16[2,64,2048]{2,1,0:T(8,128)(2,1)}, u32[]{:S(2)}, u32[]{:S(2)}) collective-permute-start(bf16[2,64,2048]{2,1,0:T(8,128)(2,1)} %get-tuple-element.29), channel_id=1, source_target_pairs={{0,4},{4,8},{8,12},{1,5},{5,9},{9,13},{2,6},{6,10},{10,14},{3,7},{... | collective-permute-start | bytes 1572872 | tf_op jit(solution)/shard_map/ppermute | solution.py:657
  18.1 20.8 %collective-permute-start.11 = (bf16[2,64,2048]{2,1,0:T(8,128)(2,1)}, bf16[2,64,2048]{2,1,0:T(8,128)(2,1)}, u32[]{:S(2)}, u32[]{:S(2)}) collective-permute-start(bf16[2,64,2048]{2,1,0:T(8,128)(2,1)} %get-tuple-element.29), channel_id=1, source_target_pairs={{12,8},{8,4},{4,0},{13,9},{9,5},{5,1},{14,10},{10,6},{6,2},{15,11}... | collective-permute-start | bytes 1572872 | tf_op jit(solution)/shard_map/ppermute | solution.py:657
  39.0 1.5 copy-start.1
  45.8 16.0 %collective-permute-start.12 = (bf16[2,64,2176]{2,1,0:T(8,128)(2,1)}, bf16[2,64,2176]{2,1,0:T(8,128)(2,1)S(1)}, u32[]{:S(2)}, u32[]{:S(2)}) collective-permute-start(bf16[2,64,2176]{2,1,0:T(8,128)(2,1)} %get-tuple-element.31), channel_id=1, source_target_pairs={{0,4},{4,8},{8,12},{1,5},{5,9},{9,13},{2,6},{6,10},{10,14},{3,7},{... | collective-permute-start | bytes 1671176 | tf_op jit(solution)/shard_map/ppermute | solution.py:657
  48.6 17.2 %collective-permute-start.13 = (bf16[2,64,2176]{2,1,0:T(8,128)(2,1)}, bf16[2,64,2176]{2,1,0:T(8,128)(2,1)S(1)}, u32[]{:S(2)}, u32[]{:S(2)}) collective-permute-start(bf16[2,64,2176]{2,1,0:T(8,128)(2,1)} %get-tuple-element.32), channel_id=1, source_target_pairs={{12,8},{8,4},{4,0},{13,9},{9,5},{5,1},{14,10},{10,6},{6,2},{15,11}... | collective-permute-start | bytes 1671176 | tf_op jit(solution)/shard_map/ppermute | solution.py:657
  55.2 18.6 %collective-permute-start.3 = (bf16[2,64,2176]{2,1,0:T(8,128)(2,1)}, bf16[2,64,2176]{2,1,0:T(8,128)(2,1)S(1)}, u32[]{:S(2)}, u32[]{:S(2)}) collective-permute-start(bf16[2,64,2176]{2,1,0:T(8,128)(2,1)} %get-tuple-element.25), channel_id=1, source_target_pairs={{0,4},{4,8},{8,12},{1,5},{5,9},{9,13},{2,6},{6,10},{10,14},{3,7},{... | collective-permute-start | bytes 1671176 | tf_op jit(solution)/shard_map/ppermute | solution.py:657
  59.0 18.7 %collective-permute-start.4 = (bf16[2,64,2176]{2,1,0:T(8,128)(2,1)}, bf16[2,64,2176]{2,1,0:T(8,128)(2,1)S(1)}, u32[]{:S(2)}, u32[]{:S(2)}) collective-permute-start(bf16[2,64,2176]{2,1,0:T(8,128)(2,1)} %get-tuple-element.26), channel_id=1, source_target_pairs={{12,8},{8,4},{4,0},{13,9},{9,5},{5,1},{14,10},{10,6},{6,2},{15,11}... | collective-permute-start | bytes 1671176 | tf_op jit(solution)/shard_map/ppermute | solution.py:657
  61.8 3.9 %copy-start.2 = (bf16[2,64,2176]{2,1,0:T(8,128)(2,1)}, bf16[2,64,2176]{2,1,0:T(8,128)(2,1)S(1)}, u32[]{:S(2)}) copy-start(bf16[2,64,2176]{2,1,0:T(8,128)(2,1)S(1)} %collective-permute-done.12.rest_0_.rest_1_) | copy-start | bytes 1671172
  65.8 0.8 copy-start.4
  71.8 17.9 %collective-permute-start.14 = (bf16[2,64,2176]{2,1,0:T(8,128)(2,1)}, bf16[2,64,2176]{2,1,0:T(8,128)(2,1)S(1)}, u32[]{:S(2)}, u32[]{:S(2)}) collective-permute-start(bf16[2,64,2176]{2,1,0:T(8,128)(2,1)} %get-tuple-element.33), channel_id=1, source_target_pairs={{8,12},{4,0},{12,8},{0,4},{9,13},{5,1},{13,9},{1,5},{10,14},{6,2},... | collective-permute-start | bytes 1671176 | tf_op jit(solution)/shard_map/ppermute | solution.py:657
  72.4 25.4 %collective-permute-start.16 = (bf16[2,64,2176]{2,1,0:T(8,128)(2,1)}, bf16[2,64,2176]{2,1,0:T(8,128)(2,1)S(1)}, u32[]{:S(2)}, u32[]{:S(2)}) collective-permute-start(bf16[2,64,2176]{2,1,0:T(8,128)(2,1)} %get-tuple-element.34), channel_id=1, source_target_pairs={{4,8},{8,4},{5,9},{9,5},{6,10},{10,6},{7,11},{11,7},{20,24},{24,20... | collective-permute-start | bytes 1671176 | tf_op jit(solution)/shard_map/ppermute | solution.py:657
  73.8 3.9 %copy-start.3 = (bf16[2,64,2176]{2,1,0:T(8,128)(2,1)}, bf16[2,64,2176]{2,1,0:T(8,128)(2,1)S(1)}, u32[]{:S(2)}) copy-start(bf16[2,64,2176]{2,1,0:T(8,128)(2,1)S(1)} %collective-permute-done.3.rest_0_.rest_1_) | copy-start | bytes 1671172
  77.7 0.8 copy-start.5
  83.1 18.5 %collective-permute-start.5 = (bf16[2,64,2176]{2,1,0:T(8,128)(2,1)}, bf16[2,64,2176]{2,1,0:T(8,128)(2,1)S(1)}, u32[]{:S(2)}, u32[]{:S(2)}) collective-permute-start(bf16[2,64,2176]{2,1,0:T(8,128)(2,1)} %get-tuple-element.27), channel_id=1, source_target_pairs={{8,12},{4,0},{12,8},{0,4},{9,13},{5,1},{13,9},{1,5},{10,14},{6,2},... | collective-permute-start | bytes 1671176 | tf_op jit(solution)/shard_map/ppermute | solution.py:657
  84.5 29.3 %collective-permute-start.7 = (bf16[2,64,2176]{2,1,0:T(8,128)(2,1)}, bf16[2,64,2176]{2,1,0:T(8,128)(2,1)S(1)}, u32[]{:S(2)}, u32[]{:S(2)}) collective-permute-start(bf16[2,64,2176]{2,1,0:T(8,128)(2,1)} %get-tuple-element.28), channel_id=1, source_target_pairs={{4,8},{8,4},{5,9},{9,5},{6,10},{10,6},{7,11},{11,7},{20,24},{24,20... | collective-permute-start | bytes 1671176 | tf_op jit(solution)/shard_map/ppermute | solution.py:657
  89.7 0.8 copy-start.7
  97.5 28.6 %collective-permute-start.15 = (bf16[2,64,2176]{2,1,0:T(8,128)(2,1)}, bf16[2,64,2176]{2,1,0:T(8,128)(2,1)S(1)}, u32[]{:S(2)}, u32[]{:S(2)}) collective-permute-start(bf16[2,64,2176]{2,1,0:T(8,128)(2,1)} %merge_pair.6), channel_id=1, source_target_pairs={{4,8},{8,4},{12,0},{0,12},{5,9},{9,5},{13,1},{1,13},{6,10},{10,6},... | collective-permute-start | bytes 1671176 | tf_op jit(solution)/shard_map/ppermute | solution.py:657
  97.8 0.8 copy-start.13
  100.3 36.5 %collective-permute-start.17 = (bf16[2,64,2176]{2,1,0:T(8,128)(2,1)}, bf16[2,64,2176]{2,1,0:T(8,128)(2,1)S(1)}, u32[]{:S(2)}, u32[]{:S(2)}) collective-permute-start(bf16[2,64,2176]{2,1,0:T(8,128)(2,1)} %merge_pair.7), channel_id=1, source_target_pairs={{8,12},{4,0},{9,13},{5,1},{10,14},{6,2},{11,15},{7,3},{24,28},{20,... | collective-permute-start | bytes 1671176 | tf_op jit(solution)/shard_map/ppermute | solution.py:657
  101.6 0.8 copy-start.6
  109.2 32.4 %collective-permute-start.6 = (bf16[2,64,2176]{2,1,0:T(8,128)(2,1)}, bf16[2,64,2176]{2,1,0:T(8,128)(2,1)S(1)}, u32[]{:S(2)}, u32[]{:S(2)}) collective-permute-start(bf16[2,64,2176]{2,1,0:T(8,128)(2,1)} %merge_pair.4), channel_id=1, source_target_pairs={{4,8},{8,4},{12,0},{0,12},{5,9},{9,5},{13,1},{1,13},{6,10},{10,6},... | collective-permute-start | bytes 1671176 | tf_op jit(solution)/shard_map/ppermute | solution.py:657
  113.8 0.8 copy-start.12
  116.2 32.5 %collective-permute-start.8 = (bf16[2,64,2176]{2,1,0:T(8,128)(2,1)}, bf16[2,64,2176]{2,1,0:T(8,128)(2,1)S(1)}, u32[]{:S(2)}, u32[]{:S(2)}) collective-permute-start(bf16[2,64,2176]{2,1,0:T(8,128)(2,1)} %merge_pair.5), channel_id=1, source_target_pairs={{8,12},{4,0},{9,13},{5,1},{10,14},{6,2},{11,15},{7,3},{24,28},{20,... | collective-permute-start | bytes 1671176 | tf_op jit(solution)/shard_map/ppermute | solution.py:657
  126.1 10.7 %copy-start.8 = (bf16[2,64,2176]{2,1,0:T(8,128)(2,1)}, bf16[2,64,2176]{2,1,0:T(8,128)(2,1)S(1)}, u32[]{:S(2)}) copy-start(bf16[2,64,2176]{2,1,0:T(8,128)(2,1)S(1)} %collective-permute-done.15.last_hbm) | copy-start | bytes 1671172
  136.8 0.8 copy-start.10
  141.5 12.0 %collective-permute-start.18 = (bf16[2,64,2048]{2,1,0:T(8,128)(2,1)}, bf16[2,64,2048]{2,1,0:T(8,128)(2,1)S(1)}, u32[]{:S(2)}, u32[]{:S(2)}) collective-permute-start(bf16[2,64,2048]{2,1,0:T(8,128)(2,1)} %merge_final.3.own_ref), channel_id=1, source_target_pairs={{0,1},{1,0},{2,3},{3,2},{4,5},{5,4},{6,7},{7,6},{8,9},{9,8},{10,11... | collective-permute-start | bytes 1572872 | tf_op jit(solution)/shard_map/ppermute | solution.py:699
  141.6 7.1 %copy-start.9 = (bf16[2,64,2176]{2,1,0:T(8,128)(2,1)}, bf16[2,64,2176]{2,1,0:T(8,128)(2,1)S(1)}, u32[]{:S(2)}) copy-start(bf16[2,64,2176]{2,1,0:T(8,128)(2,1)S(1)} %collective-permute-done.6.last_hbm) | copy-start | bytes 1671172
  148.7 0.8 copy-start.11
  153.4 2.9 %collective-permute-start.9 = (bf16[2,64,2048]{2,1,0:T(8,128)(2,1)}, bf16[2,64,2048]{2,1,0:T(8,128)(2,1)S(1)}, u32[]{:S(2)}, u32[]{:S(2)}) collective-permute-start(bf16[2,64,2048]{2,1,0:T(8,128)(2,1)} %merge_final.2.own_ref), channel_id=1, source_target_pairs={{0,1},{1,0},{2,3},{3,2},{4,5},{5,4},{6,7},{7,6},{8,9},{9,8},{10,11... | collective-permute-start | bytes 1572872 | tf_op jit(solution)/shard_map/ppermute | solution.py:699
  153.5 0.8 copy-start.14
  156.3 0.8 copy-start.15

commit v2 on v1

--- a/solution.py
+++ b/solution.py
@@ -266,34 +266,72 @@
         home = by_chip(plan_ref[0], homes)
         return plan_ref[2 + (home * seq_dev + first + k) * record + column]
 
+    chunk = sources[0].shape[0]
+
     def body(plan_ref, *rest):
         query_refs = rest[: len(sources)]
-        page_refs = rest[len(sources) : len(sources) + refs_per_seq]
-        fresh_ref = rest[len(sources) + refs_per_seq] if fresh is not None else None
-        query_buf = rest[-1]
-        out_ref = rest[-2 - len(relays)]
-        relay_refs = rest[-1 - len(relays) : -1]
-        k = pl.program_id(0)
+        pages_hbm, twin_hbm = rest[len(sources) : len(sources) + 2]
+        fresh_ref = rest[len(sources) + 2] if fresh is not None else None
+        query_ref, page_buf, sems = rest[-3:]
+        out_ref = rest[-4 - len(relays)]
+        relay_refs = rest[-3 - len(relays) : -3]
         shard = plan_ref[0]
-        counts = [entry(plan_ref, k, refs_per_seq + n) for n in range(refs_per_seq)]
-        flag = entry(plan_ref, k, 2 * refs_per_seq)
-        if len(sources) == 1:
-            query_ref = query_refs[0]
-        else:
-            query_ref = query_buf
+        mine = pl.ds(pl.multiple_of(plan_ref[1] * part_width, LANES), part_width)
+
+        def page_copy(k, n):
+            slot = entry(plan_ref, k, n)
+            source = pages_hbm.at[slot, :, :, mine] if n < picks else twin_hbm.at[slot]
+            return pltpu.make_async_copy(source, page_buf.at[k, n], sems.at[k, n])
+
+        for k in range(count):
+            for n in range(refs_per_seq):
+                page_copy(k, n).start()
+
+        def one(k, carry):
+            attend_one(k)
+            return carry
+
+        def attend_one(k):
+            counts = [entry(plan_ref, k, refs_per_seq + n) for n in range(refs_per_seq)]
+            flag = entry(plan_ref, k, 2 * refs_per_seq)
             for n in range(len(sources)):
-                @pl.when(one_of(shard, choice, n))
+                if fresh is not None:
+                    chosen = k // chunk == n
+                else:
+                    chosen = one_of(shard, choice, n)
+
+                @pl.when(chosen)
                 def _(n=n):
-                    query_buf[...] = query_refs[n][...]
-
-        for relay, relay_ref in zip(relays, relay_refs):
-            for n in range(len(sources)):
-                if n in relay:
-                    @pl.when(one_of(shard, relay, n))
-                    def _(n=n, relay_ref=relay_ref):
-                        relay_ref[0, :, :width] = query_refs[n][0]
-
-        def attend(rows, live_rows):
+                    query_ref[...] = query_refs[n][k % chunk, :, :width]
+
+            for relay, relay_ref in zip(relays, relay_refs):
+                for n in range(len(sources)):
+                    if n in relay:
+                        @pl.when(one_of(shard, relay, n))
+                        def _(n=n, relay_ref=relay_ref):
+                            relay_ref[k, :, :width] = query_refs[n][k, :, :width]
+
+            for n in range(refs_per_seq):
+                page_copy(k, n).wait()
+
+            @pl.when(flag == 1)
+            def _():
+                attend(k, counts, row_count, row_count)
+
+            @pl.when(flag != 1)
+            def _():
+                attend(k, counts, few, 1)
+                if few < row_count:
+                    out_ref[k, few:, :] = jnp.zeros(
+                        (row_count - few, width + LANES), jnp.bfloat16
+                    )
+
+            for relay, relay_ref in zip(relays, relay_refs):
+                @pl.when(one_of(shard, relay, -1))
+                def _(relay_ref=relay_ref):
+                    relay_ref[k] = out_ref[k]
+
+        def attend(k, counts, rows, live_rows):
             lane = lax.broadcasted_iota(jnp.int32, (rows, LANES), 1)
             tile = jnp.zeros((rows, LANES), jnp.float32)
             per_block = max(1, min(group, BLOCK_ROWS // rows))
@@ -301,13 +339,13 @@
             key_lane = lax.broadcasted_iota(jnp.int32, (stacked, PAGE), 1)
             for h in range(heads_kv):
                 cols = slice(h * HD, (h + 1) * HD)
-                keys = jnp.concatenate([r[0, 0, :, cols] for r in page_refs], axis=0)
-                values = jnp.concatenate([r[0, 1, :, cols] for r in page_refs], axis=0)
+                keys = jnp.concatenate([page_buf[k, n, 0, :, cols] for n in range(refs_per_seq)], axis=0)
+                values = jnp.concatenate([page_buf[k, n, 1, :, cols] for n in range(refs_per_seq)], axis=0)
                 for g0 in range(0, group, per_block):
                     base = h * group + g0
                     q = jnp.concatenate(
                         [
-                            query_ref[0, :rows, (base + g) * HD : (base + g + 1) * HD]
+                            query_ref[:rows, (base + g) * HD : (base + g + 1) * HD]
                             for g in range(per_block)
                         ],
                         axis=0,
@@ -328,7 +366,7 @@
                     if fresh is not None:
                         s = lax.dot_general(
                             q,
-                            fresh_ref[0, 0, :, cols],
+                            fresh_ref[0, k, :, cols],
                             (((1,), (1,)), ((), ())),
                             preferred_element_type=jnp.float32,
                         )
@@ -354,7 +392,7 @@
                         weight_sum = weight_sum + jnp.sum(w, axis=1, keepdims=True)
                         numerator = numerator + lax.dot_general(
                             w.astype(jnp.bfloat16),
-                            fresh_ref[1, 0, :, cols],
+                            fresh_ref[1, k, :, cols],
                             (((1,), (0,)), ((), ())),
                             preferred_element_type=jnp.float32,
                         )
@@ -363,64 +401,47 @@
                     for g in range(per_block):
                         head = base + g
                         part = slice(g * rows, (g + 1) * rows)
-                        out_ref[0, :rows, head * HD : (head + 1) * HD] = attended[part]
-                        mine = (lane == head) | (lane == head + heads) | (lane == head + 2 * heads)
-                        tile = jnp.where(mine, lse[part], tile)
-            out_ref[0, :rows, width:] = lse_block(tile, heads)
-
-        @pl.when(flag == 1)
-        def _():
-            attend(row_count, row_count)
-
-        @pl.when(flag != 1)
-        def _():
-            attend(few, 1)
-            if few < row_count:
-                out_ref[0, few:, :] = jnp.zeros((row_count - few, width + LANES), jnp.bfloat16)
-
-        for relay, relay_ref in zip(relays, relay_refs):
-            @pl.when(one_of(shard, relay, -1))
-            def _(relay_ref=relay_ref):
-                relay_ref[...] = out_ref[...]
-
-    page_block = (1, 2, PAGE, part_width)
-    if fresh is None:
-        in_specs = [pl.BlockSpec((1, row_count, width), lambda k, p: (k, 0, 0)) for _ in sources]
-    else:
-        in_specs = [pl.BlockSpec((1, row_count, width), lambda k, p: (k, 0, p[1]))]
-    operands = list(sources)
-    for n in range(picks):
-        in_specs.append(
-            pl.BlockSpec(page_block, lambda k, p, n=n: (entry(p, k, n), 0, 0, p[1]))
-        )
-        operands.append(pages)
-    for n in range(picks, refs_per_seq):
-        in_specs.append(pl.BlockSpec(page_block, lambda k, p, n=n: (entry(p, k, n), 0, 0, 0)))
-        operands.append(twin_pages)
+                        out_ref[k, :rows, head * HD : (head + 1) * HD] = attended[part]
+                        spots = (lane == head) | (lane == head + heads) | (lane == head + 2 * heads)
+                        tile = jnp.where(spots, lse[part], tile)
+            out_ref[k, :rows, width:] = lse_block(tile, heads)
+
+        lax.fori_loop(0, count, one, 0)
+
+    vmem = pl.BlockSpec(memory_space=pltpu.VMEM)
+    hbm = pl.BlockSpec(memory_space=pltpu.HBM)
+    operands = [in_vmem(x) for x in sources] + [in_hbm(pages), in_hbm(twin_pages)]
+    in_specs = [vmem] * len(sources) + [hbm, hbm]
     if fresh is not None:
-        in_specs.append(
-            pl.BlockSpec((2, 1, row_count, part_width), lambda k, p: (0, k, 0, 0))
-        )
         operands.append(fresh)
-    message = jax.ShapeDtypeStruct((count, row_count, width + LANES), jnp.bfloat16)
+        in_specs.append(vmem)
     outs = 1 + len(relays)
     return pl.pallas_call(
         body,
-        grid_spec=pltpu.PrefetchScalarGridSpec(
-            num_scalar_prefetch=1,
-            grid=(count,),
-            in_specs=in_specs,
-            out_specs=[pl.BlockSpec((1, row_count, width + LANES), lambda k, p: (k, 0, 0))] * outs,
-            scratch_shapes=[pltpu.VMEM((1, row_count, width), jnp.bfloat16)],
-        ),
-        out_shape=[message] * outs,
+        in_specs=[pl.BlockSpec(memory_space=pltpu.SMEM)] + in_specs,
+        out_specs=[vmem] * outs,
+        out_shape=[pltpu.VMEM((count, row_count, width + LANES), jnp.bfloat16)] * outs,
+        scratch_shapes=[
+            pltpu.VMEM((row_count, width), jnp.bfloat16),
+            pltpu.VMEM((count, refs_per_seq, 2, PAGE, part_width), jnp.bfloat16),
+            pltpu.SemaphoreType.DMA((count, refs_per_seq)),
+        ],
         name="partial_attention",
+        compiler_params=pltpu.CompilerParams(vmem_limit_bytes=24 << 20),
         cost_estimate=pl.CostEstimate(
             flops=count * heads * row_count * refs_per_seq * PAGE * HD * 4,
             bytes_accessed=count * row_count * width * 8,
             transcendentals=count * heads * row_count * refs_per_seq * PAGE,
         ),
     )(plan, *operands)
+
+
+def in_hbm(array):
+    return pltpu.with_memory_space_constraint(array, pltpu.HBM)
+
+
+def in_vmem(array):
+    return pltpu.with_memory_space_constraint(array, pltpu.VMEM)
 
 
 def merge_weights(lses):
@@ -441,23 +462,13 @@
     inputs = [mine, incoming] + ([other] if other is not None else [])
 
     def body(plan_ref, *rest):
-        hbm = rest[: len(inputs)]
-        out_ref, mine_ref, incoming_ref, sems = rest[len(inputs) :]
+        out_ref = rest[len(inputs)]
         here = one_of(plan_ref[0], chips, 1)
 
         @pl.when(here)
         def _():
-            parts = [mine_ref, incoming_ref]
-            copies = [
-                [pltpu.make_async_copy(h.at[k], r.at[k], sems.at[k, n]) for n, (h, r) in enumerate(zip(hbm, parts))]
-                for k in range(count)
-            ]
-            for pair in copies:
-                for c in pair:
-                    c.start()
+            parts = rest[:2]
             for k in range(count):
-                for c in copies[k]:
-                    c.wait()
                 weights, lse = merge_weights([read_lse(r[k, :, width:], heads) for r in parts])
                 for h in range(heads):
                     cols = slice(h * HD, (h + 1) * HD)
@@ -470,27 +481,17 @@
         if other is not None:
             @pl.when(jnp.logical_not(here))
             def _():
-                copy = pltpu.make_async_copy(hbm[2], out_ref, sems.at[0, 0])
-                copy.start()
-                copy.wait()
-
-    any_spec = pl.BlockSpec(memory_space=pl.ANY)
+                out_ref[...] = rest[2][...]
+
+    vmem = pl.BlockSpec(memory_space=pltpu.VMEM)
     return pl.pallas_call(
         body,
-        grid_spec=pltpu.PrefetchScalarGridSpec(
-            num_scalar_prefetch=1,
-            grid=(1,),
-            in_specs=[any_spec] * len(inputs),
-            out_specs=pl.BlockSpec(mine.shape, lambda g, p: (0, 0, 0)),
-            scratch_shapes=[
-                pltpu.VMEM(mine.shape, jnp.bfloat16),
-                pltpu.VMEM(mine.shape, jnp.bfloat16),
-                pltpu.SemaphoreType.DMA((count, 2)),
-            ],
-        ),
-        out_shape=jax.ShapeDtypeStruct(mine.shape, jnp.bfloat16),
+        in_specs=[pl.BlockSpec(memory_space=pltpu.SMEM)] + [vmem] * len(inputs),
+        out_specs=vmem,
+        out_shape=pltpu.VMEM(mine.shape, jnp.bfloat16),
         name="merge_pair",
-    )(plan, *inputs)
+        compiler_params=pltpu.CompilerParams(vmem_limit_bytes=16 << 20),
+    )(plan, *[in_vmem(x) for x in inputs])
 
 
 def merge_final(plan, own, last_in, first_in, choice, *, first, seq_dev, record):
@@ -498,106 +499,90 @@
     width = full - LANES
     heads = width // HD
 
-    def body(plan_ref, own_hbm, last_hbm, *rest):
-        first_hbm = rest[: len(first_in)]
-        out_ref, own_ref, last_ref, first_ref, sems = rest[len(first_in) :]
+    def body(plan_ref, own_ref, last_ref, *rest):
+        first_refs = rest[: len(first_in)]
+        out_ref = rest[len(first_in)]
         shard = plan_ref[0]
-        parts = [own_ref, last_ref, first_ref]
-
-        def copy(source, n, k):
-            return pltpu.make_async_copy(source, parts[n].at[k], sems.at[n, k])
-
-        for k in range(count):
-            copy(own_hbm.at[first + k], 0, k).start()
-            copy(last_hbm.at[k], 1, k).start()
-            for n, r in enumerate(first_hbm):
-                @pl.when(one_of(shard, choice, n))
-                def _(r=r, k=k):
-                    copy(r.at[k], 2, k).start()
-        for k in range(count):
-            for n, r in enumerate((own_hbm, last_hbm, first_hbm[0])):
-                copy(r.at[k], n, k).wait()
-            weights, _ = merge_weights([read_lse(r[k, :, width:], heads) for r in parts])
-            row = lax.broadcasted_iota(jnp.int32, (row_count, HD), 0)
-            flag = plan_ref[2 + (shard * seq_dev + first + k) * record + record - 1]
-            live = row < jnp.where(flag == 1, row_count, 1)
-            for h in range(heads):
-                cols = slice(h * HD, (h + 1) * HD)
-                total = sum(
-                    r[k, :, cols].astype(jnp.float32) * w[:, h : h + 1]
-                    for r, w in zip(parts, weights)
-                )
-                out_ref[k, :, cols] = jnp.where(live, total, 0.0).astype(jnp.bfloat16)
-
-    any_spec = pl.BlockSpec(memory_space=pl.ANY)
+
+        def finish(first_ref):
+            for k in range(count):
+                parts = [own_ref.at[first + k], last_ref.at[k], first_ref.at[k]]
+                weights, _ = merge_weights([read_lse(r[:, width:], heads) for r in parts])
+                row = lax.broadcasted_iota(jnp.int32, (row_count, HD), 0)
+                flag = plan_ref[2 + (shard * seq_dev + first + k) * record + record - 1]
+                live = row < jnp.where(flag == 1, row_count, 1)
+                for h in range(heads):
+                    cols = slice(h * HD, (h + 1) * HD)
+                    total = sum(
+                        r[:, cols].astype(jnp.float32) * w[:, h : h + 1]
+                        for r, w in zip(parts, weights)
+                    )
+                    out_ref[k, :, cols] = jnp.where(live, total, 0.0).astype(jnp.bfloat16)
+
+        for n, r in enumerate(first_refs):
+            @pl.when(one_of(shard, choice, n))
+            def _(r=r):
+                finish(r)
+
+    vmem = pl.BlockSpec(memory_space=pltpu.VMEM)
+    operands = [own, last_in, *first_in]
     return pl.pallas_call(
         body,
-        grid_spec=pltpu.PrefetchScalarGridSpec(
-            num_scalar_prefetch=1,
-            grid=(1,),
-            in_specs=[any_spec] * (2 + len(first_in)),
-            out_specs=pl.BlockSpec((count, row_count, width), lambda g, p: (0, 0, 0)),
-            scratch_shapes=[pltpu.VMEM(last_in.shape, jnp.bfloat16)] * 3
-            + [pltpu.SemaphoreType.DMA((3, count))],
-        ),
-        out_shape=jax.ShapeDtypeStruct((count, row_count, width), jnp.bfloat16),
+        in_specs=[pl.BlockSpec(memory_space=pltpu.SMEM)] + [vmem] * len(operands),
+        out_specs=vmem,
+        out_shape=pltpu.VMEM((count, row_count, width), jnp.bfloat16),
         name="merge_final",
-    )(plan, own, last_in, *first_in)
+        compiler_params=pltpu.CompilerParams(vmem_limit_bytes=16 << 20),
+    )(plan, *[in_vmem(x) for x in operands])
 
 
 CHUNKS = 2
 BLOCK_ROWS = 512
 
 
-def own_columns(core_of, queries, parts, chunk):
-    seqs, row_count, full = queries.shape
+def own_columns(core_of, queries, parts, first, count):
+    _, row_count, full = queries.shape
     width = full // parts
 
-    def body(core_ref, *refs):
-        count = len(refs) // 2
-        for k in range(count):
-            refs[count + k][...] = refs[k][...]
-
-    pieces = seqs // chunk
+    def body(core_ref, source, out_ref, sem):
+        cols = pl.ds(pl.multiple_of(core_ref[0] * width, LANES), width)
+        copy = pltpu.make_async_copy(source.at[first : first + count, :, cols], out_ref, sem)
+        copy.start()
+        copy.wait()
+
     return pl.pallas_call(
         body,
-        grid_spec=pltpu.PrefetchScalarGridSpec(
-            num_scalar_prefetch=1,
-            grid=(chunk,),
-            in_specs=[
-                pl.BlockSpec((1, row_count, width), lambda k, c, n=n: (n * chunk + k, 0, c[0]))
-                for n in range(pieces)
-            ],
-            out_specs=[
-                pl.BlockSpec((1, row_count, width), lambda k, c: (k, 0, 0)) for _ in range(pieces)
-            ],
-        ),
-        out_shape=[
-            jax.ShapeDtypeStruct((chunk, row_count, width), queries.dtype) for _ in range(pieces)
+        in_specs=[
+            pl.BlockSpec(memory_space=pltpu.SMEM),
+            pl.BlockSpec(memory_space=pltpu.HBM),
         ],
+        out_specs=pl.BlockSpec(memory_space=pltpu.VMEM),
+        out_shape=pltpu.VMEM((count, row_count, width), queries.dtype),
+        scratch_shapes=[pltpu.SemaphoreType.DMA],
         name="own_columns",
-    )(core_of, *([queries] * pieces))
+        compiler_params=pltpu.CompilerParams(vmem_limit_bytes=16 << 20),
+    )(core_of, in_hbm(queries))
 
 
 def place_columns(core_of, own, other, whole, *, first, seqs):
     count, row_count, width = own.shape
 
     def body(core_ref, own_ref, other_ref, *rest):
-        out_ref = rest[-1]
-
-        @pl.when(core_ref[0] == 0)
-        def _():
-            out_ref[:, :, :width] = own_ref[...]
-            out_ref[:, :, width:] = other_ref[...]
-
-        @pl.when(core_ref[0] != 0)
-        def _():
-            out_ref[:, :, :width] = other_ref[...]
-            out_ref[:, :, width:] = own_ref[...]
-
-    block = pl.BlockSpec((1, row_count, width), lambda k, c: (k, 0, 0))
-    operands = [own, other]
-    specs = [block, block]
+        out_ref, sems = rest[-2:]
+        copies = []
+        for n, r in enumerate((own_ref, other_ref)):
+            core = core_ref[0] if n == 0 else 1 - core_ref[0]
+            cols = pl.ds(pl.multiple_of(core * width, LANES), width)
+            target = out_ref.at[first : first + count, :, cols]
+            copies.append(pltpu.make_async_copy(r, target, sems.at[n]))
+        for c in copies:
+            c.start()
+        for c in copies:
+            c.wait()
+
+    vmem = pl.BlockSpec(memory_space=pltpu.VMEM)
+    operands = [in_vmem(own), in_vmem(other)]
+    specs = [vmem, vmem]
     aliases = {}
     if whole is not None:
         operands.append(whole)
@@ -605,15 +590,13 @@
         aliases = {3: 0}
     return pl.pallas_call(
         body,
-        grid_spec=pltpu.PrefetchScalarGridSpec(
-            num_scalar_prefetch=1,
-            grid=(count,),
-            in_specs=specs,
-            out_specs=pl.BlockSpec((1, row_count, 2 * width), lambda k, c: (first + k, 0, 0)),
-        ),
+        in_specs=[pl.BlockSpec(memory_space=pltpu.SMEM)] + specs,
+        out_specs=pl.BlockSpec(memory_space=pl.ANY),
         out_shape=jax.ShapeDtypeStruct((seqs, row_count, 2 * width), own.dtype),
+        scratch_shapes=[pltpu.SemaphoreType.DMA((2,))],
         input_output_aliases=aliases,
         name="place_columns",
+        compiler_params=pltpu.CompilerParams(vmem_limit_bytes=16 << 20),
     )(core_of, *operands)
 
 
@@ -632,8 +615,10 @@
     firsts = [n * chunk for n in range(CHUNKS)]
 
     core_of = core.astype(jnp.int32)[None]
-    own_queries = own_columns(core_of, queries, sub_count, chunk)
-    *own_queries, later_pages = lax.optimization_barrier((*own_queries, kv_pages))
+    own_queries = []
+    for n in range(CHUNKS):
+        own_queries.append(own_columns(core_of, queries, sub_count, firsts[n], chunk))
+    _, later_pages = lax.optimization_barrier((own_queries[-1], kv_pages))
     plan = page_plan(
         page_table, cached_len, is_prefill, shard, core, pages_dev, sub_count, picks
     )
@@ -682,7 +667,7 @@
         home = move(paired, outward)
         arrived[n] = (final, [home, right2, left2])
     (own,) = partial_attention(
-        plan, [queries], (0,) * shards, tuple(range(shards)), kv_pages, twin_pages, fresh, (),
+        plan, own_queries, (0,) * shards, tuple(range(shards)), kv_pages, twin_pages, fresh, (),
         count=seq_dev, first=0, **common
     )
     outs = []

time: 160 us -> 151 us (0.944)
  waiting for transfers between devices: 50.2 us -> 70.1 us
  Pallas kernels: 59 us -> 44.8 us
  local copies, waits for them, and re-layouts: 14.4 us -> 5.11 us
  starting transfers between devices: 33.8 us -> 28.7 us
    ppermute x16, waiting for transfers between devices: 50.2 us -> 69.2 us  [move(): return lax.ppermute(array, 'seq', pairs)]
    pallas_call x16 -> x17, Pallas kernels: 59 us -> 44.8 us  [the longest x7 29.3 us: partial_attention(): pl.pallas_call(body, in_specs=[pl.BlockSpec(memory_space=pltpu.SMEM)] + i...]
    unnamed x39 -> x25, local copies, waits for them, and re-layouts: 10.4 us -> 1.12 us
    ppermute x16, starting transfers between devices: 33.1 us -> 28 us  [move(): return lax.ppermute(array, 'seq', pairs)]
  transfers between devices with their start and end apart: 19 -> 19, of which waited for: 9 -> 11; matrix products, arithmetic and copies ran while one was open for 2% -> 1% of each run, Pallas kernels for 34% -> 28%
where the time goes in v2:
time: 151 us; the launch traced here: 150 us
  waiting for transfers between devices  70.1 us (46%)
  Pallas kernels  44.8 us (30%)
  starting transfers between devices  28.7 us (19%)
  local copies, waits for them, and re-layouts  5.11 us (3%)
    ppermute x16, waiting for transfers between devices, move(): return lax.ppermute(array, 'seq', pairs)  69.2 us
    pallas_call x7, Pallas kernels, partial_attention(): pl.pallas_call(body, in_specs=[pl.BlockSpec(memory_space=pltpu.SMEM)] + i...  29.3 us
    ppermute x16, starting transfers between devices, move(): return lax.ppermute(array, 'seq', pairs)  28 us
    pallas_call x4, Pallas kernels, merge_pair(): pl.pallas_call(body, in_specs=[pl.BlockSpec(memory_space=pltpu.SMEM)] + [...  5.75 us
    pallas_call x2, Pallas kernels, merge_final(): pl.pallas_call(body, in_specs=[pl.BlockSpec(memory_space=pltpu.SMEM)] + [...  5.66 us
    dynamic_slice x1, local copies, waits for them, and re-layouts, queries_travel(): lax.dynamic_slice_in_dim(later_pages, (1 - core) * part_width, part_width...  3.64 us
  transfers between devices with their start and end apart: 19, of which 11 were waited for; matrix products, arithmetic and copies ran while one was open for 1% of the time, Pallas kernels for 28%

profile of v2, /device:TPU:0, one launch (start us, length us, event | category | flops | bytes accessed | tf_op | source)
XLA Modules:
  0.0 150.3 jit_solution(909787989214441736)
XLA Ops:
  0.0 1.1 own_columns.3.rest_1_
  1.1 0.0 copy-start.9
  1.1 0.0 copy-start.10
  1.1 3.6 %constant_dynamic-slice_fusion.1 = bf16[21,2,128,256]{3,2,1,0:T(8,128)(2,1)} fusion(bf16[21,2,128,512]{3,2,1,0:T(8,128)(2,1)} %rest_3_.3, s32[]{:T(128)S(6)} %select_n.49), kind=kLoop, calls=%fused_computation.27 | loop fusion | bytes 5505028 | tf_op jit(solution)/shard_map/dynamic_slice | solution.py:626
  4.8 0.5 collective-permute-start
  5.3 4.6 %collective-permute-start.1 = (bf16[2,64,2048]{2,1,0:T(8,128)(2,1)S(1)}, bf16[2,64,2048]{2,1,0:T(8,128)(2,1)S(1)}, u32[]{:S(2)}, u32[]{:S(2)}) collective-permute-start(bf16[2,64,2048]{2,1,0:T(8,128)(2,1)S(1)} %own_columns.3.rest_1_), channel_id=1, source_target_pairs={{0,4},{4,8},{8,12},{1,5},{5,9},{9,13},{2,6},{6,10},{10,14},{3,7},{... | collective-permute-start | bytes 1572872 | tf_op jit(solution)/shard_map/ppermute | solution.py:642
  9.9 1.3 collective-permute-start.2
  11.2 1.1 own_columns.2.rest_0_
  12.3 4.6 %collective-permute-start.10 = (bf16[2,64,2048]{2,1,0:T(8,128)(2,1)S(1)}, bf16[2,64,2048]{2,1,0:T(8,128)(2,1)S(1)}, u32[]{:S(2)}, u32[]{:S(2)}) collective-permute-start(bf16[2,64,2048]{2,1,0:T(8,128)(2,1)S(1)} %own_columns.2.rest_0_), channel_id=1, source_target_pairs={{0,4},{4,8},{8,12},{1,5},{5,9},{9,13},{2,6},{6,10},{10,14},{3,7},{... | collective-permute-start | bytes 1572872 | tf_op jit(solution)/shard_map/ppermute | solution.py:642
  16.9 1.3 collective-permute-start.11
  18.2 0.1 fusion.2
  18.3 0.4 convert_reduce_fusion
  18.7 0.1 broadcast_compare_fusion
  18.8 0.2 fusion
  19.1 0.1 copy.11
  19.2 0.1 reshape.86
  19.2 0.1 pad_add_fusion.1.plan_ref
  19.3 13.5 %collective-permute-done.10.rest_0_.rest_2_ = bf16[2,64,2048]{2,1,0:T(8,128)(2,1)S(1)} collective-permute-done((bf16[2,64,2048]{2,1,0:T(8,128)(2,1)S(1)}, bf16[2,64,2048]{2,1,0:T(8,128)(2,1)S(1)}, u32[]{:S(2)}, u32[]{:S(2)}) %collective-permute-start.10) | collective-permute-done | bytes 524320 | tf_op jit(solution)/shard_map/ppermute | solution.py:642
  32.8 4.2 %collective-permute-done.11.rest_1_ = bf16[2,64,2048]{2,1,0:T(8,128)(2,1)} collective-permute-done((bf16[2,64,2048]{2,1,0:T(8,128)(2,1)S(1)}, bf16[2,64,2048]{2,1,0:T(8,128)(2,1)}, u32[]{:S(2)}, u32[]{:S(2)}) %collective-permute-start.11) | collective-permute-done | bytes 524320 | tf_op jit(solution)/shard_map/ppermute | solution.py:642
  37.1 0.0 collective-permute-done.rest_3_.rest_4_
  37.1 4.6 %partial_attention.11 = (bf16[2,64,2176]{2,1,0:T(8,128)(2,1)S(1)}, bf16[2,64,2176]{2,1,0:T(8,128)(2,1)S(1)}, bf16[2,64,2176]{2,1,0:T(8,128)(2,1)S(1)}) custom-call(s32[146]{0:T(256)S(1)} %pad_add_fusion.1.plan_ref, bf16[2,64,2048]{2,1,0:T(8,128)(2,1)S(1)} %collective-permute-done.10.rest_0_.rest_2_, bf16[2,64,2048]{2,1,0:T(8,128)(2,1)} %collective-permute-done.11.rest_1_, ...), custom_call_target="tpu_custom_call" | custom-call | flops 536870912 | bytes 2097152 | tf_op jit(solution)/shard_map/partial_attention/pallas_call | solution.py:419
  41.7 3.5 %collective-permute-start.12 = (bf16[2,64,2176]{2,1,0:T(8,128)(2,1)S(1)}, bf16[2,64,2176]{2,1,0:T(8,128)(2,1)S(1)}, u32[]{:S(2)}, u32[]{:S(2)}) collective-permute-start(bf16[2,64,2176]{2,1,0:T(8,128)(2,1)S(1)} %get-tuple-element.23), channel_id=1, source_target_pairs={{0,4},{4,8},{8,12},{1,5},{5,9},{9,13},{2,6},{6,10},{10,14},{3,7},{... | collective-permute-start | bytes 1671176 | tf_op jit(solution)/shard_map/ppermute | solution.py:642
  45.2 1.3 collective-permute-start.13
  46.5 0.0 copy-start.5
  46.5 4.1 %partial_attention.8 = (bf16[2,64,2176]{2,1,0:T(8,128)(2,1)S(1)}, bf16[2,64,2176]{2,1,0:T(8,128)(2,1)S(1)}, bf16[2,64,2176]{2,1,0:T(8,128)(2,1)S(1)}) custom-call(s32[146]{0:T(256)S(1)} %pad_add_fusion.1.plan_ref, bf16[2,64,2048]{2,1,0:T(8,128)(2,1)S(1)} %collective-permute-done.1.rest_0_.rest_2_, bf16[2,64,2048]{2,1,0:T(8,128)(2,1)S(1)} %collective-permute-done.2.rest_1_, ...), custom_call_target="tpu_custom_call" | custom-call | flops 536870912 | bytes 2097152 | tf_op jit(solution)/shard_map/partial_attention/pallas_call | solution.py:419
  50.7 3.8 %collective-permute-start.3 = (bf16[2,64,2176]{2,1,0:T(8,128)(2,1)S(1)}, bf16[2,64,2176]{2,1,0:T(8,128)(2,1)S(1)}, u32[]{:S(2)}, u32[]{:S(2)}) collective-permute-start(bf16[2,64,2176]{2,1,0:T(8,128)(2,1)S(1)} %get-tuple-element.18), channel_id=1, source_target_pairs={{0,4},{4,8},{8,12},{1,5},{5,9},{9,13},{2,6},{6,10},{10,14},{3,7},{... | collective-permute-start | bytes 1671176 | tf_op jit(solution)/shard_map/ppermute | solution.py:642
  54.4 1.3 collective-permute-start.4
  55.7 2.4 %collective-permute-done.12.rest_0_.rest_1_ = bf16[2,64,2176]{2,1,0:T(8,128)(2,1)S(1)} collective-permute-done((bf16[2,64,2176]{2,1,0:T(8,128)(2,1)S(1)}, bf16[2,64,2176]{2,1,0:T(8,128)(2,1)S(1)}, u32[]{:S(2)}, u32[]{:S(2)}) %collective-permute-start.12) | collective-permute-done | bytes 557088 | tf_op jit(solution)/shard_map/ppermute | solution.py:642
  58.1 4.4 %collective-permute-done.13.rest_1_.rest_2_ = bf16[2,64,2176]{2,1,0:T(8,128)(2,1)S(1)} collective-permute-done((bf16[2,64,2176]{2,1,0:T(8,128)(2,1)S(1)}, bf16[2,64,2176]{2,1,0:T(8,128)(2,1)S(1)}, u32[]{:S(2)}, u32[]{:S(2)}) %collective-permute-start.13) | collective-permute-done | bytes 557088 | tf_op jit(solution)/shard_map/ppermute | solution.py:642
  62.6 4.1 %partial_attention.12 = (bf16[2,64,2176]{2,1,0:T(8,128)(2,1)S(1)}, bf16[2,64,2176]{2,1,0:T(8,128)(2,1)S(1)}) custom-call(s32[146]{0:T(256)S(1)} %pad_add_fusion.1.plan_ref, bf16[2,64,2176]{2,1,0:T(8,128)(2,1)S(1)} %collective-permute-done.12.rest_0_.rest_1_, bf16[2,64,2176]{2,1,0:T(8,128)(2,1)S(1)} %collective-permute-done.13.rest_1_.rest_2_, ...), custom_call_target="tpu_custom_call" | custom-call | flops 536870912 | bytes 2097152 | tf_op jit(solution)/shard_map/partial_attention/pallas_call | solution.py:419
  66.7 0.8 collective-permute-start.14
  67.5 0.8 collective-permute-start.16
  68.3 1.8 %collective-permute-done.3.rest_0_.rest_1_ = bf16[2,64,2176]{2,1,0:T(8,128)(2,1)S(1)} collective-permute-done((bf16[2,64,2176]{2,1,0:T(8,128)(2,1)S(1)}, bf16[2,64,2176]{2,1,0:T(8,128)(2,1)S(1)}, u32[]{:S(2)}, u32[]{:S(2)}) %collective-permute-start.3) | collective-permute-done | bytes 557088 | tf_op jit(solution)/shard_map/ppermute | solution.py:642
  70.1 4.4 %collective-permute-done.4.rest_1_.rest_2_ = bf16[2,64,2176]{2,1,0:T(8,128)(2,1)S(1)} collective-permute-done((bf16[2,64,2176]{2,1,0:T(8,128)(2,1)S(1)}, bf16[2,64,2176]{2,1,0:T(8,128)(2,1)S(1)}, u32[]{:S(2)}, u32[]{:S(2)}) %collective-permute-start.4) | collective-permute-done | bytes 557088 | tf_op jit(solution)/shard_map/ppermute | solution.py:642
  74.5 3.3 %partial_attention.9 = (bf16[2,64,2176]{2,1,0:T(8,128)(2,1)S(1)}, bf16[2,64,2176]{2,1,0:T(8,128)(2,1)S(1)}) custom-call(s32[146]{0:T(256)S(1)} %pad_add_fusion.1.plan_ref, bf16[2,64,2176]{2,1,0:T(8,128)(2,1)S(1)} %collective-permute-done.3.rest_0_.rest_1_, bf16[2,64,2176]{2,1,0:T(8,128)(2,1)S(1)} %collective-permute-done.4.rest_1_.rest_2_, ...), custom_call_target="tpu_custom_call" | custom-call | flops 536870912 | bytes 2097152 | tf_op jit(solution)/shard_map/partial_attention/pallas_call | solution.py:419
  77.8 1.6 %collective-permute-start.5 = (bf16[2,64,2176]{2,1,0:T(8,128)(2,1)S(1)}, bf16[2,64,2176]{2,1,0:T(8,128)(2,1)S(1)}, u32[]{:S(2)}, u32[]{:S(2)}) collective-permute-start(bf16[2,64,2176]{2,1,0:T(8,128)(2,1)S(1)} %get-tuple-element.20), channel_id=1, source_target_pairs={{8,12},{4,0},{12,8},{0,4},{9,13},{5,1},{13,9},{1,5},{10,14},{6,2},... | collective-permute-start | bytes 1671176 | tf_op jit(solution)/shard_map/ppermute | solution.py:642
  79.3 0.7 collective-permute-start.7
  80.0 6.4 %collective-permute-done.14.rest_0_.rest_1_ = bf16[2,64,2176]{2,1,0:T(8,128)(2,1)S(1)} collective-permute-done((bf16[2,64,2176]{2,1,0:T(8,128)(2,1)S(1)}, bf16[2,64,2176]{2,1,0:T(8,128)(2,1)S(1)}, u32[]{:S(2)}, u32[]{:S(2)}) %collective-permute-start.14) | collective-permute-done | bytes 557088 | tf_op jit(solution)/shard_map/ppermute | solution.py:642
  86.4 3.8 %partial_attention.13.rest_2_.rest_0_ = bf16[2,64,2176]{2,1,0:T(8,128)(2,1)S(1)} custom-call(s32[146]{0:T(256)S(1)} %pad_add_fusion.1.plan_ref, bf16[2,64,2176]{2,1,0:T(8,128)(2,1)S(1)} %collective-permute-done.14.rest_0_.rest_1_, bf16[2,64,2048]{2,1,0:T(8,128)(2,1)} %collective-permute-done.11.rest_1_, bf16[2,64,2048]{2,1,0:T(8,128)(2,1)S(1)} %copy-done.8, ...), custom_call_target="tpu_custom_call" | custom-call | flops 536870912 | bytes 2097152 | tf_op jit(solution)/shard_map/partial_attention/pallas_call | solution.py:419
  90.2 0.0 copy-start.6
  90.2 1.4 merge_pair.6
  91.6 0.0 collective-permute-start.15
  91.6 0.0 collective-permute-done.16.rest_1_
  91.6 1.6 %merge_pair.7 = bf16[2,64,2176]{2,1,0:T(8,128)(2,1)} custom-call(s32[146]{0:T(256)S(1)} %pad_add_fusion.1.plan_ref, bf16[2,64,2176]{2,1,0:T(8,128)(2,1)S(1)} %partial_attention.13.rest_2_.rest_0_, bf16[2,64,2176]{2,1,0:T(8,128)(2,1)S(1)} %collective-permute-done.16.rest_1_), custom_call_target="tpu_custom_call" | custom-call | tf_op jit(solution)/shard_map/merge_pair/pallas_call | solution.py:487
  93.2 1.3 collective-permute-start.17
  94.5 20.7 %collective-permute-done.5.rest_0_.rest_1_ = bf16[2,64,2176]{2,1,0:T(8,128)(2,1)S(1)} collective-permute-done((bf16[2,64,2176]{2,1,0:T(8,128)(2,1)S(1)}, bf16[2,64,2176]{2,1,0:T(8,128)(2,1)S(1)}, u32[]{:S(2)}, u32[]{:S(2)}) %collective-permute-start.5) | collective-permute-done | bytes 557088 | tf_op jit(solution)/shard_map/ppermute | solution.py:642
  115.2 3.1 %partial_attention.10.rest_2_.rest_0_ = bf16[2,64,2176]{2,1,0:T(8,128)(2,1)S(1)} custom-call(s32[146]{0:T(256)S(1)} %pad_add_fusion.1.plan_ref, bf16[2,64,2176]{2,1,0:T(8,128)(2,1)S(1)} %collective-permute-done.5.rest_0_.rest_1_, bf16[2,64,2048]{2,1,0:T(8,128)(2,1)S(1)} %copy-done.6, bf16[2,64,2048]{2,1,0:T(8,128)(2,1)S(1)} %copy-done.4, ...), custom_call_target="tpu_custom_call" | custom-call | flops 536870912 | bytes 2097152 | tf_op jit(solution)/shard_map/partial_attention/pallas_call | solution.py:419
  118.3 1.4 merge_pair.4
  119.7 0.0 collective-permute-start.6
  119.7 0.0 collective-permute-done.7.rest_1_
  119.7 1.4 merge_pair.5
  121.1 1.3 collective-permute-start.8
  122.4 0.2 constant_dynamic-slice_fusion
  122.6 1.0 copy-done.2
  123.7 6.4 %partial_attention.7.own_ref = bf16[4,64,2176]{2,1,0:T(8,128)(2,1)S(1)} custom-call(s32[146]{0:T(256)S(1)} %pad_add_fusion.1.plan_ref, bf16[2,64,2048]{2,1,0:T(8,128)(2,1)S(1)} %copy-done.2, bf16[2,64,2048]{2,1,0:T(8,128)(2,1)S(1)} %own_columns.3.rest_1_, bf16[21,2,128,512]{3,2,1,0:T(8,128)(2,1)} %rest_3_.3, ...), custom_call_target="tpu_custom_call" | custom-call | flops 1073741824 | bytes 4194304 | tf_op jit(solution)/shard_map/partial_attention/pallas_call | solution.py:419
  130.1 3.1 %collective-permute-done.17.rest_0_ = bf16[2,64,2176]{2,1,0:T(8,128)(2,1)} collective-permute-done((bf16[2,64,2176]{2,1,0:T(8,128)(2,1)}, bf16[2,64,2176]{2,1,0:T(8,128)(2,1)}, u32[]{:S(2)}, u32[]{:S(2)}) %collective-permute-start.17) | collective-permute-done | bytes 557088 | tf_op jit(solution)/shard_map/ppermute | solution.py:642
  133.2 2.7 %merge_final.3.own_ref = bf16[2,64,2048]{2,1,0:T(8,128)(2,1)S(1)} custom-call(s32[146]{0:T(256)S(1)} %pad_add_fusion.1.plan_ref, bf16[4,64,2176]{2,1,0:T(8,128)(2,1)S(1)} %partial_attention.7.own_ref, bf16[2,64,2176]{2,1,0:T(8,128)(2,1)} %collective-permute-done.15.last_ref, bf16[2,64,2176]{2,1,0:T(8,128)(2,1)} %collective-permute-done.17.rest_0_, ...), custom_call_target="tpu_custom_call" | custom-call | tf_op jit(solution)/shard_map/merge_final/pallas_call | solution.py:529
  135.9 0.1 collective-permute-start.18
  136.0 8.2 %collective-permute-done.8.rest_0_ = bf16[2,64,2176]{2,1,0:T(8,128)(2,1)} collective-permute-done((bf16[2,64,2176]{2,1,0:T(8,128)(2,1)}, bf16[2,64,2176]{2,1,0:T(8,128)(2,1)}, u32[]{:S(2)}, u32[]{:S(2)}) %collective-permute-start.8) | collective-permute-done | bytes 557088 | tf_op jit(solution)/shard_map/ppermute | solution.py:642
  144.2 2.9 %merge_final.2.own_ref = bf16[2,64,2048]{2,1,0:T(8,128)(2,1)S(1)} custom-call(s32[146]{0:T(256)S(1)} %pad_add_fusion.1.plan_ref, bf16[4,64,2176]{2,1,0:T(8,128)(2,1)S(1)} %partial_attention.7.own_ref, bf16[2,64,2176]{2,1,0:T(8,128)(2,1)} %collective-permute-done.6.last_ref, bf16[2,64,2176]{2,1,0:T(8,128)(2,1)} %collective-permute-done.8.rest_0_, ...), custom_call_target="tpu_custom_call" | custom-call | tf_op jit(solution)/shard_map/merge_final/pallas_call | solution.py:529
  147.2 0.1 collective-permute-start.9
  147.3 1.0 place_columns.2.rest_0_
  148.3 0.9 collective-permute-done.9.other_ref
  149.1 1.0 place_columns.3
  (30 shorter events, 0.1 us)
Async XLA Ops:
  0.0 122.4 %copy-start = (bf16[4,64,2,512]{3,2,1,0:T(2,128)(2,1)S(1)}, bf16[4,64,2,512]{3,2,1,0:T(2,128)(2,1)}, u32[]{:S(2)}) copy-start(bf16[4,64,2,512]{3,2,1,0:T(2,128)(2,1)} %param.7) | copy-start | bytes 1572868
  1.1 17.1 %copy-start.9 = (s32[16,16]{1,0:T(8,128)S(1)}, s32[16,16]{1,0:T(8,128)}, u32[]{:S(2)}) copy-start(s32[16,16]{1,0:T(8,128)} %param.9) | copy-start | bytes 3076
  1.1 17.1 %copy-start.10 = (s32[16]{0:T(128)S(1)}, s32[16]{0:T(128)}, u32[]{:S(2)}) copy-start(s32[16]{0:T(128)} %param.10) | copy-start | bytes 196
  4.8 14.3 %copy-start.11 = (s32[16]{0:T(128)S(1)}, s32[16]{0:T(128)}, u32[]{:S(2)}) copy-start(s32[16]{0:T(128)} %param.11) | copy-start | bytes 196
  4.8 32.3 %collective-permute-start = (bf16[21,2,128,256]{3,2,1,0:T(8,128)(2,1)}, bf16[21,2,128,256]{3,2,1,0:T(8,128)(2,1)}, u32[]{:S(2)}, u32[]{:S(2)}) collective-permute-start(bf16[21,2,128,256]{3,2,1,0:T(8,128)(2,1)} %constant_dynamic-slice_fusion.1), channel_id=1, source_target_pairs={{0,1},{1,0},{2,3},{3,2},{4,5},{5,4},{6,7},{7,6},{8,9},{9,8},{10,11... | collective-permute-start | bytes 8257544 | tf_op jit(solution)/shard_map/ppermute | solution.py:627
  5.3 41.2 %collective-permute-start.1 = (bf16[2,64,2048]{2,1,0:T(8,128)(2,1)S(1)}, bf16[2,64,2048]{2,1,0:T(8,128)(2,1)S(1)}, u32[]{:S(2)}, u32[]{:S(2)}) collective-permute-start(bf16[2,64,2048]{2,1,0:T(8,128)(2,1)S(1)} %own_columns.3.rest_1_), channel_id=1, source_target_pairs={{0,4},{4,8},{8,12},{1,5},{5,9},{9,13},{2,6},{6,10},{10,14},{3,7},{... | collective-permute-start | bytes 1572872 | tf_op jit(solution)/shard_map/ppermute | solution.py:642
  9.9 36.6 %collective-permute-start.2 = (bf16[2,64,2048]{2,1,0:T(8,128)(2,1)S(1)}, bf16[2,64,2048]{2,1,0:T(8,128)(2,1)S(1)}, u32[]{:S(2)}, u32[]{:S(2)}) collective-permute-start(bf16[2,64,2048]{2,1,0:T(8,128)(2,1)S(1)} %own_columns.3.rest_1_), channel_id=1, source_target_pairs={{12,8},{8,4},{4,0},{13,9},{9,5},{5,1},{14,10},{10,6},{6,2},{15,11}... | collective-permute-start | bytes 1572872 | tf_op jit(solution)/shard_map/ppermute | solution.py:642
  12.3 29.4 %copy-start.1 = (bf16[2,64,2048]{2,1,0:T(8,128)(2,1)}, bf16[2,64,2048]{2,1,0:T(8,128)(2,1)S(1)}, u32[]{:S(2)}) copy-start(bf16[2,64,2048]{2,1,0:T(8,128)(2,1)S(1)} %own_columns.2.rest_0_) | copy-start | bytes 1572868
  12.3 20.5 %collective-permute-start.10 = (bf16[2,64,2048]{2,1,0:T(8,128)(2,1)S(1)}, bf16[2,64,2048]{2,1,0:T(8,128)(2,1)S(1)}, u32[]{:S(2)}, u32[]{:S(2)}) collective-permute-start(bf16[2,64,2048]{2,1,0:T(8,128)(2,1)S(1)} %own_columns.2.rest_0_), channel_id=1, source_target_pairs={{0,4},{4,8},{8,12},{1,5},{5,9},{9,13},{2,6},{6,10},{10,14},{3,7},{... | collective-permute-start | bytes 1572872 | tf_op jit(solution)/shard_map/ppermute | solution.py:642
  16.9 20.2 %collective-permute-start.11 = (bf16[2,64,2048]{2,1,0:T(8,128)(2,1)S(1)}, bf16[2,64,2048]{2,1,0:T(8,128)(2,1)}, u32[]{:S(2)}, u32[]{:S(2)}) collective-permute-start(bf16[2,64,2048]{2,1,0:T(8,128)(2,1)S(1)} %own_columns.2.rest_0_), channel_id=1, source_target_pairs={{12,8},{8,4},{4,0},{13,9},{9,5},{5,1},{14,10},{10,6},{6,2},{15,11}... | collective-permute-start | bytes 1572872 | tf_op jit(solution)/shard_map/ppermute | solution.py:642
  32.8 8.9 %copy-start.7 = (bf16[2,64,2048]{2,1,0:T(8,128)(2,1)}, bf16[2,64,2048]{2,1,0:T(8,128)(2,1)S(1)}, u32[]{:S(2)}) copy-start(bf16[2,64,2048]{2,1,0:T(8,128)(2,1)S(1)} %collective-permute-done.10.rest_0_.rest_2_) | copy-start | bytes 1572868
  41.7 16.4 %collective-permute-start.12 = (bf16[2,64,2176]{2,1,0:T(8,128)(2,1)S(1)}, bf16[2,64,2176]{2,1,0:T(8,128)(2,1)S(1)}, u32[]{:S(2)}, u32[]{:S(2)}) collective-permute-start(bf16[2,64,2176]{2,1,0:T(8,128)(2,1)S(1)} %get-tuple-element.23), channel_id=1, source_target_pairs={{0,4},{4,8},{8,12},{1,5},{5,9},{9,13},{2,6},{6,10},{10,14},{3,7},{... | collective-permute-start | bytes 1671176 | tf_op jit(solution)/shard_map/ppermute | solution.py:642
  45.2 17.4 %collective-permute-start.13 = (bf16[2,64,2176]{2,1,0:T(8,128)(2,1)S(1)}, bf16[2,64,2176]{2,1,0:T(8,128)(2,1)S(1)}, u32[]{:S(2)}, u32[]{:S(2)}) collective-permute-start(bf16[2,64,2176]{2,1,0:T(8,128)(2,1)S(1)} %get-tuple-element.24), channel_id=1, source_target_pairs={{12,8},{8,4},{4,0},{13,9},{9,5},{5,1},{14,10},{10,6},{6,2},{15,11}... | collective-permute-start | bytes 1671176 | tf_op jit(solution)/shard_map/ppermute | solution.py:642
  46.5 4.2 %copy-start.3 = (bf16[2,64,2048]{2,1,0:T(8,128)(2,1)}, bf16[2,64,2048]{2,1,0:T(8,128)(2,1)S(1)}, u32[]{:S(2)}) copy-start(bf16[2,64,2048]{2,1,0:T(8,128)(2,1)S(1)} %collective-permute-done.1.rest_0_.rest_2_) | copy-start | bytes 1572868
  46.5 4.1 %copy-start.5 = (bf16[2,64,2048]{2,1,0:T(8,128)(2,1)}, bf16[2,64,2048]{2,1,0:T(8,128)(2,1)S(1)}, u32[]{:S(2)}) copy-start(bf16[2,64,2048]{2,1,0:T(8,128)(2,1)S(1)} %collective-permute-done.2.rest_1_) | copy-start | bytes 1572868
  50.7 19.4 %collective-permute-start.3 = (bf16[2,64,2176]{2,1,0:T(8,128)(2,1)S(1)}, bf16[2,64,2176]{2,1,0:T(8,128)(2,1)S(1)}, u32[]{:S(2)}, u32[]{:S(2)}) collective-permute-start(bf16[2,64,2176]{2,1,0:T(8,128)(2,1)S(1)} %get-tuple-element.18), channel_id=1, source_target_pairs={{0,4},{4,8},{8,12},{1,5},{5,9},{9,13},{2,6},{6,10},{10,14},{3,7},{... | collective-permute-start | bytes 1671176 | tf_op jit(solution)/shard_map/ppermute | solution.py:642
  54.4 20.1 %collective-permute-start.4 = (bf16[2,64,2176]{2,1,0:T(8,128)(2,1)S(1)}, bf16[2,64,2176]{2,1,0:T(8,128)(2,1)S(1)}, u32[]{:S(2)}, u32[]{:S(2)}) collective-permute-start(bf16[2,64,2176]{2,1,0:T(8,128)(2,1)S(1)} %get-tuple-element.19), channel_id=1, source_target_pairs={{12,8},{8,4},{4,0},{13,9},{9,5},{5,1},{14,10},{10,6},{6,2},{15,11}... | collective-permute-start | bytes 1671176 | tf_op jit(solution)/shard_map/ppermute | solution.py:642
  66.7 19.8 %collective-permute-start.14 = (bf16[2,64,2176]{2,1,0:T(8,128)(2,1)S(1)}, bf16[2,64,2176]{2,1,0:T(8,128)(2,1)S(1)}, u32[]{:S(2)}, u32[]{:S(2)}) collective-permute-start(bf16[2,64,2176]{2,1,0:T(8,128)(2,1)S(1)} %get-tuple-element.25), channel_id=1, source_target_pairs={{8,12},{4,0},{12,8},{0,4},{9,13},{5,1},{13,9},{1,5},{10,14},{6,2},... | collective-permute-start | bytes 1671176 | tf_op jit(solution)/shard_map/ppermute | solution.py:642
  67.5 19.0 %copy-start.8 = (bf16[2,64,2048]{2,1,0:T(8,128)(2,1)S(1)}, bf16[2,64,2048]{2,1,0:T(8,128)(2,1)}, u32[]{:S(2)}) copy-start(bf16[2,64,2048]{2,1,0:T(8,128)(2,1)} %copy-done.7) | copy-start | bytes 1572868
  67.5 24.2 %collective-permute-start.16 = (bf16[2,64,2176]{2,1,0:T(8,128)(2,1)S(1)}, bf16[2,64,2176]{2,1,0:T(8,128)(2,1)S(1)}, u32[]{:S(2)}, u32[]{:S(2)}) collective-permute-start(bf16[2,64,2176]{2,1,0:T(8,128)(2,1)S(1)} %get-tuple-element.26), channel_id=1, source_target_pairs={{4,8},{8,4},{5,9},{9,5},{6,10},{10,6},{7,11},{11,7},{20,24},{24,20... | collective-permute-start | bytes 1671176 | tf_op jit(solution)/shard_map/ppermute | solution.py:642
  77.8 37.4 %collective-permute-start.5 = (bf16[2,64,2176]{2,1,0:T(8,128)(2,1)S(1)}, bf16[2,64,2176]{2,1,0:T(8,128)(2,1)S(1)}, u32[]{:S(2)}, u32[]{:S(2)}) collective-permute-start(bf16[2,64,2176]{2,1,0:T(8,128)(2,1)S(1)} %get-tuple-element.20), channel_id=1, source_target_pairs={{8,12},{4,0},{12,8},{0,4},{9,13},{5,1},{13,9},{1,5},{10,14},{6,2},... | collective-permute-start | bytes 1671176 | tf_op jit(solution)/shard_map/ppermute | solution.py:642
  79.3 40.4 %collective-permute-start.7 = (bf16[2,64,2176]{2,1,0:T(8,128)(2,1)S(1)}, bf16[2,64,2176]{2,1,0:T(8,128)(2,1)S(1)}, u32[]{:S(2)}, u32[]{:S(2)}) collective-permute-start(bf16[2,64,2176]{2,1,0:T(8,128)(2,1)S(1)} %get-tuple-element.21), channel_id=1, source_target_pairs={{4,8},{8,4},{5,9},{9,5},{6,10},{10,6},{7,11},{11,7},{20,24},{24,20... | collective-permute-start | bytes 1671176 | tf_op jit(solution)/shard_map/ppermute | solution.py:642
  90.2 25.0 %copy-start.4 = (bf16[2,64,2048]{2,1,0:T(8,128)(2,1)S(1)}, bf16[2,64,2048]{2,1,0:T(8,128)(2,1)}, u32[]{:S(2)}) copy-start(bf16[2,64,2048]{2,1,0:T(8,128)(2,1)} %copy-done.3) | copy-start | bytes 1572868
  90.2 25.0 %copy-start.6 = (bf16[2,64,2048]{2,1,0:T(8,128)(2,1)S(1)}, bf16[2,64,2048]{2,1,0:T(8,128)(2,1)}, u32[]{:S(2)}) copy-start(bf16[2,64,2048]{2,1,0:T(8,128)(2,1)} %copy-done.5) | copy-start | bytes 1572868
  91.6 38.4 %collective-permute-start.15 = (bf16[2,64,2176]{2,1,0:T(8,128)(2,1)}, bf16[2,64,2176]{2,1,0:T(8,128)(2,1)}, u32[]{:S(2)}, u32[]{:S(2)}) collective-permute-start(bf16[2,64,2176]{2,1,0:T(8,128)(2,1)} %merge_pair.6), channel_id=1, source_target_pairs={{4,8},{8,4},{12,0},{0,12},{5,9},{9,5},{13,1},{1,13},{6,10},{10,6},... | collective-permute-start | bytes 1671176 | tf_op jit(solution)/shard_map/ppermute | solution.py:642
  93.2 40.0 %collective-permute-start.17 = (bf16[2,64,2176]{2,1,0:T(8,128)(2,1)}, bf16[2,64,2176]{2,1,0:T(8,128)(2,1)}, u32[]{:S(2)}, u32[]{:S(2)}) collective-permute-start(bf16[2,64,2176]{2,1,0:T(8,128)(2,1)} %merge_pair.7), channel_id=1, source_target_pairs={{8,12},{4,0},{9,13},{5,1},{10,14},{6,2},{11,15},{7,3},{24,28},{20,... | collective-permute-start | bytes 1671176 | tf_op jit(solution)/shard_map/ppermute | solution.py:642
  119.7 16.3 %collective-permute-start.6 = (bf16[2,64,2176]{2,1,0:T(8,128)(2,1)}, bf16[2,64,2176]{2,1,0:T(8,128)(2,1)}, u32[]{:S(2)}, u32[]{:S(2)}) collective-permute-start(bf16[2,64,2176]{2,1,0:T(8,128)(2,1)} %merge_pair.4), channel_id=1, source_target_pairs={{4,8},{8,4},{12,0},{0,12},{5,9},{9,5},{13,1},{1,13},{6,10},{10,6},... | collective-permute-start | bytes 1671176 | tf_op jit(solution)/shard_map/ppermute | solution.py:642
  121.1 23.1 %collective-permute-start.8 = (bf16[2,64,2176]{2,1,0:T(8,128)(2,1)}, bf16[2,64,2176]{2,1,0:T(8,128)(2,1)}, u32[]{:S(2)}, u32[]{:S(2)}) collective-permute-start(bf16[2,64,2176]{2,1,0:T(8,128)(2,1)} %merge_pair.5), channel_id=1, source_target_pairs={{8,12},{4,0},{9,13},{5,1},{10,14},{6,2},{11,15},{7,3},{24,28},{20,... | collective-permute-start | bytes 1671176 | tf_op jit(solution)/shard_map/ppermute | solution.py:642
  122.6 1.0 copy-start.2
  135.9 11.3 %collective-permute-start.18 = (bf16[2,64,2048]{2,1,0:T(8,128)(2,1)S(1)}, bf16[2,64,2048]{2,1,0:T(8,128)(2,1)S(1)}, u32[]{:S(2)}, u32[]{:S(2)}) collective-permute-start(bf16[2,64,2048]{2,1,0:T(8,128)(2,1)S(1)} %merge_final.3.own_ref), channel_id=1, source_target_pairs={{0,1},{1,0},{2,3},{3,2},{4,5},{5,4},{6,7},{7,6},{8,9},{9,8},{10,11... | collective-permute-start | bytes 1572872 | tf_op jit(solution)/shard_map/ppermute | solution.py:684
  147.2 2.0 %collective-permute-start.9 = (bf16[2,64,2048]{2,1,0:T(8,128)(2,1)S(1)}, bf16[2,64,2048]{2,1,0:T(8,128)(2,1)S(1)}, u32[]{:S(2)}, u32[]{:S(2)}) collective-permute-start(bf16[2,64,2048]{2,1,0:T(8,128)(2,1)S(1)} %merge_final.2.own_ref), channel_id=1, source_target_pairs={{0,1},{1,0},{2,3},{3,2},{4,5},{5,4},{6,7},{7,6},{8,9},{9,8},{10,11... | collective-permute-start | bytes 1572872 | tf_op jit(solution)/shard_map/ppermute | solution.py:684

commit v3 on v2

--- a/solution.py
+++ b/solution.py
@@ -199,16 +199,21 @@
     return jnp.concatenate([jnp.stack([shard, core]).astype(jnp.int32), rows.reshape(-1)])
 
 
+def lse_third(shape, heads):
+    lane = lax.broadcasted_iota(jnp.int32, shape, 1)
+    return lane % (3 * heads) // heads
+
+
 def lse_block(lse_tile, heads):
-    lane = lax.broadcasted_iota(jnp.int32, lse_tile.shape, 1)
+    third = lse_third(lse_tile.shape, heads)
     high = lse_tile.astype(jnp.bfloat16)
     rest = lse_tile - high.astype(jnp.float32)
     middle = rest.astype(jnp.bfloat16)
     low = rest - middle.astype(jnp.float32)
     mixed = jnp.where(
-        lane < heads,
+        third == 0,
         high.astype(jnp.float32),
-        jnp.where(lane < 2 * heads, middle.astype(jnp.float32), low),
+        jnp.where(third == 1, middle.astype(jnp.float32), low),
     )
     return mixed.astype(jnp.bfloat16)
 
@@ -223,11 +228,11 @@
 
 
 def spread_lse(lse, heads):
-    lane = lax.broadcasted_iota(jnp.int32, lse.shape, 1)
+    third = lse_third(lse.shape, heads)
     return jnp.where(
-        lane < heads,
+        third == 0,
         lse,
-        jnp.where(lane < 2 * heads, pltpu.roll(lse, heads, 1), pltpu.roll(lse, 2 * heads, 1)),
+        jnp.where(third == 1, pltpu.roll(lse, heads, 1), pltpu.roll(lse, 2 * heads, 1)),
     )
 
 
@@ -252,7 +257,7 @@
     plan, sources, choice, homes, pages, twin_pages, fresh, relays, *, count, width, first, seq_dev,
     picks, sub_count
 ):
-    row_count = sources[0].shape[1]
+    row_count = sources[0].shape[0]
     part_width = twin_pages.shape[3]
     heads_kv = part_width // HD
     heads = width // HD
@@ -266,15 +271,15 @@
         home = by_chip(plan_ref[0], homes)
         return plan_ref[2 + (home * seq_dev + first + k) * record + column]
 
-    chunk = sources[0].shape[0]
+    total = count * width
 
     def body(plan_ref, *rest):
         query_refs = rest[: len(sources)]
         pages_hbm, twin_hbm = rest[len(sources) : len(sources) + 2]
         fresh_ref = rest[len(sources) + 2] if fresh is not None else None
-        query_ref, page_buf, sems = rest[-3:]
-        out_ref = rest[-4 - len(relays)]
-        relay_refs = rest[-3 - len(relays) : -3]
+        query_ref, result_ref, page_buf, sems = rest[-4:]
+        out_ref = rest[-5 - len(relays)]
+        relay_refs = rest[-4 - len(relays) : -4]
         shard = plan_ref[0]
         mine = pl.ds(pl.multiple_of(plan_ref[1] * part_width, LANES), part_width)
 
@@ -294,22 +299,11 @@
         def attend_one(k):
             counts = [entry(plan_ref, k, refs_per_seq + n) for n in range(refs_per_seq)]
             flag = entry(plan_ref, k, 2 * refs_per_seq)
-            for n in range(len(sources)):
-                if fresh is not None:
-                    chosen = k // chunk == n
-                else:
-                    chosen = one_of(shard, choice, n)
-
-                @pl.when(chosen)
-                def _(n=n):
-                    query_ref[...] = query_refs[n][k % chunk, :, :width]
-
-            for relay, relay_ref in zip(relays, relay_refs):
+            for j in range(count):
                 for n in range(len(sources)):
-                    if n in relay:
-                        @pl.when(one_of(shard, relay, n))
-                        def _(n=n, relay_ref=relay_ref):
-                            relay_ref[k, :, :width] = query_refs[n][k, :, :width]
+                    @pl.when((k == j) & one_of(shard, choice, n))
+                    def _(n=n, j=j):
+                        query_ref[...] = query_refs[n][:, j * width : (j + 1) * width]
 
             for n in range(refs_per_seq):
                 page_copy(k, n).wait()
@@ -322,18 +316,17 @@
             def _():
                 attend(k, counts, few, 1)
                 if few < row_count:
-                    out_ref[k, few:, :] = jnp.zeros(
-                        (row_count - few, width + LANES), jnp.bfloat16
-                    )
-
-            for relay, relay_ref in zip(relays, relay_refs):
-                @pl.when(one_of(shard, relay, -1))
-                def _(relay_ref=relay_ref):
-                    relay_ref[k] = out_ref[k]
+                    result_ref[few:, :] = jnp.zeros((row_count - few, width), jnp.bfloat16)
+
+            for j in range(count):
+                @pl.when(k == j)
+                def _(j=j):
+                    out_ref[:, j * width : (j + 1) * width] = result_ref[...]
 
         def attend(k, counts, rows, live_rows):
             lane = lax.broadcasted_iota(jnp.int32, (rows, LANES), 1)
             tile = jnp.zeros((rows, LANES), jnp.float32)
+            start = k * (3 * heads)
             per_block = max(1, min(group, BLOCK_ROWS // rows))
             stacked = per_block * rows
             key_lane = lax.broadcasted_iota(jnp.int32, (stacked, PAGE), 1)
@@ -401,12 +394,27 @@
                     for g in range(per_block):
                         head = base + g
                         part = slice(g * rows, (g + 1) * rows)
-                        out_ref[k, :rows, head * HD : (head + 1) * HD] = attended[part]
-                        spots = (lane == head) | (lane == head + heads) | (lane == head + 2 * heads)
+                        result_ref[:rows, head * HD : (head + 1) * HD] = attended[part]
+                        spot = lane - start - head
+                        spots = (spot == 0) | (spot == heads) | (spot == 2 * heads)
                         tile = jnp.where(spots, lse[part], tile)
-            out_ref[k, :rows, width:] = lse_block(tile, heads)
-
+            here = (lane >= start) & (lane < start + 3 * heads)
+            before = out_ref[:rows, total:].astype(jnp.float32)
+            block = lse_block(tile, heads).astype(jnp.float32)
+            out_ref[:rows, total:] = jnp.where(here, block, before).astype(jnp.bfloat16)
+
+        out_ref[:, total:] = jnp.zeros((row_count, LANES), jnp.bfloat16)
+        for relay, relay_ref in zip(relays, relay_refs):
+            for n in range(len(sources)):
+                if n in relay:
+                    @pl.when(one_of(shard, relay, n))
+                    def _(n=n, relay_ref=relay_ref):
+                        relay_ref[:, :total] = query_refs[n][:, :total]
         lax.fori_loop(0, count, one, 0)
+        for relay, relay_ref in zip(relays, relay_refs):
+            @pl.when(one_of(shard, relay, -1))
+            def _(relay_ref=relay_ref):
+                relay_ref[...] = out_ref[...]
 
     vmem = pl.BlockSpec(memory_space=pltpu.VMEM)
     hbm = pl.BlockSpec(memory_space=pltpu.HBM)
@@ -420,8 +428,9 @@
         body,
         in_specs=[pl.BlockSpec(memory_space=pltpu.SMEM)] + in_specs,
         out_specs=[vmem] * outs,
-        out_shape=[pltpu.VMEM((count, row_count, width + LANES), jnp.bfloat16)] * outs,
+        out_shape=[pltpu.VMEM((row_count, total + LANES), jnp.bfloat16)] * outs,
         scratch_shapes=[
+            pltpu.VMEM((row_count, width), jnp.bfloat16),
             pltpu.VMEM((row_count, width), jnp.bfloat16),
             pltpu.VMEM((count, refs_per_seq, 2, PAGE, part_width), jnp.bfloat16),
             pltpu.SemaphoreType.DMA((count, refs_per_seq)),
@@ -455,9 +464,8 @@
     return [w / total for w in weights], peak + jnp.log2(total)
 
 
-def merge_pair(plan, mine, incoming, other, *, chips):
-    count, _, full = mine.shape
-    width = full - LANES
+def merge_pair(plan, mine, incoming, other, *, chips, width):
+    total = mine.shape[1] - LANES
     heads = width // HD
     inputs = [mine, incoming] + ([other] if other is not None else [])
 
@@ -468,15 +476,16 @@
         @pl.when(here)
         def _():
             parts = rest[:2]
-            for k in range(count):
-                weights, lse = merge_weights([read_lse(r[k, :, width:], heads) for r in parts])
+            weights, lse = merge_weights([read_lse(r[:, total:], heads) for r in parts])
+            for k in range(total // width):
                 for h in range(heads):
-                    cols = slice(h * HD, (h + 1) * HD)
-                    out_ref[k, :, cols] = sum(
-                        r[k, :, cols].astype(jnp.float32) * w[:, h : h + 1]
+                    cols = slice(k * width + h * HD, k * width + (h + 1) * HD)
+                    spot = 3 * heads * k + h
+                    out_ref[:, cols] = sum(
+                        r[:, cols].astype(jnp.float32) * w[:, spot : spot + 1]
                         for r, w in zip(parts, weights)
                     ).astype(jnp.bfloat16)
-                out_ref[k, :, width:] = lse_block(spread_lse(lse, heads), heads)
+            out_ref[:, total:] = lse_block(spread_lse(lse, heads), heads)
 
         if other is not None:
             @pl.when(jnp.logical_not(here))
@@ -494,9 +503,10 @@
     )(plan, *[in_vmem(x) for x in inputs])
 
 
-def merge_final(plan, own, last_in, first_in, choice, *, first, seq_dev, record):
-    count, row_count, full = last_in.shape
-    width = full - LANES
+def merge_final(plan, own, last_in, first_in, choice, *, first, seq_dev, record, width):
+    row_count, full = last_in.shape
+    total = full - LANES
+    count = total // width
     heads = width // HD
 
     def body(plan_ref, own_ref, last_ref, *rest):
@@ -505,19 +515,22 @@
         shard = plan_ref[0]
 
         def finish(first_ref):
+            parts = [own_ref, last_ref, first_ref]
+            weights, _ = merge_weights([read_lse(r[:, total:], heads) for r in parts])
+            row = lax.broadcasted_iota(jnp.int32, (row_count, HD), 0)
             for k in range(count):
-                parts = [own_ref.at[first + k], last_ref.at[k], first_ref.at[k]]
-                weights, _ = merge_weights([read_lse(r[:, width:], heads) for r in parts])
-                row = lax.broadcasted_iota(jnp.int32, (row_count, HD), 0)
                 flag = plan_ref[2 + (shard * seq_dev + first + k) * record + record - 1]
                 live = row < jnp.where(flag == 1, row_count, 1)
                 for h in range(heads):
-                    cols = slice(h * HD, (h + 1) * HD)
-                    total = sum(
-                        r[:, cols].astype(jnp.float32) * w[:, h : h + 1]
+                    cols = slice(k * width + h * HD, k * width + (h + 1) * HD)
+                    spot = 3 * heads * k + h
+                    summed = sum(
+                        r[:, cols].astype(jnp.float32) * w[:, spot : spot + 1]
                         for r, w in zip(parts, weights)
                     )
-                    out_ref[k, :, cols] = jnp.where(live, total, 0.0).astype(jnp.bfloat16)
+                    out_ref[k, :, h * HD : (h + 1) * HD] = jnp.where(live, summed, 0.0).astype(
+                        jnp.bfloat16
+                    )
 
         for n, r in enumerate(first_refs):
             @pl.when(one_of(shard, choice, n))
@@ -544,11 +557,18 @@
     _, row_count, full = queries.shape
     width = full // parts
 
-    def body(core_ref, source, out_ref, sem):
+    def body(core_ref, source, out_ref, sems):
         cols = pl.ds(pl.multiple_of(core_ref[0] * width, LANES), width)
-        copy = pltpu.make_async_copy(source.at[first : first + count, :, cols], out_ref, sem)
-        copy.start()
-        copy.wait()
+        copies = [
+            pltpu.make_async_copy(
+                source.at[first + k, :, cols], out_ref.at[:, k * width : (k + 1) * width], sems.at[k]
+            )
+            for k in range(count)
+        ]
+        for c in copies:
+            c.start()
+        for c in copies:
+            c.wait()
 
     return pl.pallas_call(
         body,
@@ -557,8 +577,8 @@
             pl.BlockSpec(memory_space=pltpu.HBM),
         ],
         out_specs=pl.BlockSpec(memory_space=pltpu.VMEM),
-        out_shape=pltpu.VMEM((count, row_count, width), queries.dtype),
-        scratch_shapes=[pltpu.SemaphoreType.DMA],
+        out_shape=pltpu.VMEM((row_count, count * width), queries.dtype),
+        scratch_shapes=[pltpu.SemaphoreType.DMA((count,))],
         name="own_columns",
         compiler_params=pltpu.CompilerParams(vmem_limit_bytes=16 << 20),
     )(core_of, in_hbm(queries))
@@ -661,22 +681,25 @@
         third = move(pay, outward + inward)
         crossed = move(two, across)
         (three,) = attend(n, [third, left1, right1], (0, 2, 1, 0), (3, 0, 3, 0), ())
-        joined = merge_pair(plan, one, third, three, chips=inner)
+        joined = merge_pair(plan, one, third, three, chips=inner, width=whole_width)
         final = move(joined, across + ends)
-        paired = merge_pair(plan, three, crossed, None, chips=inner)
+        paired = merge_pair(plan, three, crossed, None, chips=inner, width=whole_width)
         home = move(paired, outward)
         arrived[n] = (final, [home, right2, left2])
-    (own,) = partial_attention(
-        plan, own_queries, (0,) * shards, tuple(range(shards)), kv_pages, twin_pages, fresh, (),
-        count=seq_dev, first=0, **common
-    )
+    own = []
+    for n in range(CHUNKS):
+        (mine,) = partial_attention(
+            plan, [own_queries[n]], (0,) * shards, tuple(range(shards)), kv_pages, twin_pages,
+            fresh[:, firsts[n] : firsts[n] + chunk], (), count=chunk, first=firsts[n], **common
+        )
+        own.append(mine)
     outs = []
     for n in range(CHUNKS):
         final, firsts_in = arrived[n]
         outs.append(
             merge_final(
-                plan, own, final, firsts_in, (0, 1, 2, 0),
-                first=firsts[n], seq_dev=seq_dev, record=record,
+                plan, own[n], final, firsts_in, (0, 1, 2, 0),
+                first=firsts[n], seq_dev=seq_dev, record=record, width=whole_width,
             )
         )
     whole = None
@@ -689,7 +712,7 @@
 def can_travel(shards, sub_count, seq_dev, query_width, page_count):
     heads = query_width // sub_count // HD
     spread = page_count >= shards * sub_count and shards == 4 and sub_count == 2
-    return spread and 3 * heads <= LANES and seq_dev % CHUNKS == 0
+    return spread and seq_dev % CHUNKS == 0 and 3 * heads * (seq_dev // CHUNKS) <= LANES
 
 
 def solution(mesh):

time: 151 us -> 147 us (0.974)
  waiting for transfers between devices: 70.1 us -> 66.5 us
    ppermute x16, waiting for transfers between devices: 69.2 us -> 65.6 us  [move(): return lax.ppermute(array, 'seq', pairs)]
    pallas_call x7 -> x8, Pallas kernels: 29.3 us -> 31.4 us  [partial_attention(): pl.pallas_call(body, in_specs=[pl.BlockSpec(memory_space=pltpu.SMEM)] + i...]
  transfers between devices with their start and end apart: 19 -> 19, of which waited for: 11 -> 11; matrix products, arithmetic and copies ran while one was open for 1% -> 1% of each run, Pallas kernels for 28% -> 30%
where the time goes in v3:
time: 147 us; the launch traced here: 146 us
  waiting for transfers between devices  66.5 us (45%)
  Pallas kernels  46 us (31%)
  starting transfers between devices  28.3 us (19%)
  local copies, waits for them, and re-layouts  4.12 us (3%)
    ppermute x16, waiting for transfers between devices, move(): return lax.ppermute(array, 'seq', pairs)  65.6 us
    pallas_call x8, Pallas kernels, partial_attention(): pl.pallas_call(body, in_specs=[pl.BlockSpec(memory_space=pltpu.SMEM)] + i...  31.4 us
    ppermute x16, starting transfers between devices, move(): return lax.ppermute(array, 'seq', pairs)  27.7 us
    pallas_call x4, Pallas kernels, merge_pair(): pl.pallas_call(body, in_specs=[pl.BlockSpec(memory_space=pltpu.SMEM)] + [...  5.7 us
    pallas_call x2, Pallas kernels, merge_final(): pl.pallas_call(body, in_specs=[pl.BlockSpec(memory_space=pltpu.SMEM)] + [...  4.77 us
    dynamic_slice x1, local copies, waits for them, and re-layouts, queries_travel(): lax.dynamic_slice_in_dim(later_pages, (1 - core) * part_width, part_width...  3.66 us
  transfers between devices with their start and end apart: 19, of which 11 were waited for; matrix products, arithmetic and copies ran while one was open for 1% of the time, Pallas kernels for 30%

profile of v3, /device:TPU:0, one launch (start us, length us, event | category | flops | bytes accessed | tf_op | source)
XLA Modules:
  0.0 146.5 jit_solution(17513401415763810771)
XLA Ops:
  0.0 1.1 own_columns.2.rest_0_
  1.1 0.0 copy-start.9
  1.1 0.0 copy-start.10
  1.1 3.7 %constant_dynamic-slice_fusion.1 = bf16[21,2,128,256]{3,2,1,0:T(8,128)(2,1)} fusion(bf16[21,2,128,512]{3,2,1,0:T(8,128)(2,1)} %rest_3_.3, s32[]{:T(128)S(6)} %select_n.49), kind=kLoop, calls=%fused_computation.27 | loop fusion | bytes 5505028 | tf_op jit(solution)/shard_map/dynamic_slice | solution.py:646
  4.8 0.5 collective-permute-start
  5.3 4.6 %collective-permute-start.1 = (bf16[64,4096]{1,0:T(8,128)(2,1)S(1)}, bf16[64,4096]{1,0:T(8,128)(2,1)S(1)}, u32[]{:S(2)}, u32[]{:S(2)}) collective-permute-start(bf16[64,4096]{1,0:T(8,128)(2,1)S(1)} %own_columns.2.rest_0_), channel_id=1, source_target_pairs={{0,4},{4,8},{8,12},{1,5},{5,9},{9,13},{2,6},{6,10},{10,14},{3,7},{... | collective-permute-start | bytes 1572872 | tf_op jit(solution)/shard_map/ppermute | solution.py:662
  9.9 1.3 collective-permute-start.2
  11.2 1.1 own_columns.3.rest_0_
  12.3 4.6 %collective-permute-start.10 = (bf16[64,4096]{1,0:T(8,128)(2,1)S(1)}, bf16[64,4096]{1,0:T(8,128)(2,1)S(1)}, u32[]{:S(2)}, u32[]{:S(2)}) collective-permute-start(bf16[64,4096]{1,0:T(8,128)(2,1)S(1)} %own_columns.3.rest_0_), channel_id=1, source_target_pairs={{0,4},{4,8},{8,12},{1,5},{5,9},{9,13},{2,6},{6,10},{10,14},{3,7},{... | collective-permute-start | bytes 1572872 | tf_op jit(solution)/shard_map/ppermute | solution.py:662
  16.9 1.3 collective-permute-start.11
  18.3 0.1 fusion.2
  18.3 0.4 convert_reduce_fusion
  18.8 0.1 broadcast_compare_fusion
  18.8 0.2 fusion
  19.1 0.1 copy.11
  19.2 0.1 reshape.86
  19.3 0.1 pad_add_fusion.1.plan_ref
  19.3 13.5 %collective-permute-done.10.rest_0_.rest_2_ = bf16[64,4096]{1,0:T(8,128)(2,1)S(1)} collective-permute-done((bf16[64,4096]{1,0:T(8,128)(2,1)S(1)}, bf16[64,4096]{1,0:T(8,128)(2,1)S(1)}, u32[]{:S(2)}, u32[]{:S(2)}) %collective-permute-start.10) | collective-permute-done | bytes 524320 | tf_op jit(solution)/shard_map/ppermute | solution.py:662
  32.8 4.1 %collective-permute-done.11.rest_1_ = bf16[64,4096]{1,0:T(8,128)(2,1)S(1)} collective-permute-done((bf16[64,4096]{1,0:T(8,128)(2,1)S(1)}, bf16[64,4096]{1,0:T(8,128)(2,1)S(1)}, u32[]{:S(2)}, u32[]{:S(2)}) %collective-permute-start.11) | collective-permute-done | bytes 524320 | tf_op jit(solution)/shard_map/ppermute | solution.py:662
  37.0 0.0 collective-permute-done.rest_2_.rest_3_.rest_4_
  37.0 4.1 %partial_attention.13 = (bf16[64,4224]{1,0:T(8,128)(2,1)S(1)}, bf16[64,4224]{1,0:T(8,128)(2,1)S(1)}, bf16[64,4224]{1,0:T(8,128)(2,1)S(1)}) custom-call(s32[146]{0:T(256)S(1)} %pad_add_fusion.1.plan_ref, bf16[64,4096]{1,0:T(8,128)(2,1)S(1)} %collective-permute-done.10.rest_0_.rest_2_, bf16[64,4096]{1,0:T(8,128)(2,1)S(1)} %collective-permute-done.11.rest_1_, ...), custom_call_target="tpu_custom_call" | custom-call | flops 536870912 | bytes 2097152 | tf_op jit(solution)/shard_map/partial_attention/pallas_call | solution.py:427
  41.1 3.5 %collective-permute-start.12 = (bf16[64,4224]{1,0:T(8,128)(2,1)S(1)}, bf16[64,4224]{1,0:T(8,128)(2,1)S(1)}, u32[]{:S(2)}, u32[]{:S(2)}) collective-permute-start(bf16[64,4224]{1,0:T(8,128)(2,1)S(1)} %get-tuple-element.23), channel_id=1, source_target_pairs={{0,4},{4,8},{8,12},{1,5},{5,9},{9,13},{2,6},{6,10},{10,14},{3,7},{... | collective-permute-start | bytes 1622024 | tf_op jit(solution)/shard_map/ppermute | solution.py:662
  44.6 1.3 collective-permute-start.13
  45.9 0.0 copy-start.3
  45.9 0.0 collective-permute-done.2.rest_1_
  45.9 4.8 %partial_attention.9 = (bf16[64,4224]{1,0:T(8,128)(2,1)S(1)}, bf16[64,4224]{1,0:T(8,128)(2,1)S(1)}, bf16[64,4224]{1,0:T(8,128)(2,1)S(1)}) custom-call(s32[146]{0:T(256)S(1)} %pad_add_fusion.1.plan_ref, bf16[64,4096]{1,0:T(8,128)(2,1)S(1)} %collective-permute-done.1.rest_0_.rest_2_, bf16[64,4096]{1,0:T(8,128)(2,1)} %collective-permute-done.2.rest_1_, ...), custom_call_target="tpu_custom_call" | custom-call | flops 536870912 | bytes 2097152 | tf_op jit(solution)/shard_map/partial_attention/pallas_call | solution.py:427
  50.8 3.8 %collective-permute-start.3 = (bf16[64,4224]{1,0:T(8,128)(2,1)S(1)}, bf16[64,4224]{1,0:T(8,128)(2,1)S(1)}, u32[]{:S(2)}, u32[]{:S(2)}) collective-permute-start(bf16[64,4224]{1,0:T(8,128)(2,1)S(1)} %get-tuple-element.18), channel_id=1, source_target_pairs={{0,4},{4,8},{8,12},{1,5},{5,9},{9,13},{2,6},{6,10},{10,14},{3,7},{... | collective-permute-start | bytes 1622024 | tf_op jit(solution)/shard_map/ppermute | solution.py:662
  54.6 1.3 collective-permute-start.4
  55.9 1.4 collective-permute-done.12.rest_0_.rest_1_
  57.2 4.1 %collective-permute-done.13.rest_1_.rest_2_ = bf16[64,4224]{1,0:T(8,128)(2,1)S(1)} collective-permute-done((bf16[64,4224]{1,0:T(8,128)(2,1)S(1)}, bf16[64,4224]{1,0:T(8,128)(2,1)S(1)}, u32[]{:S(2)}, u32[]{:S(2)}) %collective-permute-start.13) | collective-permute-done | bytes 540704 | tf_op jit(solution)/shard_map/ppermute | solution.py:662
  61.3 4.1 %partial_attention.14 = (bf16[64,4224]{1,0:T(8,128)(2,1)S(1)}, bf16[64,4224]{1,0:T(8,128)(2,1)S(1)}) custom-call(s32[146]{0:T(256)S(1)} %pad_add_fusion.1.plan_ref, bf16[64,4224]{1,0:T(8,128)(2,1)S(1)} %collective-permute-done.12.rest_0_.rest_1_, bf16[64,4224]{1,0:T(8,128)(2,1)S(1)} %collective-permute-done.13.rest_1_.rest_2_, ...), custom_call_target="tpu_custom_call" | custom-call | flops 536870912 | bytes 2097152 | tf_op jit(solution)/shard_map/partial_attention/pallas_call | solution.py:427
  65.4 0.6 collective-permute-start.14
  66.0 0.8 collective-permute-start.16
  66.8 2.0 %collective-permute-done.3.rest_0_.rest_1_ = bf16[64,4224]{1,0:T(8,128)(2,1)S(1)} collective-permute-done((bf16[64,4224]{1,0:T(8,128)(2,1)S(1)}, bf16[64,4224]{1,0:T(8,128)(2,1)S(1)}, u32[]{:S(2)}, u32[]{:S(2)}) %collective-permute-start.3) | collective-permute-done | bytes 540704 | tf_op jit(solution)/shard_map/ppermute | solution.py:662
  68.8 4.1 %collective-permute-done.4.rest_1_.rest_2_ = bf16[64,4224]{1,0:T(8,128)(2,1)S(1)} collective-permute-done((bf16[64,4224]{1,0:T(8,128)(2,1)S(1)}, bf16[64,4224]{1,0:T(8,128)(2,1)S(1)}, u32[]{:S(2)}, u32[]{:S(2)}) %collective-permute-start.4) | collective-permute-done | bytes 540704 | tf_op jit(solution)/shard_map/ppermute | solution.py:662
  72.9 3.3 %partial_attention.10 = (bf16[64,4224]{1,0:T(8,128)(2,1)S(1)}, bf16[64,4224]{1,0:T(8,128)(2,1)S(1)}) custom-call(s32[146]{0:T(256)S(1)} %pad_add_fusion.1.plan_ref, bf16[64,4224]{1,0:T(8,128)(2,1)S(1)} %collective-permute-done.3.rest_0_.rest_1_, bf16[64,4224]{1,0:T(8,128)(2,1)S(1)} %collective-permute-done.4.rest_1_.rest_2_, ...), custom_call_target="tpu_custom_call" | custom-call | flops 536870912 | bytes 2097152 | tf_op jit(solution)/shard_map/partial_attention/pallas_call | solution.py:427
  76.2 1.4 collective-permute-start.5
  77.5 0.7 collective-permute-start.7
  78.2 6.2 %collective-permute-done.14.rest_0_.rest_1_ = bf16[64,4224]{1,0:T(8,128)(2,1)S(1)} collective-permute-done((bf16[64,4224]{1,0:T(8,128)(2,1)S(1)}, bf16[64,4224]{1,0:T(8,128)(2,1)S(1)}, u32[]{:S(2)}, u32[]{:S(2)}) %collective-permute-start.14) | collective-permute-done | bytes 540704 | tf_op jit(solution)/shard_map/ppermute | solution.py:662
  84.5 3.3 %partial_attention.15.rest_2_.rest_0_ = bf16[64,4224]{1,0:T(8,128)(2,1)S(1)} custom-call(s32[146]{0:T(256)S(1)} %pad_add_fusion.1.plan_ref, bf16[64,4224]{1,0:T(8,128)(2,1)S(1)} %collective-permute-done.14.rest_0_.rest_1_, bf16[64,4096]{1,0:T(8,128)(2,1)S(1)} %copy-done.8, bf16[64,4096]{1,0:T(8,128)(2,1)S(1)} %copy-done.6, ...), custom_call_target="tpu_custom_call" | custom-call | flops 536870912 | bytes 2097152 | tf_op jit(solution)/shard_map/partial_attention/pallas_call | solution.py:427
  87.8 0.0 copy-start.4
  87.8 1.4 merge_pair.6
  89.2 0.1 collective-permute-start.15
  89.3 0.0 collective-permute-done.16.rest_1_
  89.3 1.6 %merge_pair.7 = bf16[64,4224]{1,0:T(8,128)(2,1)} custom-call(s32[146]{0:T(256)S(1)} %pad_add_fusion.1.plan_ref, bf16[64,4224]{1,0:T(8,128)(2,1)S(1)} %partial_attention.15.rest_2_.rest_0_, bf16[64,4224]{1,0:T(8,128)(2,1)S(1)} %collective-permute-done.16.rest_1_), custom_call_target="tpu_custom_call" | custom-call | tf_op jit(solution)/shard_map/merge_pair/pallas_call | solution.py:496
  90.8 1.3 collective-permute-start.17
  92.1 20.9 %collective-permute-done.5.rest_0_.rest_1_ = bf16[64,4224]{1,0:T(8,128)(2,1)S(1)} collective-permute-done((bf16[64,4224]{1,0:T(8,128)(2,1)S(1)}, bf16[64,4224]{1,0:T(8,128)(2,1)S(1)}, u32[]{:S(2)}, u32[]{:S(2)}) %collective-permute-start.5) | collective-permute-done | bytes 540704 | tf_op jit(solution)/shard_map/ppermute | solution.py:662
  113.1 3.7 %partial_attention.11.rest_2_.rest_0_ = bf16[64,4224]{1,0:T(8,128)(2,1)S(1)} custom-call(s32[146]{0:T(256)S(1)} %pad_add_fusion.1.plan_ref, bf16[64,4224]{1,0:T(8,128)(2,1)S(1)} %collective-permute-done.5.rest_0_.rest_1_, bf16[64,4096]{1,0:T(8,128)(2,1)} %collective-permute-done.2.rest_1_, bf16[64,4096]{1,0:T(8,128)(2,1)S(1)} %copy-done.4, ...), custom_call_target="tpu_custom_call" | custom-call | flops 536870912 | bytes 2097152 | tf_op jit(solution)/shard_map/partial_attention/pallas_call | solution.py:427
  116.8 1.4 merge_pair.4
  118.1 0.0 collective-permute-start.6
  118.2 1.3 merge_pair.5
  119.5 1.3 collective-permute-start.8
  120.8 0.2 constant_dynamic-slice_fusion
  121.1 4.7 %partial_attention.8.own_ref = bf16[64,4224]{1,0:T(8,128)(2,1)S(1)} custom-call(s32[146]{0:T(256)S(1)} %pad_add_fusion.1.plan_ref, bf16[64,4096]{1,0:T(8,128)(2,1)S(1)} %own_columns.2.rest_0_, bf16[21,2,128,512]{3,2,1,0:T(8,128)(2,1)} %rest_3_.3, bf16[21,2,128,256]{3,2,1,0:T(8,128)(2,1)} %collective-permute-done.rest_2_.rest_3_.rest_4_, ...), custom_call_target="tpu_custom_call" | custom-call | flops 536870912 | bytes 2097152 | tf_op jit(solution)/shard_map/partial_attention/pallas_call | solution.py:427
  125.8 3.4 %partial_attention.12.own_ref = bf16[64,4224]{1,0:T(8,128)(2,1)S(1)} custom-call(s32[146]{0:T(256)S(1)} %pad_add_fusion.1.plan_ref, bf16[64,4096]{1,0:T(8,128)(2,1)S(1)} %copy-done.2, bf16[21,2,128,512]{3,2,1,0:T(8,128)(2,1)} %rest_3_.3, bf16[21,2,128,256]{3,2,1,0:T(8,128)(2,1)} %collective-permute-done.rest_2_.rest_3_.rest_4_, ...), custom_call_target="tpu_custom_call" | custom-call | flops 536870912 | bytes 2097152 | tf_op jit(solution)/shard_map/partial_attention/pallas_call | solution.py:427
  129.2 1.3 collective-permute-done.17.rest_0_
  130.5 2.3 %merge_final.3.own_ref = bf16[2,64,2048]{2,1,0:T(8,128)(2,1)S(1)} custom-call(s32[146]{0:T(256)S(1)} %pad_add_fusion.1.plan_ref, bf16[64,4224]{1,0:T(8,128)(2,1)S(1)} %partial_attention.12.own_ref, bf16[64,4224]{1,0:T(8,128)(2,1)} %collective-permute-done.15.last_ref, bf16[64,4224]{1,0:T(8,128)(2,1)} %collective-permute-done.17.rest_0_, ...), custom_call_target="tpu_custom_call" | custom-call | tf_op jit(solution)/shard_map/merge_final/pallas_call | solution.py:542
  132.8 0.1 collective-permute-start.18
  132.9 7.9 %collective-permute-done.8.rest_0_ = bf16[64,4224]{1,0:T(8,128)(2,1)} collective-permute-done((bf16[64,4224]{1,0:T(8,128)(2,1)}, bf16[64,4224]{1,0:T(8,128)(2,1)}, u32[]{:S(2)}, u32[]{:S(2)}) %collective-permute-start.8) | collective-permute-done | bytes 540704 | tf_op jit(solution)/shard_map/ppermute | solution.py:662
  140.9 2.5 %merge_final.2.own_ref = bf16[2,64,2048]{2,1,0:T(8,128)(2,1)S(1)} custom-call(s32[146]{0:T(256)S(1)} %pad_add_fusion.1.plan_ref, bf16[64,4224]{1,0:T(8,128)(2,1)S(1)} %partial_attention.8.own_ref, bf16[64,4224]{1,0:T(8,128)(2,1)} %collective-permute-done.6.last_ref, bf16[64,4224]{1,0:T(8,128)(2,1)} %collective-permute-done.8.rest_0_, ...), custom_call_target="tpu_custom_call" | custom-call | tf_op jit(solution)/shard_map/merge_final/pallas_call | solution.py:542
  143.4 0.1 collective-permute-start.9
  143.4 1.0 place_columns.2.rest_0_
  144.4 0.9 collective-permute-done.9.other_ref
  145.3 1.0 place_columns.3
  (32 shorter events, 0.1 us)
Async XLA Ops:
  0.0 120.8 %copy-start = (bf16[4,64,2,512]{3,2,1,0:T(2,128)(2,1)S(1)}, bf16[4,64,2,512]{3,2,1,0:T(2,128)(2,1)}, u32[]{:S(2)}) copy-start(bf16[4,64,2,512]{3,2,1,0:T(2,128)(2,1)} %param.7) | copy-start | bytes 1572868
  1.1 17.1 %copy-start.9 = (s32[16,16]{1,0:T(8,128)S(1)}, s32[16,16]{1,0:T(8,128)}, u32[]{:S(2)}) copy-start(s32[16,16]{1,0:T(8,128)} %param.9) | copy-start | bytes 3076
  1.1 17.1 %copy-start.10 = (s32[16]{0:T(128)S(1)}, s32[16]{0:T(128)}, u32[]{:S(2)}) copy-start(s32[16]{0:T(128)} %param.10) | copy-start | bytes 196
  4.8 14.3 %copy-start.11 = (s32[16]{0:T(128)S(1)}, s32[16]{0:T(128)}, u32[]{:S(2)}) copy-start(s32[16]{0:T(128)} %param.11) | copy-start | bytes 196
  4.8 32.2 %collective-permute-start = (bf16[21,2,128,256]{3,2,1,0:T(8,128)(2,1)}, bf16[21,2,128,256]{3,2,1,0:T(8,128)(2,1)}, u32[]{:S(2)}, u32[]{:S(2)}) collective-permute-start(bf16[21,2,128,256]{3,2,1,0:T(8,128)(2,1)} %constant_dynamic-slice_fusion.1), channel_id=1, source_target_pairs={{0,1},{1,0},{2,3},{3,2},{4,5},{5,4},{6,7},{7,6},{8,9},{9,8},{10,11... | collective-permute-start | bytes 8257544 | tf_op jit(solution)/shard_map/ppermute | solution.py:647
  5.3 40.6 %collective-permute-start.1 = (bf16[64,4096]{1,0:T(8,128)(2,1)S(1)}, bf16[64,4096]{1,0:T(8,128)(2,1)S(1)}, u32[]{:S(2)}, u32[]{:S(2)}) collective-permute-start(bf16[64,4096]{1,0:T(8,128)(2,1)S(1)} %own_columns.2.rest_0_), channel_id=1, source_target_pairs={{0,4},{4,8},{8,12},{1,5},{5,9},{9,13},{2,6},{6,10},{10,14},{3,7},{... | collective-permute-start | bytes 1572872 | tf_op jit(solution)/shard_map/ppermute | solution.py:662
  9.9 36.0 %collective-permute-start.2 = (bf16[64,4096]{1,0:T(8,128)(2,1)S(1)}, bf16[64,4096]{1,0:T(8,128)(2,1)}, u32[]{:S(2)}, u32[]{:S(2)}) collective-permute-start(bf16[64,4096]{1,0:T(8,128)(2,1)S(1)} %own_columns.2.rest_0_), channel_id=1, source_target_pairs={{12,8},{8,4},{4,0},{13,9},{9,5},{5,1},{14,10},{10,6},{6,2},{15,11}... | collective-permute-start | bytes 1572872 | tf_op jit(solution)/shard_map/ppermute | solution.py:662
  12.3 28.8 %copy-start.1 = (bf16[64,4096]{1,0:T(8,128)(2,1)}, bf16[64,4096]{1,0:T(8,128)(2,1)S(1)}, u32[]{:S(2)}) copy-start(bf16[64,4096]{1,0:T(8,128)(2,1)S(1)} %own_columns.3.rest_0_) | copy-start | bytes 1572868
  12.3 20.5 %collective-permute-start.10 = (bf16[64,4096]{1,0:T(8,128)(2,1)S(1)}, bf16[64,4096]{1,0:T(8,128)(2,1)S(1)}, u32[]{:S(2)}, u32[]{:S(2)}) collective-permute-start(bf16[64,4096]{1,0:T(8,128)(2,1)S(1)} %own_columns.3.rest_0_), channel_id=1, source_target_pairs={{0,4},{4,8},{8,12},{1,5},{5,9},{9,13},{2,6},{6,10},{10,14},{3,7},{... | collective-permute-start | bytes 1572872 | tf_op jit(solution)/shard_map/ppermute | solution.py:662
  16.9 20.1 %collective-permute-start.11 = (bf16[64,4096]{1,0:T(8,128)(2,1)S(1)}, bf16[64,4096]{1,0:T(8,128)(2,1)S(1)}, u32[]{:S(2)}, u32[]{:S(2)}) collective-permute-start(bf16[64,4096]{1,0:T(8,128)(2,1)S(1)} %own_columns.3.rest_0_), channel_id=1, source_target_pairs={{12,8},{8,4},{4,0},{13,9},{9,5},{5,1},{14,10},{10,6},{6,2},{15,11}... | collective-permute-start | bytes 1572872 | tf_op jit(solution)/shard_map/ppermute | solution.py:662
  32.8 8.3 %copy-start.5 = (bf16[64,4096]{1,0:T(8,128)(2,1)}, bf16[64,4096]{1,0:T(8,128)(2,1)S(1)}, u32[]{:S(2)}) copy-start(bf16[64,4096]{1,0:T(8,128)(2,1)S(1)} %collective-permute-done.10.rest_0_.rest_2_) | copy-start | bytes 1572868
  37.0 4.2 %copy-start.7 = (bf16[64,4096]{1,0:T(8,128)(2,1)}, bf16[64,4096]{1,0:T(8,128)(2,1)S(1)}, u32[]{:S(2)}) copy-start(bf16[64,4096]{1,0:T(8,128)(2,1)S(1)} %collective-permute-done.11.rest_1_) | copy-start | bytes 1572868
  41.1 16.1 %collective-permute-start.12 = (bf16[64,4224]{1,0:T(8,128)(2,1)S(1)}, bf16[64,4224]{1,0:T(8,128)(2,1)S(1)}, u32[]{:S(2)}, u32[]{:S(2)}) collective-permute-start(bf16[64,4224]{1,0:T(8,128)(2,1)S(1)} %get-tuple-element.23), channel_id=1, source_target_pairs={{0,4},{4,8},{8,12},{1,5},{5,9},{9,13},{2,6},{6,10},{10,14},{3,7},{... | collective-permute-start | bytes 1622024 | tf_op jit(solution)/shard_map/ppermute | solution.py:662
  44.6 16.7 %collective-permute-start.13 = (bf16[64,4224]{1,0:T(8,128)(2,1)S(1)}, bf16[64,4224]{1,0:T(8,128)(2,1)S(1)}, u32[]{:S(2)}, u32[]{:S(2)}) collective-permute-start(bf16[64,4224]{1,0:T(8,128)(2,1)S(1)} %get-tuple-element.24), channel_id=1, source_target_pairs={{12,8},{8,4},{4,0},{13,9},{9,5},{5,1},{14,10},{10,6},{6,2},{15,11}... | collective-permute-start | bytes 1622024 | tf_op jit(solution)/shard_map/ppermute | solution.py:662
  45.9 4.8 %copy-start.3 = (bf16[64,4096]{1,0:T(8,128)(2,1)}, bf16[64,4096]{1,0:T(8,128)(2,1)S(1)}, u32[]{:S(2)}) copy-start(bf16[64,4096]{1,0:T(8,128)(2,1)S(1)} %collective-permute-done.1.rest_0_.rest_2_) | copy-start | bytes 1572868
  50.8 18.0 %collective-permute-start.3 = (bf16[64,4224]{1,0:T(8,128)(2,1)S(1)}, bf16[64,4224]{1,0:T(8,128)(2,1)S(1)}, u32[]{:S(2)}, u32[]{:S(2)}) collective-permute-start(bf16[64,4224]{1,0:T(8,128)(2,1)S(1)} %get-tuple-element.18), channel_id=1, source_target_pairs={{0,4},{4,8},{8,12},{1,5},{5,9},{9,13},{2,6},{6,10},{10,14},{3,7},{... | collective-permute-start | bytes 1622024 | tf_op jit(solution)/shard_map/ppermute | solution.py:662
  54.6 18.3 %collective-permute-start.4 = (bf16[64,4224]{1,0:T(8,128)(2,1)S(1)}, bf16[64,4224]{1,0:T(8,128)(2,1)S(1)}, u32[]{:S(2)}, u32[]{:S(2)}) collective-permute-start(bf16[64,4224]{1,0:T(8,128)(2,1)S(1)} %get-tuple-element.19), channel_id=1, source_target_pairs={{12,8},{8,4},{4,0},{13,9},{9,5},{5,1},{14,10},{10,6},{6,2},{15,11}... | collective-permute-start | bytes 1622024 | tf_op jit(solution)/shard_map/ppermute | solution.py:662
  65.4 19.1 %collective-permute-start.14 = (bf16[64,4224]{1,0:T(8,128)(2,1)S(1)}, bf16[64,4224]{1,0:T(8,128)(2,1)S(1)}, u32[]{:S(2)}, u32[]{:S(2)}) collective-permute-start(bf16[64,4224]{1,0:T(8,128)(2,1)S(1)} %get-tuple-element.25), channel_id=1, source_target_pairs={{8,12},{4,0},{12,8},{0,4},{9,13},{5,1},{13,9},{1,5},{10,14},{6,2},... | collective-permute-start | bytes 1622024 | tf_op jit(solution)/shard_map/ppermute | solution.py:662
  66.0 18.5 %copy-start.6 = (bf16[64,4096]{1,0:T(8,128)(2,1)S(1)}, bf16[64,4096]{1,0:T(8,128)(2,1)}, u32[]{:S(2)}) copy-start(bf16[64,4096]{1,0:T(8,128)(2,1)} %copy-done.5) | copy-start | bytes 1572868
  66.0 18.5 %copy-start.8 = (bf16[64,4096]{1,0:T(8,128)(2,1)S(1)}, bf16[64,4096]{1,0:T(8,128)(2,1)}, u32[]{:S(2)}) copy-start(bf16[64,4096]{1,0:T(8,128)(2,1)} %copy-done.7) | copy-start | bytes 1572868
  66.0 23.3 %collective-permute-start.16 = (bf16[64,4224]{1,0:T(8,128)(2,1)S(1)}, bf16[64,4224]{1,0:T(8,128)(2,1)S(1)}, u32[]{:S(2)}, u32[]{:S(2)}) collective-permute-start(bf16[64,4224]{1,0:T(8,128)(2,1)S(1)} %get-tuple-element.26), channel_id=1, source_target_pairs={{4,8},{8,4},{5,9},{9,5},{6,10},{10,6},{7,11},{11,7},{20,24},{24,20... | collective-permute-start | bytes 1622024 | tf_op jit(solution)/shard_map/ppermute | solution.py:662
  76.2 36.9 %collective-permute-start.5 = (bf16[64,4224]{1,0:T(8,128)(2,1)S(1)}, bf16[64,4224]{1,0:T(8,128)(2,1)S(1)}, u32[]{:S(2)}, u32[]{:S(2)}) collective-permute-start(bf16[64,4224]{1,0:T(8,128)(2,1)S(1)} %get-tuple-element.20), channel_id=1, source_target_pairs={{8,12},{4,0},{12,8},{0,4},{9,13},{5,1},{13,9},{1,5},{10,14},{6,2},... | collective-permute-start | bytes 1622024 | tf_op jit(solution)/shard_map/ppermute | solution.py:662
  77.5 40.6 %collective-permute-start.7 = (bf16[64,4224]{1,0:T(8,128)(2,1)S(1)}, bf16[64,4224]{1,0:T(8,128)(2,1)S(1)}, u32[]{:S(2)}, u32[]{:S(2)}) collective-permute-start(bf16[64,4224]{1,0:T(8,128)(2,1)S(1)} %get-tuple-element.21), channel_id=1, source_target_pairs={{4,8},{8,4},{5,9},{9,5},{6,10},{10,6},{7,11},{11,7},{20,24},{24,20... | collective-permute-start | bytes 1622024 | tf_op jit(solution)/shard_map/ppermute | solution.py:662
  87.8 25.3 %copy-start.4 = (bf16[64,4096]{1,0:T(8,128)(2,1)S(1)}, bf16[64,4096]{1,0:T(8,128)(2,1)}, u32[]{:S(2)}) copy-start(bf16[64,4096]{1,0:T(8,128)(2,1)} %copy-done.3) | copy-start | bytes 1572868
  89.2 40.0 %collective-permute-start.15 = (bf16[64,4224]{1,0:T(8,128)(2,1)}, bf16[64,4224]{1,0:T(8,128)(2,1)}, u32[]{:S(2)}, u32[]{:S(2)}) collective-permute-start(bf16[64,4224]{1,0:T(8,128)(2,1)} %merge_pair.6), channel_id=1, source_target_pairs={{4,8},{8,4},{12,0},{0,12},{5,9},{9,5},{13,1},{1,13},{6,10},{10,6},... | collective-permute-start | bytes 1622024 | tf_op jit(solution)/shard_map/ppermute | solution.py:662
  90.8 39.7 %collective-permute-start.17 = (bf16[64,4224]{1,0:T(8,128)(2,1)}, bf16[64,4224]{1,0:T(8,128)(2,1)}, u32[]{:S(2)}, u32[]{:S(2)}) collective-permute-start(bf16[64,4224]{1,0:T(8,128)(2,1)} %merge_pair.7), channel_id=1, source_target_pairs={{8,12},{4,0},{9,13},{5,1},{10,14},{6,2},{11,15},{7,3},{24,28},{20,... | collective-permute-start | bytes 1622024 | tf_op jit(solution)/shard_map/ppermute | solution.py:662
  118.1 14.8 %collective-permute-start.6 = (bf16[64,4224]{1,0:T(8,128)(2,1)}, bf16[64,4224]{1,0:T(8,128)(2,1)}, u32[]{:S(2)}, u32[]{:S(2)}) collective-permute-start(bf16[64,4224]{1,0:T(8,128)(2,1)} %merge_pair.4), channel_id=1, source_target_pairs={{4,8},{8,4},{12,0},{0,12},{5,9},{9,5},{13,1},{1,13},{6,10},{10,6},... | collective-permute-start | bytes 1622024 | tf_op jit(solution)/shard_map/ppermute | solution.py:662
  119.5 21.3 %collective-permute-start.8 = (bf16[64,4224]{1,0:T(8,128)(2,1)}, bf16[64,4224]{1,0:T(8,128)(2,1)}, u32[]{:S(2)}, u32[]{:S(2)}) collective-permute-start(bf16[64,4224]{1,0:T(8,128)(2,1)} %merge_pair.5), channel_id=1, source_target_pairs={{8,12},{4,0},{9,13},{5,1},{10,14},{6,2},{11,15},{7,3},{24,28},{20,... | collective-permute-start | bytes 1622024 | tf_op jit(solution)/shard_map/ppermute | solution.py:662
  121.1 4.7 %copy-start.2 = (bf16[64,4096]{1,0:T(8,128)(2,1)S(1)}, bf16[64,4096]{1,0:T(8,128)(2,1)}, u32[]{:S(2)}) copy-start(bf16[64,4096]{1,0:T(8,128)(2,1)} %copy-done.1) | copy-start | bytes 1572868
  132.8 10.6 %collective-permute-start.18 = (bf16[2,64,2048]{2,1,0:T(8,128)(2,1)S(1)}, bf16[2,64,2048]{2,1,0:T(8,128)(2,1)S(1)}, u32[]{:S(2)}, u32[]{:S(2)}) collective-permute-start(bf16[2,64,2048]{2,1,0:T(8,128)(2,1)S(1)} %merge_final.3.own_ref), channel_id=1, source_target_pairs={{0,1},{1,0},{2,3},{3,2},{4,5},{5,4},{6,7},{7,6},{8,9},{9,8},{10,11... | collective-permute-start | bytes 1572872 | tf_op jit(solution)/shard_map/ppermute | solution.py:707
  143.4 2.0 %collective-permute-start.9 = (bf16[2,64,2048]{2,1,0:T(8,128)(2,1)S(1)}, bf16[2,64,2048]{2,1,0:T(8,128)(2,1)S(1)}, u32[]{:S(2)}, u32[]{:S(2)}) collective-permute-start(bf16[2,64,2048]{2,1,0:T(8,128)(2,1)S(1)} %merge_final.2.own_ref), channel_id=1, source_target_pairs={{0,1},{1,0},{2,3},{3,2},{4,5},{5,4},{6,7},{7,6},{8,9},{9,8},{10,11... | collective-permute-start | bytes 1572872 | tf_op jit(solution)/shard_map/ppermute | solution.py:707

commit v4 on v3

--- a/solution.py
+++ b/solution.py
@@ -661,31 +661,27 @@
     def move(array, pairs):
         return lax.ppermute(array, "seq", pairs)
 
-    up = [(0, 1), (1, 2), (2, 3)]
-    down = [(3, 2), (2, 1), (1, 0)]
-    outward = [(2, 3), (1, 0)]
-    inward = [(3, 2), (0, 1)]
+    outer = [(0, 1), (1, 0), (2, 3), (3, 2)]
     across = [(1, 2), (2, 1)]
     ends = [(3, 0), (0, 3)]
     inner = (0, 1, 1, 0)
+    relay = ((-1, 1, 1, -1),)
     arrived = {}
     for n in range(CHUNKS):
-        right1 = move(own_queries[n], up)
-        left1 = move(own_queries[n], down)
-        one, pay_right, pay_left = attend(
-            n, [right1, left1], (1, 1, 0, 0), (1, 2, 1, 2), ((-1, 0, 0, 0), (1, 1, 1, -1))
-        )
-        right2 = move(pay_right, up)
-        left2 = move(pay_left, down)
-        two, pay = attend(n, [right2, left2], (1, 1, 0, 0), (2, 3, 0, 1), ((-1, 1, 0, -1),))
-        third = move(pay, outward + inward)
+        middle1 = move(own_queries[n], across)
+        outer1 = move(own_queries[n], outer)
+        middle2 = move(outer1, across)
+        one, pay = attend(n, [outer1, middle1], inner, (1, 2, 1, 2), relay)
+        outer2 = move(pay, outer)
+        two, pay = attend(n, [outer2, middle2], inner, (2, 3, 0, 1), relay)
         crossed = move(two, across)
-        (three,) = attend(n, [third, left1, right1], (0, 2, 1, 0), (3, 0, 3, 0), ())
-        joined = merge_pair(plan, one, third, three, chips=inner, width=whole_width)
+        outer3 = move(pay, outer)
+        (three,) = attend(n, [outer3, outer1], inner, (3, 0, 3, 0), ())
+        joined = merge_pair(plan, one, outer3, three, chips=inner, width=whole_width)
         final = move(joined, across + ends)
         paired = merge_pair(plan, three, crossed, None, chips=inner, width=whole_width)
-        home = move(paired, outward)
-        arrived[n] = (final, [home, right2, left2])
+        home = move(paired, [(1, 0), (2, 3)])
+        arrived[n] = (final, [home, outer2])
     own = []
     for n in range(CHUNKS):
         (mine,) = partial_attention(
@@ -698,7 +694,7 @@
         final, firsts_in = arrived[n]
         outs.append(
             merge_final(
-                plan, own[n], final, firsts_in, (0, 1, 2, 0),
+                plan, own[n], final, firsts_in, inner,
                 first=firsts[n], seq_dev=seq_dev, record=record, width=whole_width,
             )
         )

time: 147 us -> 141 us (0.959)
  waiting for transfers between devices: 66.5 us -> 55 us
  starting transfers between devices: 28.3 us -> 34.6 us
    ppermute x16, waiting for transfers between devices: 65.6 us -> 54.1 us  [move(): return lax.ppermute(array, 'seq', pairs)]
    ppermute x16, starting transfers between devices: 27.7 us -> 34 us  [move(): return lax.ppermute(array, 'seq', pairs)]
  transfers between devices with their start and end apart: 19 -> 19, of which waited for: 11 -> 8; matrix products, arithmetic and copies ran while one was open for 1% -> 1% of each run, Pallas kernels for 30% -> 31%
where the time goes in v4:
time: 141 us; the launch traced here: 140 us
  waiting for transfers between devices  55 us (39%)
  Pallas kernels  45 us (32%)
  starting transfers between devices  34.6 us (25%)
  local copies, waits for them, and re-layouts  4.09 us (3%)
    ppermute x16, waiting for transfers between devices, move(): return lax.ppermute(array, 'seq', pairs)  54.1 us
    ppermute x16, starting transfers between devices, move(): return lax.ppermute(array, 'seq', pairs)  34 us
    pallas_call x8, Pallas kernels, partial_attention(): pl.pallas_call(body, in_specs=[pl.BlockSpec(memory_space=pltpu.SMEM)] + i...  30.7 us
    pallas_call x4, Pallas kernels, merge_pair(): pl.pallas_call(body, in_specs=[pl.BlockSpec(memory_space=pltpu.SMEM)] + [...  5.55 us
    pallas_call x2, Pallas kernels, merge_final(): pl.pallas_call(body, in_specs=[pl.BlockSpec(memory_space=pltpu.SMEM)] + [...  4.56 us
    dynamic_slice x1, local copies, waits for them, and re-layouts, queries_travel(): lax.dynamic_slice_in_dim(later_pages, (1 - core) * part_width, part_width...  3.66 us
  transfers between devices with their start and end apart: 19, of which 8 were waited for; matrix products, arithmetic and copies ran while one was open for 1% of the time, Pallas kernels for 31%

profile of v4, /device:TPU:0, one launch (start us, length us, event | category | flops | bytes accessed | tf_op | source)
XLA Modules:
  0.0 140.1 jit_solution(10123522057257292468)
XLA Ops:
  0.0 1.1 own_columns.2.rest_0_
  1.1 0.0 copy-start.3
  1.1 0.0 copy-start.4
  1.1 3.7 %constant_dynamic-slice_fusion.1 = bf16[21,2,128,256]{3,2,1,0:T(8,128)(2,1)} fusion(bf16[21,2,128,512]{3,2,1,0:T(8,128)(2,1)} %rest_2_.11, s32[]{:T(128)S(6)} %select_n.49), kind=kLoop, calls=%fused_computation.27 | loop fusion | bytes 5505028 | tf_op jit(solution)/shard_map/dynamic_slice | solution.py:646
  4.8 0.5 collective-permute-start
  5.3 2.6 %collective-permute-start.1 = (bf16[64,4096]{1,0:T(8,128)(2,1)S(1)}, bf16[64,4096]{1,0:T(8,128)(2,1)S(1)}, u32[]{:S(2)}, u32[]{:S(2)}) collective-permute-start(bf16[64,4096]{1,0:T(8,128)(2,1)S(1)} %own_columns.2.rest_0_), channel_id=1, source_target_pairs={{0,4},{4,0},{8,12},{12,8},{1,5},{5,1},{9,13},{13,9},{2,6},{6,2},{1... | collective-permute-start | bytes 1572872 | tf_op jit(solution)/shard_map/ppermute | solution.py:662
  7.9 0.7 collective-permute-start.2
  8.6 1.1 own_columns.3.rest_0_
  9.6 4.4 %collective-permute-start.10 = (bf16[64,4096]{1,0:T(8,128)(2,1)S(1)}, bf16[64,4096]{1,0:T(8,128)(2,1)S(1)}, u32[]{:S(2)}, u32[]{:S(2)}) collective-permute-start(bf16[64,4096]{1,0:T(8,128)(2,1)S(1)} %own_columns.3.rest_0_), channel_id=1, source_target_pairs={{0,4},{4,0},{8,12},{12,8},{1,5},{5,1},{9,13},{13,9},{2,6},{6,2},{1... | collective-permute-start | bytes 1572872 | tf_op jit(solution)/shard_map/ppermute | solution.py:662
  14.1 1.4 %collective-permute-start.11 = (bf16[64,4096]{1,0:T(8,128)(2,1)S(1)}, bf16[64,4096]{1,0:T(8,128)(2,1)}, u32[]{:S(2)}, u32[]{:S(2)}) collective-permute-start(bf16[64,4096]{1,0:T(8,128)(2,1)S(1)} %own_columns.3.rest_0_), channel_id=1, source_target_pairs={{4,8},{8,4},{5,9},{9,5},{6,10},{10,6},{7,11},{11,7},{20,24},{24,20... | collective-permute-start | bytes 1572872 | tf_op jit(solution)/shard_map/ppermute | solution.py:662
  15.5 0.1 fusion.2
  15.6 0.4 convert_reduce_fusion
  16.1 0.1 broadcast_compare_fusion
  16.1 0.2 fusion
  16.4 0.1 copy.11
  16.5 0.1 reshape.86
  16.6 0.1 pad_add_fusion.1.plan_ref
  16.6 15.1 %collective-permute-done.10.rest_0_.rest_1_ = bf16[64,4096]{1,0:T(8,128)(2,1)S(1)} collective-permute-done((bf16[64,4096]{1,0:T(8,128)(2,1)S(1)}, bf16[64,4096]{1,0:T(8,128)(2,1)S(1)}, u32[]{:S(2)}, u32[]{:S(2)}) %collective-permute-start.10) | collective-permute-done | bytes 524320 | tf_op jit(solution)/shard_map/ppermute | solution.py:662
  31.7 0.0 collective-permute-done.11.rest_1_
  31.7 0.0 collective-permute-done.rest_2_.rest_3_
  31.7 4.6 %partial_attention.13 = (bf16[64,4224]{1,0:T(8,128)(2,1)S(1)}, bf16[64,4224]{1,0:T(8,128)(2,1)S(1)}) custom-call(s32[146]{0:T(256)S(1)} %pad_add_fusion.1.plan_ref, bf16[64,4096]{1,0:T(8,128)(2,1)S(1)} %collective-permute-done.10.rest_0_.rest_1_, bf16[64,4096]{1,0:T(8,128)(2,1)} %collective-permute-done.11.rest_1_, bf16[21,2,128,512]{3,2,1,0:T(8,128)(2,1)} %rest_2_.11, ...), custom_call_target="tpu_custom_call" | custom-call | flops 536870912 | bytes 2097152 | tf_op jit(solution)/shard_map/partial_attention/pallas_call | solution.py:427
  36.4 4.9 %collective-permute-start.12 = (bf16[64,4224]{1,0:T(8,128)(2,1)S(1)}, bf16[64,4224]{1,0:T(8,128)(2,1)S(1)}, u32[]{:S(2)}, u32[]{:S(2)}) collective-permute-start(bf16[64,4224]{1,0:T(8,128)(2,1)S(1)} %get-tuple-element.20), channel_id=1, source_target_pairs={{0,4},{4,0},{8,12},{12,8},{1,5},{5,1},{9,13},{13,9},{2,6},{6,2},{1... | collective-permute-start | bytes 1622024 | tf_op jit(solution)/shard_map/ppermute | solution.py:662
  41.3 0.7 collective-permute-start.13
  41.9 0.0 collective-permute-done.1.rest_0_.rest_1_
  42.0 0.0 collective-permute-done.2.rest_1_
  42.0 4.2 %partial_attention.9 = (bf16[64,4224]{1,0:T(8,128)(2,1)S(1)}, bf16[64,4224]{1,0:T(8,128)(2,1)S(1)}) custom-call(s32[146]{0:T(256)S(1)} %pad_add_fusion.1.plan_ref, bf16[64,4096]{1,0:T(8,128)(2,1)S(1)} %collective-permute-done.1.rest_0_.rest_1_, bf16[64,4096]{1,0:T(8,128)(2,1)S(1)} %collective-permute-done.2.rest_1_, bf16[21,2,128,512]{3,2,1,0:T(8,128)(2,1)} %rest_2_.11, ...), custom_call_target="tpu_custom_call" | custom-call | flops 536870912 | bytes 2097152 | tf_op jit(solution)/shard_map/partial_attention/pallas_call | solution.py:427
  46.1 2.2 %collective-permute-start.3 = (bf16[64,4224]{1,0:T(8,128)(2,1)S(1)}, bf16[64,4224]{1,0:T(8,128)(2,1)S(1)}, u32[]{:S(2)}, u32[]{:S(2)}) collective-permute-start(bf16[64,4224]{1,0:T(8,128)(2,1)S(1)} %get-tuple-element.16), channel_id=1, source_target_pairs={{0,4},{4,0},{8,12},{12,8},{1,5},{5,1},{9,13},{13,9},{2,6},{6,2},{1... | collective-permute-start | bytes 1622024 | tf_op jit(solution)/shard_map/ppermute | solution.py:662
  48.3 0.7 collective-permute-start.4
  49.0 0.0 collective-permute-done.13.rest_1_
  49.0 5.4 %collective-permute-done.12.rest_0_.rest_1_ = bf16[64,4224]{1,0:T(8,128)(2,1)S(1)} collective-permute-done((bf16[64,4224]{1,0:T(8,128)(2,1)S(1)}, bf16[64,4224]{1,0:T(8,128)(2,1)S(1)}, u32[]{:S(2)}, u32[]{:S(2)}) %collective-permute-start.12) | collective-permute-done | bytes 540704 | tf_op jit(solution)/shard_map/ppermute | solution.py:662
  54.4 4.2 %partial_attention.14 = (bf16[64,4224]{1,0:T(8,128)(2,1)S(1)}, bf16[64,4224]{1,0:T(8,128)(2,1)S(1)}) custom-call(s32[146]{0:T(256)S(1)} %pad_add_fusion.1.plan_ref, bf16[64,4224]{1,0:T(8,128)(2,1)S(1)} %collective-permute-done.12.rest_0_.rest_1_, bf16[64,4096]{1,0:T(8,128)(2,1)S(1)} %collective-permute-done.13.rest_1_, bf16[21,2,128,512]{3,2,1,0:T(8,128)(2,1)} %rest_2_.11, ...), custom_call_target="tpu_custom_call" | custom-call | flops 536870912 | bytes 2097152 | tf_op jit(solution)/shard_map/partial_attention/pallas_call | solution.py:427
  58.5 2.8 %collective-permute-start.14 = (bf16[64,4224]{1,0:T(8,128)(2,1)S(1)}, bf16[64,4224]{1,0:T(8,128)(2,1)S(1)}, u32[]{:S(2)}, u32[]{:S(2)}) collective-permute-start(bf16[64,4224]{1,0:T(8,128)(2,1)S(1)} %get-tuple-element.21), channel_id=1, source_target_pairs={{0,4},{4,0},{8,12},{12,8},{1,5},{5,1},{9,13},{13,9},{2,6},{6,2},{1... | collective-permute-start | bytes 1622024 | tf_op jit(solution)/shard_map/ppermute | solution.py:662
  61.3 0.7 collective-permute-start.16
  62.0 0.0 collective-permute-done.4.rest_1_
  62.0 4.0 %collective-permute-done.3.rest_0_.rest_1_ = bf16[64,4224]{1,0:T(8,128)(2,1)S(1)} collective-permute-done((bf16[64,4224]{1,0:T(8,128)(2,1)S(1)}, bf16[64,4224]{1,0:T(8,128)(2,1)S(1)}, u32[]{:S(2)}, u32[]{:S(2)}) %collective-permute-start.3) | collective-permute-done | bytes 540704 | tf_op jit(solution)/shard_map/ppermute | solution.py:662
  66.0 3.3 %partial_attention.10 = (bf16[64,4224]{1,0:T(8,128)(2,1)S(1)}, bf16[64,4224]{1,0:T(8,128)(2,1)S(1)}) custom-call(s32[146]{0:T(256)S(1)} %pad_add_fusion.1.plan_ref, bf16[64,4224]{1,0:T(8,128)(2,1)S(1)} %collective-permute-done.3.rest_0_.rest_1_, bf16[64,4096]{1,0:T(8,128)(2,1)S(1)} %collective-permute-done.4.rest_1_, bf16[21,2,128,512]{3,2,1,0:T(8,128)(2,1)} %rest_2_.11, ...), custom_call_target="tpu_custom_call" | custom-call | flops 536870912 | bytes 2097152 | tf_op jit(solution)/shard_map/partial_attention/pallas_call | solution.py:427
  69.2 3.2 %collective-permute-start.5 = (bf16[64,4224]{1,0:T(8,128)(2,1)S(1)}, bf16[64,4224]{1,0:T(8,128)(2,1)S(1)}, u32[]{:S(2)}, u32[]{:S(2)}) collective-permute-start(bf16[64,4224]{1,0:T(8,128)(2,1)S(1)} %get-tuple-element.17), channel_id=1, source_target_pairs={{0,4},{4,0},{8,12},{12,8},{1,5},{5,1},{9,13},{13,9},{2,6},{6,2},{1... | collective-permute-start | bytes 1622024 | tf_op jit(solution)/shard_map/ppermute | solution.py:662
  72.5 0.7 collective-permute-start.7
  73.2 4.4 %collective-permute-done.14.rest_0_.rest_1_ = bf16[64,4224]{1,0:T(8,128)(2,1)S(1)} collective-permute-done((bf16[64,4224]{1,0:T(8,128)(2,1)S(1)}, bf16[64,4224]{1,0:T(8,128)(2,1)S(1)}, u32[]{:S(2)}, u32[]{:S(2)}) %collective-permute-start.14) | collective-permute-done | bytes 540704 | tf_op jit(solution)/shard_map/ppermute | solution.py:662
  77.6 3.3 %partial_attention.15.rest_2_.rest_0_ = bf16[64,4224]{1,0:T(8,128)(2,1)S(1)} custom-call(s32[146]{0:T(256)S(1)} %pad_add_fusion.1.plan_ref, bf16[64,4224]{1,0:T(8,128)(2,1)S(1)} %collective-permute-done.14.rest_0_.rest_1_, bf16[64,4096]{1,0:T(8,128)(2,1)S(1)} %collective-permute-done.10.rest_0_.rest_1_, bf16[21,2,128,512]{3,2,1,0:T(8,128)(2,1)} %rest_2_.11, ...), custom_call_target="tpu_custom_call" | custom-call | flops 536870912 | bytes 2097152 | tf_op jit(solution)/shard_map/partial_attention/pallas_call | solution.py:427
  80.8 1.4 %merge_pair.6 = bf16[64,4224]{1,0:T(8,128)(2,1)} custom-call(s32[146]{0:T(256)S(1)} %pad_add_fusion.1.plan_ref, bf16[64,4224]{1,0:T(8,128)(2,1)S(1)} %get-tuple-element.19.rest_0_, bf16[64,4224]{1,0:T(8,128)(2,1)S(1)} %collective-permute-done.14.rest_0_.rest_1_, bf16[64,4224]{1,0:T(8,128)(2,1)S(1)} %partial_attention.15.rest_2_.rest_0_), custom_call_target="tpu_custom_call" | custom-call | tf_op jit(solution)/shard_map/merge_pair/pallas_call | solution.py:496
  82.2 2.6 %collective-permute-start.15 = (bf16[64,4224]{1,0:T(8,128)(2,1)}, bf16[64,4224]{1,0:T(8,128)(2,1)}, u32[]{:S(2)}, u32[]{:S(2)}) collective-permute-start(bf16[64,4224]{1,0:T(8,128)(2,1)} %merge_pair.6), channel_id=1, source_target_pairs={{4,8},{8,4},{12,0},{0,12},{5,9},{9,5},{13,1},{1,13},{6,10},{10,6},... | collective-permute-start | bytes 1622024 | tf_op jit(solution)/shard_map/ppermute | solution.py:662
  84.9 0.0 collective-permute-done.16.rest_1_
  84.9 1.4 merge_pair.7
  86.3 1.5 %collective-permute-start.17 = (bf16[64,4224]{1,0:T(8,128)(2,1)}, bf16[64,4224]{1,0:T(8,128)(2,1)}, u32[]{:S(2)}, u32[]{:S(2)}) collective-permute-start(bf16[64,4224]{1,0:T(8,128)(2,1)} %merge_pair.7), channel_id=1, source_target_pairs={{4,0},{8,12},{5,1},{9,13},{6,2},{10,14},{7,3},{11,15},{20,16},{24,... | collective-permute-start | bytes 1622024 | tf_op jit(solution)/shard_map/ppermute | solution.py:662
  87.7 1.0 collective-permute-done.5.rest_0_.rest_1_
  88.7 3.2 %partial_attention.11.rest_2_.rest_0_ = bf16[64,4224]{1,0:T(8,128)(2,1)S(1)} custom-call(s32[146]{0:T(256)S(1)} %pad_add_fusion.1.plan_ref, bf16[64,4224]{1,0:T(8,128)(2,1)S(1)} %collective-permute-done.5.rest_0_.rest_1_, bf16[64,4096]{1,0:T(8,128)(2,1)S(1)} %collective-permute-done.1.rest_0_.rest_1_, bf16[21,2,128,512]{3,2,1,0:T(8,128)(2,1)} %rest_2_.11, ...), custom_call_target="tpu_custom_call" | custom-call | flops 536870912 | bytes 2097152 | tf_op jit(solution)/shard_map/partial_attention/pallas_call | solution.py:427
  91.9 1.4 merge_pair.4
  93.2 3.7 %collective-permute-start.6 = (bf16[64,4224]{1,0:T(8,128)(2,1)}, bf16[64,4224]{1,0:T(8,128)(2,1)}, u32[]{:S(2)}, u32[]{:S(2)}) collective-permute-start(bf16[64,4224]{1,0:T(8,128)(2,1)} %merge_pair.4), channel_id=1, source_target_pairs={{4,8},{8,4},{12,0},{0,12},{5,9},{9,5},{13,1},{1,13},{6,10},{10,6},... | collective-permute-start | bytes 1622024 | tf_op jit(solution)/shard_map/ppermute | solution.py:662
  96.9 0.0 collective-permute-done.7.rest_1_
  96.9 1.4 merge_pair.5
  98.3 1.3 collective-permute-start.8
  99.6 0.2 constant_dynamic-slice_fusion
  99.9 4.7 %partial_attention.8.own_ref = bf16[64,4224]{1,0:T(8,128)(2,1)S(1)} custom-call(s32[146]{0:T(256)S(1)} %pad_add_fusion.1.plan_ref, bf16[64,4096]{1,0:T(8,128)(2,1)S(1)} %own_columns.2.rest_0_, bf16[21,2,128,512]{3,2,1,0:T(8,128)(2,1)} %rest_2_.11, bf16[21,2,128,256]{3,2,1,0:T(8,128)(2,1)} %collective-permute-done.rest_2_.rest_3_, ...), custom_call_target="tpu_custom_call" | custom-call | flops 536870912 | bytes 2097152 | tf_op jit(solution)/shard_map/partial_attention/pallas_call | solution.py:427
  104.6 3.4 %partial_attention.12.own_ref = bf16[64,4224]{1,0:T(8,128)(2,1)S(1)} custom-call(s32[146]{0:T(256)S(1)} %pad_add_fusion.1.plan_ref, bf16[64,4096]{1,0:T(8,128)(2,1)S(1)} %copy-done.2, bf16[21,2,128,512]{3,2,1,0:T(8,128)(2,1)} %rest_2_.11, bf16[21,2,128,256]{3,2,1,0:T(8,128)(2,1)} %collective-permute-done.rest_2_.rest_3_, ...), custom_call_target="tpu_custom_call" | custom-call | flops 536870912 | bytes 2097152 | tf_op jit(solution)/shard_map/partial_attention/pallas_call | solution.py:427
  108.0 17.1 %collective-permute-done.17.rest_0_ = bf16[64,4224]{1,0:T(8,128)(2,1)} collective-permute-done((bf16[64,4224]{1,0:T(8,128)(2,1)}, bf16[64,4224]{1,0:T(8,128)(2,1)}, u32[]{:S(2)}, u32[]{:S(2)}) %collective-permute-start.17) | collective-permute-done | bytes 540704 | tf_op jit(solution)/shard_map/ppermute | solution.py:662
  125.1 2.3 %merge_final.3.own_ref = bf16[2,64,2048]{2,1,0:T(8,128)(2,1)S(1)} custom-call(s32[146]{0:T(256)S(1)} %pad_add_fusion.1.plan_ref, bf16[64,4224]{1,0:T(8,128)(2,1)S(1)} %partial_attention.12.own_ref, bf16[64,4224]{1,0:T(8,128)(2,1)} %collective-permute-done.15.last_ref, bf16[64,4224]{1,0:T(8,128)(2,1)} %collective-permute-done.17.rest_0_, ...), custom_call_target="tpu_custom_call" | custom-call | tf_op jit(solution)/shard_map/merge_final/pallas_call | solution.py:542
  127.4 0.1 collective-permute-start.18
  127.5 7.2 %collective-permute-done.8.rest_0_ = bf16[64,4224]{1,0:T(8,128)(2,1)} collective-permute-done((bf16[64,4224]{1,0:T(8,128)(2,1)}, bf16[64,4224]{1,0:T(8,128)(2,1)}, u32[]{:S(2)}, u32[]{:S(2)}) %collective-permute-start.8) | collective-permute-done | bytes 540704 | tf_op jit(solution)/shard_map/ppermute | solution.py:662
  134.7 2.3 %merge_final.2.own_ref = bf16[2,64,2048]{2,1,0:T(8,128)(2,1)S(1)} custom-call(s32[146]{0:T(256)S(1)} %pad_add_fusion.1.plan_ref, bf16[64,4224]{1,0:T(8,128)(2,1)S(1)} %partial_attention.8.own_ref, bf16[64,4224]{1,0:T(8,128)(2,1)} %collective-permute-done.6.last_ref, bf16[64,4224]{1,0:T(8,128)(2,1)} %collective-permute-done.8.rest_0_, ...), custom_call_target="tpu_custom_call" | custom-call | tf_op jit(solution)/shard_map/merge_final/pallas_call | solution.py:542
  137.0 0.1 collective-permute-start.9
  137.1 1.0 place_columns.2.rest_0_
  138.1 0.9 collective-permute-done.9.other_ref
  139.0 1.0 place_columns.3
  (20 shorter events, 0.1 us)
Async XLA Ops:
  0.0 99.6 %copy-start = (bf16[4,64,2,512]{3,2,1,0:T(2,128)(2,1)S(1)}, bf16[4,64,2,512]{3,2,1,0:T(2,128)(2,1)}, u32[]{:S(2)}) copy-start(bf16[4,64,2,512]{3,2,1,0:T(2,128)(2,1)} %param.7) | copy-start | bytes 1572868
  1.1 14.4 %copy-start.3 = (s32[16,16]{1,0:T(8,128)S(1)}, s32[16,16]{1,0:T(8,128)}, u32[]{:S(2)}) copy-start(s32[16,16]{1,0:T(8,128)} %param.9) | copy-start | bytes 3076
  1.1 14.4 %copy-start.4 = (s32[16]{0:T(128)S(1)}, s32[16]{0:T(128)}, u32[]{:S(2)}) copy-start(s32[16]{0:T(128)} %param.10) | copy-start | bytes 196
  4.8 11.6 %copy-start.5 = (s32[16]{0:T(128)S(1)}, s32[16]{0:T(128)}, u32[]{:S(2)}) copy-start(s32[16]{0:T(128)} %param.11) | copy-start | bytes 196
  4.8 26.9 %collective-permute-start = (bf16[21,2,128,256]{3,2,1,0:T(8,128)(2,1)}, bf16[21,2,128,256]{3,2,1,0:T(8,128)(2,1)}, u32[]{:S(2)}, u32[]{:S(2)}) collective-permute-start(bf16[21,2,128,256]{3,2,1,0:T(8,128)(2,1)} %constant_dynamic-slice_fusion.1), channel_id=1, source_target_pairs={{0,1},{1,0},{2,3},{3,2},{4,5},{5,4},{6,7},{7,6},{8,9},{9,8},{10,11... | collective-permute-start | bytes 8257544 | tf_op jit(solution)/shard_map/ppermute | solution.py:647
  5.3 36.6 %collective-permute-start.1 = (bf16[64,4096]{1,0:T(8,128)(2,1)S(1)}, bf16[64,4096]{1,0:T(8,128)(2,1)S(1)}, u32[]{:S(2)}, u32[]{:S(2)}) collective-permute-start(bf16[64,4096]{1,0:T(8,128)(2,1)S(1)} %own_columns.2.rest_0_), channel_id=1, source_target_pairs={{0,4},{4,0},{8,12},{12,8},{1,5},{5,1},{9,13},{13,9},{2,6},{6,2},{1... | collective-permute-start | bytes 1572872 | tf_op jit(solution)/shard_map/ppermute | solution.py:662
  7.9 34.1 %collective-permute-start.2 = (bf16[64,4096]{1,0:T(8,128)(2,1)S(1)}, bf16[64,4096]{1,0:T(8,128)(2,1)S(1)}, u32[]{:S(2)}, u32[]{:S(2)}) collective-permute-start(bf16[64,4096]{1,0:T(8,128)(2,1)S(1)} %own_columns.2.rest_0_), channel_id=1, source_target_pairs={{4,8},{8,4},{5,9},{9,5},{6,10},{10,6},{7,11},{11,7},{20,24},{24,20... | collective-permute-start | bytes 1572872 | tf_op jit(solution)/shard_map/ppermute | solution.py:662
  9.6 26.7 %copy-start.1 = (bf16[64,4096]{1,0:T(8,128)(2,1)}, bf16[64,4096]{1,0:T(8,128)(2,1)S(1)}, u32[]{:S(2)}) copy-start(bf16[64,4096]{1,0:T(8,128)(2,1)S(1)} %own_columns.3.rest_0_) | copy-start | bytes 1572868
  9.6 22.1 %collective-permute-start.10 = (bf16[64,4096]{1,0:T(8,128)(2,1)S(1)}, bf16[64,4096]{1,0:T(8,128)(2,1)S(1)}, u32[]{:S(2)}, u32[]{:S(2)}) collective-permute-start(bf16[64,4096]{1,0:T(8,128)(2,1)S(1)} %own_columns.3.rest_0_), channel_id=1, source_target_pairs={{0,4},{4,0},{8,12},{12,8},{1,5},{5,1},{9,13},{13,9},{2,6},{6,2},{1... | collective-permute-start | bytes 1572872 | tf_op jit(solution)/shard_map/ppermute | solution.py:662
  14.1 17.6 %collective-permute-start.11 = (bf16[64,4096]{1,0:T(8,128)(2,1)S(1)}, bf16[64,4096]{1,0:T(8,128)(2,1)}, u32[]{:S(2)}, u32[]{:S(2)}) collective-permute-start(bf16[64,4096]{1,0:T(8,128)(2,1)S(1)} %own_columns.3.rest_0_), channel_id=1, source_target_pairs={{4,8},{8,4},{5,9},{9,5},{6,10},{10,6},{7,11},{11,7},{20,24},{24,20... | collective-permute-start | bytes 1572872 | tf_op jit(solution)/shard_map/ppermute | solution.py:662
  36.4 18.0 %collective-permute-start.12 = (bf16[64,4224]{1,0:T(8,128)(2,1)S(1)}, bf16[64,4224]{1,0:T(8,128)(2,1)S(1)}, u32[]{:S(2)}, u32[]{:S(2)}) collective-permute-start(bf16[64,4224]{1,0:T(8,128)(2,1)S(1)} %get-tuple-element.20), channel_id=1, source_target_pairs={{0,4},{4,0},{8,12},{12,8},{1,5},{5,1},{9,13},{13,9},{2,6},{6,2},{1... | collective-permute-start | bytes 1622024 | tf_op jit(solution)/shard_map/ppermute | solution.py:662
  41.3 7.7 %collective-permute-start.13 = (bf16[64,4096]{1,0:T(8,128)(2,1)S(1)}, bf16[64,4096]{1,0:T(8,128)(2,1)S(1)}, u32[]{:S(2)}, u32[]{:S(2)}) collective-permute-start(bf16[64,4096]{1,0:T(8,128)(2,1)S(1)} %collective-permute-done.10.rest_0_.rest_1_), channel_id=1, source_target_pairs={{4,8},{8,4},{5,9},{9,5},{6,10},{10,6},{7,11},{11,7},{20,24},{24,20... | collective-permute-start | bytes 1572872 | tf_op jit(solution)/shard_map/ppermute | solution.py:662
  46.1 19.8 %collective-permute-start.3 = (bf16[64,4224]{1,0:T(8,128)(2,1)S(1)}, bf16[64,4224]{1,0:T(8,128)(2,1)S(1)}, u32[]{:S(2)}, u32[]{:S(2)}) collective-permute-start(bf16[64,4224]{1,0:T(8,128)(2,1)S(1)} %get-tuple-element.16), channel_id=1, source_target_pairs={{0,4},{4,0},{8,12},{12,8},{1,5},{5,1},{9,13},{13,9},{2,6},{6,2},{1... | collective-permute-start | bytes 1622024 | tf_op jit(solution)/shard_map/ppermute | solution.py:662
  48.3 13.7 %collective-permute-start.4 = (bf16[64,4096]{1,0:T(8,128)(2,1)S(1)}, bf16[64,4096]{1,0:T(8,128)(2,1)S(1)}, u32[]{:S(2)}, u32[]{:S(2)}) collective-permute-start(bf16[64,4096]{1,0:T(8,128)(2,1)S(1)} %collective-permute-done.1.rest_0_.rest_1_), channel_id=1, source_target_pairs={{4,8},{8,4},{5,9},{9,5},{6,10},{10,6},{7,11},{11,7},{20,24},{24,20... | collective-permute-start | bytes 1572872 | tf_op jit(solution)/shard_map/ppermute | solution.py:662
  58.5 19.0 %collective-permute-start.14 = (bf16[64,4224]{1,0:T(8,128)(2,1)S(1)}, bf16[64,4224]{1,0:T(8,128)(2,1)S(1)}, u32[]{:S(2)}, u32[]{:S(2)}) collective-permute-start(bf16[64,4224]{1,0:T(8,128)(2,1)S(1)} %get-tuple-element.21), channel_id=1, source_target_pairs={{0,4},{4,0},{8,12},{12,8},{1,5},{5,1},{9,13},{13,9},{2,6},{6,2},{1... | collective-permute-start | bytes 1622024 | tf_op jit(solution)/shard_map/ppermute | solution.py:662
  61.3 23.6 %collective-permute-start.16 = (bf16[64,4224]{1,0:T(8,128)(2,1)S(1)}, bf16[64,4224]{1,0:T(8,128)(2,1)S(1)}, u32[]{:S(2)}, u32[]{:S(2)}) collective-permute-start(bf16[64,4224]{1,0:T(8,128)(2,1)S(1)} %get-tuple-element.22), channel_id=1, source_target_pairs={{4,8},{8,4},{5,9},{9,5},{6,10},{10,6},{7,11},{11,7},{20,24},{24,20... | collective-permute-start | bytes 1622024 | tf_op jit(solution)/shard_map/ppermute | solution.py:662
  69.2 19.4 %collective-permute-start.5 = (bf16[64,4224]{1,0:T(8,128)(2,1)S(1)}, bf16[64,4224]{1,0:T(8,128)(2,1)S(1)}, u32[]{:S(2)}, u32[]{:S(2)}) collective-permute-start(bf16[64,4224]{1,0:T(8,128)(2,1)S(1)} %get-tuple-element.17), channel_id=1, source_target_pairs={{0,4},{4,0},{8,12},{12,8},{1,5},{5,1},{9,13},{13,9},{2,6},{6,2},{1... | collective-permute-start | bytes 1622024 | tf_op jit(solution)/shard_map/ppermute | solution.py:662
  72.5 24.4 %collective-permute-start.7 = (bf16[64,4224]{1,0:T(8,128)(2,1)S(1)}, bf16[64,4224]{1,0:T(8,128)(2,1)S(1)}, u32[]{:S(2)}, u32[]{:S(2)}) collective-permute-start(bf16[64,4224]{1,0:T(8,128)(2,1)S(1)} %get-tuple-element.18), channel_id=1, source_target_pairs={{4,8},{8,4},{5,9},{9,5},{6,10},{10,6},{7,11},{11,7},{20,24},{24,20... | collective-permute-start | bytes 1622024 | tf_op jit(solution)/shard_map/ppermute | solution.py:662
  82.2 25.7 %collective-permute-start.15 = (bf16[64,4224]{1,0:T(8,128)(2,1)}, bf16[64,4224]{1,0:T(8,128)(2,1)}, u32[]{:S(2)}, u32[]{:S(2)}) collective-permute-start(bf16[64,4224]{1,0:T(8,128)(2,1)} %merge_pair.6), channel_id=1, source_target_pairs={{4,8},{8,4},{12,0},{0,12},{5,9},{9,5},{13,1},{1,13},{6,10},{10,6},... | collective-permute-start | bytes 1622024 | tf_op jit(solution)/shard_map/ppermute | solution.py:662
  86.3 38.9 %collective-permute-start.17 = (bf16[64,4224]{1,0:T(8,128)(2,1)}, bf16[64,4224]{1,0:T(8,128)(2,1)}, u32[]{:S(2)}, u32[]{:S(2)}) collective-permute-start(bf16[64,4224]{1,0:T(8,128)(2,1)} %merge_pair.7), channel_id=1, source_target_pairs={{4,0},{8,12},{5,1},{9,13},{6,2},{10,14},{7,3},{11,15},{20,16},{24,... | collective-permute-start | bytes 1622024 | tf_op jit(solution)/shard_map/ppermute | solution.py:662
  93.2 34.3 %collective-permute-start.6 = (bf16[64,4224]{1,0:T(8,128)(2,1)}, bf16[64,4224]{1,0:T(8,128)(2,1)}, u32[]{:S(2)}, u32[]{:S(2)}) collective-permute-start(bf16[64,4224]{1,0:T(8,128)(2,1)} %merge_pair.4), channel_id=1, source_target_pairs={{4,8},{8,4},{12,0},{0,12},{5,9},{9,5},{13,1},{1,13},{6,10},{10,6},... | collective-permute-start | bytes 1622024 | tf_op jit(solution)/shard_map/ppermute | solution.py:662
  98.3 36.4 %collective-permute-start.8 = (bf16[64,4224]{1,0:T(8,128)(2,1)}, bf16[64,4224]{1,0:T(8,128)(2,1)}, u32[]{:S(2)}, u32[]{:S(2)}) collective-permute-start(bf16[64,4224]{1,0:T(8,128)(2,1)} %merge_pair.5), channel_id=1, source_target_pairs={{4,0},{8,12},{5,1},{9,13},{6,2},{10,14},{7,3},{11,15},{20,16},{24,... | collective-permute-start | bytes 1622024 | tf_op jit(solution)/shard_map/ppermute | solution.py:662
  99.8 4.7 %copy-start.2 = (bf16[64,4096]{1,0:T(8,128)(2,1)S(1)}, bf16[64,4096]{1,0:T(8,128)(2,1)}, u32[]{:S(2)}) copy-start(bf16[64,4096]{1,0:T(8,128)(2,1)} %copy-done.1) | copy-start | bytes 1572868
  127.4 9.7 %collective-permute-start.18 = (bf16[2,64,2048]{2,1,0:T(8,128)(2,1)S(1)}, bf16[2,64,2048]{2,1,0:T(8,128)(2,1)S(1)}, u32[]{:S(2)}, u32[]{:S(2)}) collective-permute-start(bf16[2,64,2048]{2,1,0:T(8,128)(2,1)S(1)} %merge_final.3.own_ref), channel_id=1, source_target_pairs={{0,1},{1,0},{2,3},{3,2},{4,5},{5,4},{6,7},{7,6},{8,9},{9,8},{10,11... | collective-permute-start | bytes 1572872 | tf_op jit(solution)/shard_map/ppermute | solution.py:703
  137.0 2.0 %collective-permute-start.9 = (bf16[2,64,2048]{2,1,0:T(8,128)(2,1)S(1)}, bf16[2,64,2048]{2,1,0:T(8,128)(2,1)S(1)}, u32[]{:S(2)}, u32[]{:S(2)}) collective-permute-start(bf16[2,64,2048]{2,1,0:T(8,128)(2,1)S(1)} %merge_final.2.own_ref), channel_id=1, source_target_pairs={{0,1},{1,0},{2,3},{3,2},{4,5},{5,4},{6,7},{7,6},{8,9},{9,8},{10,11... | collective-permute-start | bytes 1572872 | tf_op jit(solution)/shard_map/ppermute | solution.py:703
